TPU v7x, 128 devices: a whole 4x4x4 slice. The times are simulated.
128 devices in a mesh: grp: 4 (over z), dev: 32 (over x, y, core).
Axes of the slice: x: 4, y: 4, z: 4, core: 2. Of those that a mesh axis runs over, the one named last changes fastest.
Arguments:
- matrix_tiles: bfloat16 [10240, 128, 1024], P(('grp', 'dev')), may hold values from -0.125 to 0.125
- tile_column: int32 [10240], P(('grp', 'dev')), may hold values from 0 to 255
- block_counts: int32 [4096], P(('grp', 'dev')), may hold values from 1 to 4, as said below
- destination: int32 [4096], P(('grp', 'dev')), may hold values from 0 to 31, as said below
- row_bounds: bfloat16 [524288], P(('grp', 'dev')), may hold values from -6 to 6
- dual_start: bfloat16 [524288], P(('grp', 'dev')), may hold values from 0 to 1
- primal_start: float32 [262144], replicated, may hold values from 0 to 0.5
- cost_vector: float32 [262144], replicated, may hold values from -6 to 6
- upper_bound: float32 [262144], replicated, may hold values from 0.5 to 2
Outputs:
- primal_final: float32 [262144], replicated
- dual_final: float32 [524288], P(('grp', 'dev'))
- weight_final: float32 [1], replicated
Inputs may be any that keep to these rules, and one draw needn't show every extreme that they name: `block_counts`: each device's 32 row blocks have 1 to 4 tiles each and 80 at most together; some device has exactly 80 in every draw. `destination`: on every device the 32 entries are each of 0 to 31 once.
All inputs are finite; a program needn't handle non-finite values.
Results may differ from a plain program's by a relative error of at most 0.0015.
Values may be sent and summed in bfloat16 or wider, within the bound.
No kernel may reach another device: no remote copies, remote signals or barrier semaphores. Data moves between devices by JAX's collectives and lax.ppermute only.
A program may use at most 128 MiB of HBM per device.

v0:
```python
import jax
import jax.numpy as jnp
from jax import lax
from jax.sharding import Mesh
from jax.sharding import PartitionSpec as P

NCB = 256
ITERS = 3
GRP_DEV = ("grp", "dev_0", "dev_1", "dev_2")
DEV = ("dev_0", "dev_1", "dev_2")


step_scale = 0.3


def in_blocks(array, dim, length):
    before, after = (array.shape[:dim], array.shape[dim + 1 :])
    return jnp.moveaxis(array.reshape(*before, length, -1, *after), dim, 0)


def summed_on_arrival(array, axis, dim):
    length = lax.axis_size(axis)
    tiles = lax.all_to_all(in_blocks(array, dim, length), axis, 0, 0, tiled=True)
    return jnp.sum(tiles, axis=0)


def sum_by_axis(array, axes, dim):
    far, near = axes
    own = summed_on_arrival(in_blocks(array, dim, lax.axis_size(far)), near, dim + 1)
    return jnp.sum(lax.all_to_all(own, far, 0, 0, tiled=True), axis=0)


def copy_for_each(array, axis):
    length = lax.axis_size(axis)
    return lax.all_to_all(
        jnp.broadcast_to(array[None], (length, *array.shape)), axis, 0, 0, tiled=True
    )


def laid_out(tiles, dim):
    tiles = jnp.moveaxis(tiles, 0, dim)
    dims = tiles.shape
    return tiles.reshape(*dims[:dim], dims[dim] * dims[dim + 1], *dims[dim + 2 :])


def gathered_by_axis(array, axes, dim):
    far, near = axes
    tiles = copy_for_each(copy_for_each(array, far), near)
    return laid_out(tiles.swapaxes(0, 1).reshape(-1, *array.shape), dim)


def taken_together(array, axis):
    everything = copy_for_each(array, axis)
    return jnp.sum(everything, axis=0)


def by_axis(array, axes):
    far, near = axes
    nearer = taken_together(array, near)
    return taken_together(nearer, far)


def together(arrays, axis):
    ends = [0]
    for a in arrays:
        ends.append(ends[-1] + a.size)
    running = by_axis(jnp.concatenate([a.ravel() for a in arrays]), axis)
    return tuple((running[b:e].reshape(a.shape) for a, b, e in zip(arrays, ends, ends[1:])))


def row_products(tile_store, vector_bf, blocks):
    tile_set, tile_cols, owners, live_flags = tile_store
    vector_table = vector_bf.reshape(-1, tile_set.shape[2])
    column_hot = (
        tile_cols[:, None] == jnp.arange(vector_table.shape[0], dtype=jnp.int32)[None, :]
    ).astype(jnp.bfloat16)
    picked = jnp.dot(column_hot, vector_table, preferred_element_type=jnp.float32).astype(
        jnp.bfloat16
    )
    product = jnp.einsum("src,sc->sr", tile_set, picked, preferred_element_type=jnp.float32)
    product = jnp.where(live_flags[:, None], product, 0.0)
    owner_hot = (jnp.arange(blocks, dtype=jnp.int32)[:, None] == owners[None, :]).astype(
        jnp.float32
    )
    return jnp.dot(owner_hot, product, precision=lax.Precision.HIGHEST)


def column_products(tile_store, rows_bf):
    tile_set, tile_cols, owners, live_flags = tile_store
    blocks = rows_bf.shape[0]
    owner_hot = (owners[:, None] == jnp.arange(blocks, dtype=jnp.int32)[None, :]).astype(
        jnp.bfloat16
    )
    picked_rows = jnp.dot(owner_hot, rows_bf, preferred_element_type=jnp.float32).astype(
        jnp.bfloat16
    )
    product = jnp.einsum("src,sr->sc", tile_set, picked_rows, preferred_element_type=jnp.float32)
    product = jnp.where(live_flags[:, None], product, 0.0)
    column_hot = (jnp.arange(NCB, dtype=jnp.int32)[:, None] == tile_cols[None, :]).astype(
        jnp.float32
    )
    return jnp.dot(column_hot, product, precision=lax.Precision.HIGHEST).reshape(-1)


def per_device(
    matrix_tiles,
    tile_column,
    block_counts,
    destination,
    row_bounds,
    dual_start,
    primal_start,
    cost_vector,
    upper_bound,
):
    blocks = block_counts.shape[0]
    rows_per = matrix_tiles.shape[1]
    slot_count = matrix_tiles.shape[0]
    starts = jnp.cumsum(block_counts) - block_counts
    slot_ids = jnp.arange(slot_count, dtype=jnp.int32)
    owners = jnp.sum((starts[None, 1:] <= slot_ids[:, None]).astype(jnp.int32), axis=1)
    bounds_here = row_bounds.reshape(blocks, rows_per)
    dual_here = dual_start.reshape(blocks, rows_per)
    peer_ids = jnp.arange(blocks, dtype=jnp.int32)
    inverse = jnp.sum(
        jnp.where(destination[None, :] == peer_ids[:, None], peer_ids[None, :], 0), axis=1
    )
    tile_store = (matrix_tiles, tile_column, owners, slot_ids < jnp.sum(block_counts))
    bounds = bounds_here.astype(jnp.float32)
    dual_state = dual_here.astype(jnp.float32)
    primal = primal_start
    weight = jnp.ones((), jnp.float32)
    row_image = row_products(tile_store, primal.astype(jnp.bfloat16), blocks)
    for iteration in range(ITERS):
        step_primal = step_scale / weight
        step_dual = step_scale * weight
        partial_value = column_products(tile_store, dual_state.astype(jnp.bfloat16))
        column_share = sum_by_axis(partial_value, (("grp", "dev_0", "dev_1"), "dev_2"), 0)
        share_len = column_share.shape[0]
        share_start = lax.axis_index(GRP_DEV) * share_len
        primal_share = lax.dynamic_slice_in_dim(primal, share_start, share_len)
        cost_share = lax.dynamic_slice_in_dim(cost_vector, share_start, share_len)
        upper_share = lax.dynamic_slice_in_dim(upper_bound, share_start, share_len)
        new_share = jnp.clip(
            primal_share - step_primal * (cost_share - column_share), 0.0, upper_share
        )
        change_part = jnp.sum((new_share - primal_share) ** 2)
        primal_next = gathered_by_axis(new_share, (("grp", "dev_0", "dev_1"), "dev_2"), 0)
        next_image = row_products(tile_store, primal_next.astype(jnp.bfloat16), blocks)
        dual_state = jnp.maximum(
            dual_state + step_dual * (bounds - (2.0 * next_image - row_image)), 0.0
        )
        violation_part = jnp.sum(jnp.maximum(bounds - next_image, 0.0) ** 2)
        violation, change = together(
            (violation_part, change_part), (("grp", "dev_0", "dev_1"), "dev_2")
        )
        weight = jnp.sqrt(weight * jnp.sqrt((violation + 1e-06) / (change + 1e-06)))
        primal = primal_next
        row_image = next_image
    dual_final = lax.all_to_all(
        dual_state[inverse], DEV, split_axis=0, concat_axis=0, tiled=True
    ).reshape(-1)
    return (primal, dual_final, jnp.reshape(weight, (1,)))


def solution(mesh):
    split = Mesh(
        mesh.devices.reshape(mesh.shape["grp"], 4, 4, 2), ("grp", "dev_0", "dev_1", "dev_2")
    )
    return jax.shard_map(
        per_device,
        mesh=split,
        in_specs=(
            P(GRP_DEV, None, None),
            P(GRP_DEV),
            P(GRP_DEV),
            P(GRP_DEV),
            P(GRP_DEV),
            P(GRP_DEV),
            P(),
            P(),
            P(),
        ),
        out_specs=(P(), P(GRP_DEV), P()),
        check_vma=False,
    )
```

profile of v0, /device:TPU:1, one launch (start us, length us, event | category | flops | bytes accessed | tf_op | source)
XLA Modules:
  0.0 307.3 jit_solution(17771277475727326074)
XLA Ops:
  0.7 0.8 copy.36
  1.6 1.3 fusion.98
  3.8 0.9 fusion.4
  4.7 8.4 %fusion.38 = f32[80,1,1024]{2,1,0:T(1,128)S(1)} fusion(bf16[80,128,1024]{2,1,0:T(8,128)(2,1)} %param.9, bf16[80,128,1]{1,0,2:T(8,128)(2,1)S(1)} %fusion.4), kind=kOutput, calls=%fused_computation.61 | convolution fusion | flops 20971520 | bytes 21319680 | tf_op jit(solution)/shard_map/src,sr->sc/dot_general | solution.py:97
  13.1 0.7 fusion.13
  15.1 5.6 %all_to_all.120 = f32[2,64,2048]{2,1,0:T(8,128)S(1)} all-to-all(f32[2,64,2048]{2,1,0:T(8,128)S(1)} %bitcast.120), channel_id=1, replica_groups=mesh['grp'=4,'dev_0'=4,'dev_1'=4,'dev_2'=2] {'dev_2'}, dimensions={0} | all-to-all | bytes 2097152 | tf_op jit(solution)/shard_map/all_to_all | solution.py:23
  20.8 1.2 all_to_all.79
  22.0 11.2 %all-to-all-start.1 = ((f32[64,1,2048]{2,1,0:T(1,128)}), f32[64,1,2048]{2,1,0:T(1,128)S(1)}, u32[]{:S(2)}, u32[]{:S(2)}) async-start(f32[64,1,2048]{2,1,0:T(1,128)} %all_to_all.79), calls=%async_computation.1 | async-start | bytes 1048576 | tf_op jit(solution)/shard_map/all_to_all | solution.py:30
  33.8 11.7 %all-to-all-done.1 = f32[64,1,2048]{2,1,0:T(1,128)S(1)} async-done(((f32[64,1,2048]{2,1,0:T(1,128)}), f32[64,1,2048]{2,1,0:T(1,128)S(1)}, u32[]{:S(2)}, u32[]{:S(2)}) %all-to-all-start.1) | async-done | bytes 524320 | tf_op jit(solution)/shard_map/all_to_all | solution.py:30
  45.8 1.3 multiply_reduce_fusion.2
  47.1 1.1 broadcast_in_dim.88
  48.2 4.7 %all-to-all-start.2 = ((f32[64,1,2048]{2,1,0:T(1,128)}), f32[64,1,2048]{2,1,0:T(1,128)S(1)}, u32[]{:S(2)}, u32[]{:S(2)}) async-start(f32[64,1,2048]{2,1,0:T(1,128)} %broadcast_in_dim.88), calls=%async_computation.2 | async-start | bytes 1048576 | tf_op jit(solution)/shard_map/all_to_all | solution.py:35
  52.9 9.8 %fusion.20 = f32[80,1,128]{2,1,0:T(1,128)S(1)} fusion(bf16[80,128,1024]{2,1,0:T(8,128)(2,1)} %param.9, bf16[80,1024,1]{1,0,2:T(8,128)(2,1)S(1)} %fusion.1), kind=kOutput, calls=%fused_computation.41 | convolution fusion | flops 20971520 | bytes 21176320 | tf_op jit(solution)/shard_map/src,sc->sr/dot_general | solution.py:80
  62.7 1.1 all-to-all-done.2
  64.1 7.5 %all_to_all.121 = f32[2,64,2048]{2,1,0:T(8,128)S(1)} all-to-all(f32[2,64,2048]{2,1,0:T(8,128)S(1)} %broadcast_in_dim.90), channel_id=1, replica_groups=mesh['grp'=4,'dev_0'=4,'dev_1'=4,'dev_2'=2] {'dev_2'}, dimensions={0} | all-to-all | bytes 2097152 | tf_op jit(solution)/shard_map/all_to_all | solution.py:35
  72.8 9.8 %fusion.22 = f32[80,1,128]{2,1,0:T(1,128)S(1)} fusion(bf16[80,128,1024]{2,1,0:T(8,128)(2,1)} %param.9, bf16[80,1024,1]{1,0,2:T(8,128)(2,1)S(1)} %fusion), kind=kOutput, calls=%fused_computation.43 | convolution fusion | flops 20971520 | bytes 21176320 | tf_op jit(solution)/shard_map/src,sc->sr/dot_general | solution.py:80
  82.7 0.8 fusion.64
  83.5 1.4 pad_maximum_fusion
  84.9 4.0 %all_to_all.122 = f32[2,1,2]{2,1,0:T(1,128)S(1)} all-to-all(f32[2,1,2]{2,1,0:T(1,128)S(1)} %broadcast_in_dim.93), channel_id=1, replica_groups=mesh['grp'=4,'dev_0'=4,'dev_1'=4,'dev_2'=2] {'dev_2'}, dimensions={0} | all-to-all | bytes 32 | tf_op jit(solution)/shard_map/all_to_all | solution.py:35
  89.3 8.4 %fusion.36 = f32[80,1,1024]{2,1,0:T(1,128)S(1)} fusion(bf16[80,128,1024]{2,1,0:T(8,128)(2,1)} %param.9, bf16[80,128,1]{1,0,2:T(8,128)(2,1)S(1)} %fusion.5), kind=kOutput, calls=%fused_computation.59 | convolution fusion | flops 20971520 | bytes 21319680 | tf_op jit(solution)/shard_map/src,sr->sc/dot_general | solution.py:97
  97.7 0.7 fusion.12
  98.4 0.7 reshape_reshape_reshape.10
  99.7 4.5 %all_to_all.123 = f32[2,64,2048]{2,1,0:T(8,128)S(1)} all-to-all(f32[2,64,2048]{2,1,0:T(8,128)S(1)} %bitcast.121), channel_id=1, replica_groups=mesh['grp'=4,'dev_0'=4,'dev_1'=4,'dev_2'=2] {'dev_2'}, dimensions={0} | all-to-all | bytes 2097152 | tf_op jit(solution)/shard_map/all_to_all | solution.py:23
  104.9 7.8 %all-to-all-start.5 = ((f32[64,1,2]{2,1,0:T(1,128)}), f32[64,1,2]{2,1,0:T(1,128)S(1)}, u32[]{:S(2)}, u32[]{:S(2)}) async-start(f32[64,1,2]{2,1,0:T(1,128)} %broadcast_in_dim.94), calls=%async_computation.5 | async-start | bytes 65536 | tf_op jit(solution)/shard_map/all_to_all | solution.py:35
  112.8 1.2 all_to_all.86
  113.9 7.2 %all-to-all-done.5 = f32[64,1,2]{2,1,0:T(1,128)S(1)} async-done(((f32[64,1,2]{2,1,0:T(1,128)}), f32[64,1,2]{2,1,0:T(1,128)S(1)}, u32[]{:S(2)}, u32[]{:S(2)}) %all-to-all-start.5) | async-done | bytes 544 | tf_op jit(solution)/shard_map/all_to_all | solution.py:35
  121.1 4.7 %all-to-all-start.7 = ((f32[64,1,2048]{2,1,0:T(1,128)}), f32[64,1,2048]{2,1,0:T(1,128)S(1)}, u32[]{:S(2)}, u32[]{:S(2)}) async-start(f32[64,1,2048]{2,1,0:T(1,128)} %all_to_all.86), calls=%async_computation.7 | async-start | bytes 1048576 | tf_op jit(solution)/shard_map/all_to_all | solution.py:30
  125.8 0.8 copy.121
  128.8 8.0 %all-to-all-done.7 = f32[64,1,2048]{2,1,0:T(1,128)S(1)} async-done(((f32[64,1,2048]{2,1,0:T(1,128)}), f32[64,1,2048]{2,1,0:T(1,128)S(1)}, u32[]{:S(2)}, u32[]{:S(2)}) %all-to-all-start.7) | async-done | bytes 524320 | tf_op jit(solution)/shard_map/all_to_all | solution.py:30
  137.1 1.3 multiply_reduce_fusion.1
  138.4 1.1 broadcast_in_dim.95
  139.5 4.6 %all-to-all-start.8 = ((f32[64,1,2048]{2,1,0:T(1,128)}), f32[64,1,2048]{2,1,0:T(1,128)S(1)}, u32[]{:S(2)}, u32[]{:S(2)}) async-start(f32[64,1,2048]{2,1,0:T(1,128)} %broadcast_in_dim.95), calls=%async_computation.8 | async-start | bytes 1048576 | tf_op jit(solution)/shard_map/all_to_all | solution.py:35
  144.1 11.0 %all-to-all-done.8 = f32[64,1,2048]{2,1,0:T(1,128)S(1)} async-done(((f32[64,1,2048]{2,1,0:T(1,128)}), f32[64,1,2048]{2,1,0:T(1,128)S(1)}, u32[]{:S(2)}, u32[]{:S(2)}) %all-to-all-start.8) | async-done | bytes 524320 | tf_op jit(solution)/shard_map/all_to_all | solution.py:35
  155.4 8.5 %all_to_all.124 = f32[2,64,2048]{2,1,0:T(8,128)S(1)} all-to-all(f32[2,64,2048]{2,1,0:T(8,128)S(1)} %broadcast_in_dim.97), channel_id=1, replica_groups=mesh['grp'=4,'dev_0'=4,'dev_1'=4,'dev_2'=2] {'dev_2'}, dimensions={0} | all-to-all | bytes 2097152 | tf_op jit(solution)/shard_map/all_to_all | solution.py:35
  165.1 9.8 %fusion.17 = f32[80,1,128]{2,1,0:T(1,128)S(1)} fusion(bf16[80,128,1024]{2,1,0:T(8,128)(2,1)} %param.9, bf16[80,1024,1]{1,0,2:T(8,128)(2,1)S(1)} %fusion.2), kind=kOutput, calls=%fused_computation.38 | convolution fusion | flops 20971520 | bytes 21176320 | tf_op jit(solution)/shard_map/src,sc->sr/dot_general | solution.py:80
  174.9 0.8 fusion.67
  175.8 1.4 pad_maximum_fusion.1
  177.1 13.8 %all_to_all.125 = f32[2,1,2]{2,1,0:T(1,128)S(1)} all-to-all(f32[2,1,2]{2,1,0:T(1,128)S(1)} %broadcast_in_dim.98), channel_id=1, replica_groups=mesh['grp'=4,'dev_0'=4,'dev_1'=4,'dev_2'=2] {'dev_2'}, dimensions={0} | all-to-all | bytes 32 | tf_op jit(solution)/shard_map/all_to_all | solution.py:35
  191.2 8.4 %fusion.34 = f32[80,1,1024]{2,1,0:T(1,128)S(1)} fusion(bf16[80,128,1024]{2,1,0:T(8,128)(2,1)} %param.9, bf16[80,128,1]{1,0,2:T(8,128)(2,1)S(1)} %fusion.6), kind=kOutput, calls=%fused_computation.57 | convolution fusion | flops 20971520 | bytes 21319680 | tf_op jit(solution)/shard_map/src,sr->sc/dot_general | solution.py:97
  199.6 0.7 fusion.11
  200.3 0.7 reshape_reshape_reshape.11
  201.6 4.4 %all_to_all.126 = f32[2,64,2048]{2,1,0:T(8,128)S(1)} all-to-all(f32[2,64,2048]{2,1,0:T(8,128)S(1)} %bitcast.123), channel_id=1, replica_groups=mesh['grp'=4,'dev_0'=4,'dev_1'=4,'dev_2'=2] {'dev_2'}, dimensions={0} | all-to-all | bytes 2097152 | tf_op jit(solution)/shard_map/all_to_all | solution.py:23
  206.7 4.6 %all-to-all-start.11 = ((f32[64,1,2]{2,1,0:T(1,128)}), f32[64,1,2]{2,1,0:T(1,128)S(1)}, u32[]{:S(2)}, u32[]{:S(2)}) async-start(f32[64,1,2]{2,1,0:T(1,128)} %broadcast_in_dim.99), calls=%async_computation.11 | async-start | bytes 65536 | tf_op jit(solution)/shard_map/all_to_all | solution.py:35
  211.4 1.2 all_to_all.93
  212.6 7.2 %all-to-all-done.11 = f32[64,1,2]{2,1,0:T(1,128)S(1)} async-done(((f32[64,1,2]{2,1,0:T(1,128)}), f32[64,1,2]{2,1,0:T(1,128)S(1)}, u32[]{:S(2)}, u32[]{:S(2)}) %all-to-all-start.11) | async-done | bytes 544 | tf_op jit(solution)/shard_map/all_to_all | solution.py:35
  219.8 4.7 %all-to-all-start.13 = ((f32[64,1,2048]{2,1,0:T(1,128)}), f32[64,1,2048]{2,1,0:T(1,128)S(1)}, u32[]{:S(2)}, u32[]{:S(2)}) async-start(f32[64,1,2048]{2,1,0:T(1,128)} %all_to_all.93), calls=%async_computation.13 | async-start | bytes 1048576 | tf_op jit(solution)/shard_map/all_to_all | solution.py:30
  224.4 0.8 copy.119
  227.5 8.0 %all-to-all-done.13 = f32[64,1,2048]{2,1,0:T(1,128)S(1)} async-done(((f32[64,1,2048]{2,1,0:T(1,128)}), f32[64,1,2048]{2,1,0:T(1,128)S(1)}, u32[]{:S(2)}, u32[]{:S(2)}) %all-to-all-start.13) | async-done | bytes 524320 | tf_op jit(solution)/shard_map/all_to_all | solution.py:30
  235.8 1.3 multiply_reduce_fusion
  237.1 1.1 broadcast_in_dim.100
  238.2 4.6 %all-to-all-start.14 = ((f32[64,1,2048]{2,1,0:T(1,128)}), f32[64,1,2048]{2,1,0:T(1,128)S(1)}, u32[]{:S(2)}, u32[]{:S(2)}) async-start(f32[64,1,2048]{2,1,0:T(1,128)} %broadcast_in_dim.100), calls=%async_computation.14 | async-start | bytes 1048576 | tf_op jit(solution)/shard_map/all_to_all | solution.py:35
  243.0 10.8 %all-to-all-done.14 = f32[64,1,2048]{2,1,0:T(1,128)S(1)} async-done(((f32[64,1,2048]{2,1,0:T(1,128)}), f32[64,1,2048]{2,1,0:T(1,128)S(1)}, u32[]{:S(2)}, u32[]{:S(2)}) %all-to-all-start.14) | async-done | bytes 524320 | tf_op jit(solution)/shard_map/all_to_all | solution.py:35
  254.1 8.5 %all_to_all.127 = f32[2,64,2048]{2,1,0:T(8,128)S(1)} all-to-all(f32[2,64,2048]{2,1,0:T(8,128)S(1)} %broadcast_in_dim.102), channel_id=1, replica_groups=mesh['grp'=4,'dev_0'=4,'dev_1'=4,'dev_2'=2] {'dev_2'}, dimensions={0} | all-to-all | bytes 2097152 | tf_op jit(solution)/shard_map/all_to_all | solution.py:35
  263.8 9.8 %fusion.14 = f32[80,1,128]{2,1,0:T(1,128)S(1)} fusion(bf16[80,128,1024]{2,1,0:T(8,128)(2,1)} %param.9, bf16[80,1024,1]{1,0,2:T(8,128)(2,1)S(1)} %fusion.3), kind=kOutput, calls=%fused_computation.35 | convolution fusion | flops 20971520 | bytes 21176320 | tf_op jit(solution)/shard_map/src,sc->sr/dot_general | solution.py:80
  273.6 0.8 fusion.76
  274.4 1.4 pad_maximum_fusion.2
  275.8 3.7 %all_to_all.128 = f32[2,1,2]{2,1,0:T(1,128)S(1)} all-to-all(f32[2,1,2]{2,1,0:T(1,128)S(1)} %broadcast_in_dim.105), channel_id=1, replica_groups=mesh['grp'=4,'dev_0'=4,'dev_1'=4,'dev_2'=2] {'dev_2'}, dimensions={0} | all-to-all | bytes 32 | tf_op jit(solution)/shard_map/all_to_all | solution.py:35
  280.2 4.6 %all-to-all-start.18 = ((f32[64,1,2]{2,1,0:T(1,128)}), f32[64,1,2]{2,1,0:T(1,128)S(1)}, u32[]{:S(2)}, u32[]{:S(2)}) async-start(f32[64,1,2]{2,1,0:T(1,128)} %broadcast_in_dim.106), calls=%async_computation.18 | async-start | bytes 65536 | tf_op jit(solution)/shard_map/all_to_all | solution.py:35
  284.8 0.8 copy.117
  285.6 1.0 copy.81
  286.7 1.2 gather_fusion
  287.8 5.4 %all-to-all-done.18 = f32[64,1,2]{2,1,0:T(1,128)S(1)} async-done(((f32[64,1,2]{2,1,0:T(1,128)}), f32[64,1,2]{2,1,0:T(1,128)S(1)}, u32[]{:S(2)}, u32[]{:S(2)}) %all-to-all-start.18) | async-done | bytes 544 | tf_op jit(solution)/shard_map/all_to_all | solution.py:35
  293.2 5.2 %all-to-all-start.16 = ((f32[32,1,128]{2,1,0:T(1,128)}), f32[32,1,128]{2,1,0:T(1,128)S(1)}, u32[]{:S(2)}, u32[]{:S(2)}) async-start(f32[32,1,128]{2,1,0:T(1,128)} %bitcast.41), calls=%async_computation.16 | async-start | bytes 32768 | tf_op jit(solution)/shard_map/all_to_all | solution.py:160
  300.6 4.9 %all-to-all-done.16 = f32[32,1,128]{2,1,0:T(1,128)S(1)} async-done(((f32[32,1,128]{2,1,0:T(1,128)}), f32[32,1,128]{2,1,0:T(1,128)S(1)}, u32[]{:S(2)}, u32[]{:S(2)}) %all-to-all-start.16) | async-done | bytes 16416 | tf_op jit(solution)/shard_map/all_to_all | solution.py:160
  (70 shorter events, 15.1 us)
Async XLA Ops:
  0.6 12.5 %copy-start.2 = (s32[80]{0:T(128)S(1)}, s32[80]{0:T(128)}, u32[]{:S(2)}) copy-start(s32[80]{0:T(128)} %param.10) | copy-start | bytes 964
  0.6 32.6 %copy-start = (f32[262144]{0:T(1024)S(1)}, f32[262144]{0:T(1024)}, u32[]{:S(2)}) copy-start(f32[262144]{0:T(1024)} %param.15) | copy-start | bytes 3145732
  22.0 23.5 %all-to-all-start.1 = ((f32[64,1,2048]{2,1,0:T(1,128)}), f32[64,1,2048]{2,1,0:T(1,128)S(1)}, u32[]{:S(2)}, u32[]{:S(2)}) async-start(f32[64,1,2048]{2,1,0:T(1,128)} %all_to_all.79), calls=%async_computation.1 | async-start | bytes 1048576 | tf_op jit(solution)/shard_map/all_to_all | solution.py:30
  48.2 15.7 %all-to-all-start.2 = ((f32[64,1,2048]{2,1,0:T(1,128)}), f32[64,1,2048]{2,1,0:T(1,128)S(1)}, u32[]{:S(2)}, u32[]{:S(2)}) async-start(f32[64,1,2048]{2,1,0:T(1,128)} %broadcast_in_dim.88), calls=%async_computation.2 | async-start | bytes 1048576 | tf_op jit(solution)/shard_map/all_to_all | solution.py:35
  71.7 11.0 %copy-start.1 = (bf16[4096]{0:T(1024)(128)(2,1)S(1)}, bf16[4096]{0:T(1024)(128)(2,1)}, u32[]{:S(2)}) copy-start(bf16[4096]{0:T(1024)(128)(2,1)} %param.13) | copy-start | bytes 24580
  71.7 17.2 %copy-start.3 = (bf16[4096]{0:T(1024)(128)(2,1)S(1)}, bf16[4096]{0:T(1024)(128)(2,1)}, u32[]{:S(2)}) copy-start(bf16[4096]{0:T(1024)(128)(2,1)} %param.14) | copy-start | bytes 24580
  104.9 16.2 %all-to-all-start.5 = ((f32[64,1,2]{2,1,0:T(1,128)}), f32[64,1,2]{2,1,0:T(1,128)S(1)}, u32[]{:S(2)}, u32[]{:S(2)}) async-start(f32[64,1,2]{2,1,0:T(1,128)} %broadcast_in_dim.94), calls=%async_computation.5 | async-start | bytes 65536 | tf_op jit(solution)/shard_map/all_to_all | solution.py:35
  121.1 15.7 %all-to-all-start.7 = ((f32[64,1,2048]{2,1,0:T(1,128)}), f32[64,1,2048]{2,1,0:T(1,128)S(1)}, u32[]{:S(2)}, u32[]{:S(2)}) async-start(f32[64,1,2048]{2,1,0:T(1,128)} %all_to_all.86), calls=%async_computation.7 | async-start | bytes 1048576 | tf_op jit(solution)/shard_map/all_to_all | solution.py:30
  139.5 15.6 %all-to-all-start.8 = ((f32[64,1,2048]{2,1,0:T(1,128)}), f32[64,1,2048]{2,1,0:T(1,128)S(1)}, u32[]{:S(2)}, u32[]{:S(2)}) async-start(f32[64,1,2048]{2,1,0:T(1,128)} %broadcast_in_dim.95), calls=%async_computation.8 | async-start | bytes 1048576 | tf_op jit(solution)/shard_map/all_to_all | solution.py:35
  191.2 51.6 %copy-start.4 = (s32[32]{0:T(128)S(1)}, s32[32]{0:T(128)}, u32[]{:S(2)}) copy-start(s32[32]{0:T(128)} %param.12) | copy-start | bytes 388
  206.7 13.1 %all-to-all-start.11 = ((f32[64,1,2]{2,1,0:T(1,128)}), f32[64,1,2]{2,1,0:T(1,128)S(1)}, u32[]{:S(2)}, u32[]{:S(2)}) async-start(f32[64,1,2]{2,1,0:T(1,128)} %broadcast_in_dim.99), calls=%async_computation.11 | async-start | bytes 65536 | tf_op jit(solution)/shard_map/all_to_all | solution.py:35
  219.8 15.7 %all-to-all-start.13 = ((f32[64,1,2048]{2,1,0:T(1,128)}), f32[64,1,2048]{2,1,0:T(1,128)S(1)}, u32[]{:S(2)}, u32[]{:S(2)}) async-start(f32[64,1,2048]{2,1,0:T(1,128)} %all_to_all.93), calls=%async_computation.13 | async-start | bytes 1048576 | tf_op jit(solution)/shard_map/all_to_all | solution.py:30
  238.2 15.6 %all-to-all-start.14 = ((f32[64,1,2048]{2,1,0:T(1,128)}), f32[64,1,2048]{2,1,0:T(1,128)S(1)}, u32[]{:S(2)}, u32[]{:S(2)}) async-start(f32[64,1,2048]{2,1,0:T(1,128)} %broadcast_in_dim.100), calls=%async_computation.14 | async-start | bytes 1048576 | tf_op jit(solution)/shard_map/all_to_all | solution.py:35
  280.2 13.1 %all-to-all-start.18 = ((f32[64,1,2]{2,1,0:T(1,128)}), f32[64,1,2]{2,1,0:T(1,128)S(1)}, u32[]{:S(2)}, u32[]{:S(2)}) async-start(f32[64,1,2]{2,1,0:T(1,128)} %broadcast_in_dim.106), calls=%async_computation.18 | async-start | bytes 65536 | tf_op jit(solution)/shard_map/all_to_all | solution.py:35
  293.2 12.2 %all-to-all-start.16 = ((f32[32,1,128]{2,1,0:T(1,128)}), f32[32,1,128]{2,1,0:T(1,128)S(1)}, u32[]{:S(2)}, u32[]{:S(2)}) async-start(f32[32,1,128]{2,1,0:T(1,128)} %bitcast.41), calls=%async_computation.16 | async-start | bytes 32768 | tf_op jit(solution)/shard_map/all_to_all | solution.py:160
where the time goes:
time: 312 us; the launch traced here: 307 us
  waiting for transfers between devices  75.1 us (24%)
  matrix products  71.7 us (23%)
  blocking collectives  60.6 us (19%)
  starting transfers between devices  56.7 us (18%)
  local copies, waits for them, and re-layouts  24.1 us (8%)
  other arithmetic  12.3 us (4%)
  between operations  6.81 us (2%)
    all_to_all x6, blocking collectives, copy_for_each(): lax.all_to_all(jnp.broadcast_to(array[None], (length, *array.shape)), axi...  46 us
    all_to_all x6, waiting for transfers between devices, copy_for_each(): lax.all_to_all(jnp.broadcast_to(array[None], (length, *array.shape)), axi...  42.7 us
    dot_general x4, matrix products, row_products(): jnp.einsum('src,sc->sr', tile_set, picked, preferred_element_type=jnp.flo...  39.3 us
    all_to_all x6, starting transfers between devices, copy_for_each(): lax.all_to_all(jnp.broadcast_to(array[None], (length, *array.shape)), axi...  31 us
    all_to_all x3, waiting for transfers between devices, sum_by_axis(): return jnp.sum(lax.all_to_all(own, far, 0, 0, tiled=True), axis=0)  27.6 us
    dot_general x3, matrix products, column_products(): jnp.einsum('src,sr->sc', tile_set, picked_rows, preferred_element_type=jn...  25.3 us
    all_to_all x3, starting transfers between devices, sum_by_axis(): return jnp.sum(lax.all_to_all(own, far, 0, 0, tiled=True), axis=0)  20.6 us
    all_to_all x3, blocking collectives, summed_on_arrival(): lax.all_to_all(in_blocks(array, dim, length), axis, 0, 0, tiled=True)  14.6 us
  transfers between devices with their start and end apart: 10, of which 10 were waited for; matrix products, arithmetic and copies ran while one was open for 6% of the time, Pallas kernels for 0%

commit v1 on v0

v1 whole, which is shorter than its diff:
```python
import jax
import jax.numpy as jnp
from jax import lax
from jax.experimental import pallas as pl
from jax.experimental.pallas import tpu as pltpu
from jax.sharding import Mesh
from jax.sharding import PartitionSpec as P

ITERS = 3
STEP = 0.3
TINY = 1e-06
BLOCKS = 32
SLOTS = 80
TR = 128
CB = 1024
COL_BLOCKS = 256
ROWS_P = 2048
CHIPS = 64
SHARE = 16
DMA_TILES = 8
UNROLL = 8

CHIP = ("grp", "dev_0", "dev_1")
CORE = "dev_2"
ALL = ("grp", "dev_0", "dev_1", "dev_2")
SWAP = [(0, 1), (1, 0)]
MIB = 1 << 20

f32 = jnp.float32
bf16 = jnp.bfloat16


def round_bf16(x):
    return x.astype(bf16).astype(f32)


def row_phase(count_ref, column_ref, tile_ref, table_ref, acc_ref, owner_ref, image_ref, arrive):
    def clear(s, carry):
        owner_ref[s] = BLOCKS
        return carry

    lax.fori_loop(0, SLOTS, clear, 0)

    def block(b, start):
        stop = start + count_ref[b]

        def tile(s, acc):
            arrive(s)
            owner_ref[s] = b
            col = column_ref[s]
            entries = [
                jnp.broadcast_to(table_ref[col, pl.ds(part, 1), :], (8, 128)) for part in range(8)
            ]
            out = []
            for g in range(TR // 8):
                rows = tile_ref[s, pl.ds(8 * g, 8), :].astype(f32)
                a = acc[g]
                for part in range(8):
                    a = a + rows[:, 128 * part : 128 * part + 128] * entries[part]
                out.append(a)
            return tuple(out)

        zero = tuple(jnp.zeros((8, 128), f32) for _ in range(TR // 8))
        acc = lax.fori_loop(start, stop, tile, zero)
        for g in range(TR // 8):
            acc_ref[b, pl.ds(8 * g, 8), :] = acc[g]
        return stop

    total = lax.fori_loop(0, BLOCKS, block, 0)

    def reduce_block(i, carry):
        for u in range(4):
            b = i * 4 + u
            image_ref[pl.ds(b, 1), :] = jnp.sum(acc_ref[b].T, axis=0, keepdims=True)
        return carry

    lax.fori_loop(0, BLOCKS // 4, reduce_block, 0)
    return total


def spread_rows(dual, spread_ref):
    for b in range(BLOCKS):
        spread_ref[b] = jnp.broadcast_to(dual[b : b + 1, :], (16, TR)).astype(bf16)
    spread_ref[BLOCKS] = jnp.zeros((16, TR), bf16)


def column_phase(column_ref, tile_ref, spread_ref, owner_ref, core, share_ref, rows):
    def clear(i, carry):
        for h in range(2):
            share_ref[h, i, pl.ds(0, SHARE), :] = jnp.zeros((SHARE, 128), f32)
        return carry

    lax.fori_loop(0, CHIPS, clear, 0)
    sub = lax.broadcasted_iota(jnp.int32, (8, 128), 0)

    def step(i, carry):
        results = []
        for u in range(UNROLL):
            s = i * UNROLL + u
            out = jnp.dot(
                spread_ref[owner_ref[s]], tile_ref[s], preferred_element_type=f32
            )
            r = out[0:8, 0:128]
            for part in range(1, 8):
                r = jnp.where(sub == part, out[0:8, 128 * part : 128 * part + 128], r)
            results.append(r)
        for u in range(UNROLL):
            col = column_ref[i * UNROLL + u]
            side = jnp.bitwise_xor(jnp.right_shift(col, 7), core)
            chunk = jnp.bitwise_and(jnp.right_shift(col, 1), CHIPS - 1)
            row = pl.multiple_of(jnp.bitwise_and(col, 1) * 8, 8)
            share_ref[side, chunk, pl.ds(row, 8), :] += results[u]
        return carry

    lax.fori_loop(0, SLOTS // UNROLL, step, 0)


def first_kernel(
    count_ref, column_ref, place_ref, tiles_hbm, table_in, dual_in, primal_hbm, cost_hbm, upper_hbm,
    tile_ref, image_ref, share_ref, primal_ref, cost_ref, upper_ref,
    table_ref, acc_ref, spread_ref, owner_ref, tile_sem, slice_sem,
):
    copies = [
        pltpu.make_async_copy(
            tiles_hbm.at[pl.ds(i * DMA_TILES, DMA_TILES)],
            tile_ref.at[pl.ds(i * DMA_TILES, DMA_TILES)],
            tile_sem.at[i],
        )
        for i in range(SLOTS // DMA_TILES)
    ]
    for c in copies:
        c.start()
    start = pl.multiple_of(place_ref[1] * SHARE, SHARE)
    slices = [
        pltpu.make_async_copy(src.at[pl.ds(start, SHARE)], dst, slice_sem.at[i])
        for i, (src, dst) in enumerate(
            ((primal_hbm, primal_ref), (cost_hbm, cost_ref), (upper_hbm, upper_ref))
        )
    ]
    for c in slices:
        c.start()

    def fill(i, carry):
        table_ref[pl.ds(i * 8, 8)] = round_bf16(table_in[pl.ds(i * 8, 8)])
        return carry

    lax.fori_loop(0, COL_BLOCKS // 8, fill, 0)

    def arrive(s):
        for i in range(SLOTS // DMA_TILES):

            @pl.when(s == i * DMA_TILES)
            def _():
                copies[i].wait()

    total = row_phase(
        count_ref, column_ref, tile_ref, table_ref, acc_ref, owner_ref, image_ref, arrive
    )
    for i in range(SLOTS // DMA_TILES):

        @pl.when(i * DMA_TILES >= total)
        def _():
            copies[i].wait()

    spread_rows(dual_in[...].astype(f32), spread_ref)
    column_phase(column_ref, tile_ref, spread_ref, owner_ref, place_ref[0], share_ref, SHARE)
    for c in slices:
        c.wait()


def fill_table(own_ref, other_ref, core, table_ref):
    def fill(i, carry):
        for ref, side in ((own_ref, core), (other_ref, 1 - core)):
            part = ref[i].astype(f32) if ref.dtype == bf16 else round_bf16(ref[i])
            at = side * (COL_BLOCKS // 2) + 2 * i
            table_ref[at] = part[0:8]
            table_ref[at + 1] = part[8:16]
        return carry

    lax.fori_loop(0, CHIPS, fill, 0)


def dual_step(bounds_ref, dual_in, image_in, image_ref, change_in, sigma):
    bounds = bounds_ref[...].astype(f32)
    image = image_ref[...]
    dual = jnp.maximum(
        dual_in[...].astype(f32) + sigma * (bounds - (2.0 * image - image_in[...])), 0.0
    )
    short = jnp.maximum(bounds - image, 0.0)
    violation = jnp.sum(short * short)
    lane = lax.broadcasted_iota(jnp.int32, (8, 128), 1)
    scalars = jnp.where(lane == 0, violation, jnp.where(lane == 1, change_in[...], 0.0))
    return dual, scalars


def middle_kernel(
    count_ref, column_ref, place_ref, tile_ref, own_ref, other_ref, bounds_ref, dual_in, image_in,
    change_in, sigma_in,
    dual_ref, image_ref, share_ref,
    table_ref, acc_ref, spread_ref, owner_ref,
):
    core = place_ref[0]
    fill_table(own_ref, other_ref, core, table_ref)
    row_phase(
        count_ref, column_ref, tile_ref, table_ref, acc_ref, owner_ref, image_ref, lambda s: None
    )
    dual, scalars = dual_step(
        bounds_ref, dual_in, image_in, image_ref, change_in, sigma_in[0:1, :]
    )
    dual_ref[...] = dual
    spread_rows(dual, spread_ref)

    def put(i, carry):
        for h in range(2):
            share_ref[h, i, pl.ds(SHARE, 8), :] = scalars
        return carry

    lax.fori_loop(0, CHIPS, put, 0)
    column_phase(column_ref, tile_ref, spread_ref, owner_ref, core, share_ref, SHARE + 8)


def last_kernel(
    count_ref, column_ref, place_ref, target_ref, tile_ref, own_ref, other_ref, bounds_ref, dual_in,
    image_in, change_in, sigma_in,
    primal_ref, send_ref,
    table_ref, acc_ref, owner_ref, image_ref,
):
    core = place_ref[0]
    fill_table(own_ref, other_ref, core, table_ref)

    def lay(i, carry):
        for ref, side in ((own_ref, core), (other_ref, 1 - core)):
            at = pl.multiple_of((side * CHIPS + i) * SHARE, SHARE)
            primal_ref[pl.ds(at, SHARE), :] = ref[i]
        return carry

    lax.fori_loop(0, CHIPS, lay, 0)
    row_phase(
        count_ref, column_ref, tile_ref, table_ref, acc_ref, owner_ref, image_ref, lambda s: None
    )
    dual, scalars = dual_step(
        bounds_ref, dual_in, image_in, image_ref, change_in, sigma_in[0:1, :]
    )

    def put(i, carry):
        send_ref[i] = scalars
        return carry

    lax.fori_loop(0, 4 * BLOCKS, put, 0)
    sub = lax.broadcasted_iota(jnp.int32, (8, 128), 0)
    first = place_ref[2] * BLOCKS
    for b in range(BLOCKS):
        send_ref[first + target_ref[b]] = jnp.where(
            sub == 0, jnp.broadcast_to(dual[b : b + 1, :], (8, 128)), scalars
        )


def next_weight(weight, scalars):
    lane = lax.broadcasted_iota(jnp.int32, (8, 128), 1)
    violation = jnp.sum(jnp.where(lane == 0, scalars, 0.0), axis=1, keepdims=True)
    change = jnp.sum(jnp.where(lane == 1, scalars, 0.0), axis=1, keepdims=True)
    ratio = jnp.broadcast_to((violation + TINY) / (change + TINY), (8, 128))
    return jnp.sqrt(weight * jnp.sqrt(ratio))


def update_kernel(
    arrived_ref, primal_in, cost_ref, upper_ref, weight_in,
    primal_ref, send_ref, change_ref, weight_ref, sigma_ref,
):
    rows = arrived_ref.shape[1]

    def add(i, total):
        return total + arrived_ref[i]

    total = lax.fori_loop(0, CHIPS, add, jnp.zeros((rows, 128), f32), unroll=8)
    weight = weight_in[...]
    if rows > SHARE:
        weight = next_weight(weight, total[SHARE:, :])
    tau = STEP / weight[0:1, :]
    primal = primal_in[...]
    new = jnp.clip(primal - tau * (cost_ref[...] - total[:SHARE, :]), 0.0, upper_ref[...])
    primal_ref[...] = new
    moved = new - primal
    change_ref[...] = jnp.full((8, 128), jnp.sum(moved * moved), f32)
    weight_ref[...] = weight
    sigma_ref[...] = STEP * weight
    out = new.astype(send_ref.dtype)

    def put(i, carry):
        send_ref[i] = out
        return carry

    lax.fori_loop(0, CHIPS, put, 0, unroll=8)


def finish_kernel(place_ref, arrived_ref, weight_in, dual_ref, weight_ref):
    def add(i, total):
        return total + arrived_ref[i]

    total = lax.fori_loop(0, 4 * BLOCKS, add, jnp.zeros((8, 128), f32), unroll=8)
    total = jnp.broadcast_to(total[1:2, :], (8, 128))
    weight_ref[...] = next_weight(weight_in[...], total)
    first = place_ref[2] * BLOCKS
    for b in range(BLOCKS):
        dual_ref[pl.ds(b, 1), :] = arrived_ref[first + b, pl.ds(0, 1), :]


SMEM = pl.BlockSpec(memory_space=pltpu.SMEM)
VMEM = pl.BlockSpec(memory_space=pltpu.VMEM)
ANY = pl.BlockSpec(memory_space=pl.ANY)


def sds(shape, dtype=f32):
    return jax.ShapeDtypeStruct(shape, dtype)


def call(kernel, name, in_specs, out_shape, out_specs, scratch=(), limit=24):
    return pl.pallas_call(
        kernel,
        name=name,
        in_specs=in_specs,
        out_specs=out_specs,
        out_shape=out_shape,
        scratch_shapes=list(scratch),
        compiler_params=pltpu.CompilerParams(vmem_limit_bytes=limit * MIB),
    )


TABLE = pltpu.VMEM((COL_BLOCKS, 8, 128), f32)
ACC = pltpu.VMEM((BLOCKS, TR, 128), f32)
SPREAD = pltpu.VMEM((BLOCKS + 1, 16, TR), bf16)
OWNER = pltpu.SMEM((SLOTS,), jnp.int32)
TILES = (SLOTS, TR, CB)


def both_sides(share):
    other = lax.ppermute(share[1], CORE, SWAP)
    return lax.all_to_all(share[0] + other, CHIP, 0, 0, tiled=True)


def gathered(send):
    own = lax.all_to_all(send, CHIP, 0, 0, tiled=True)
    return own, lax.ppermute(own, CORE, SWAP)


def per_device(
    matrix_tiles,
    tile_column,
    block_counts,
    destination,
    row_bounds,
    dual_start,
    primal_start,
    cost_vector,
    upper_bound,
):
    core = lax.axis_index(CORE)
    place = jnp.stack(
        [core, core * CHIPS + lax.axis_index(CHIP), lax.axis_index("grp")]
    ).astype(jnp.int32)
    bounds = row_bounds.reshape(BLOCKS, TR)
    dual = dual_start.reshape(BLOCKS, TR)
    wide = (ROWS_P, 128)

    tiles, image, share, primal, cost, upper = call(
        first_kernel,
        "first_pass",
        [SMEM, SMEM, SMEM, ANY, VMEM, VMEM, ANY, ANY, ANY],
        (
            pltpu.VMEM(TILES, bf16),
            sds((BLOCKS, TR)),
            sds((2, CHIPS, SHARE, 128)),
            sds((SHARE, 128)),
            sds((SHARE, 128)),
            sds((SHARE, 128)),
        ),
        (VMEM,) * 6,
        (TABLE, ACC, SPREAD, OWNER, pltpu.SemaphoreType.DMA((SLOTS // DMA_TILES,)),
         pltpu.SemaphoreType.DMA((3,))),
    )(
        block_counts, tile_column, place, matrix_tiles,
        primal_start.reshape(COL_BLOCKS, 8, 128), dual,
        primal_start.reshape(wide), cost_vector.reshape(wide), upper_bound.reshape(wide),
    )

    weight = jnp.ones((8, 128), f32)
    for iteration in range(ITERS):
        last = iteration == ITERS - 1
        arrived = both_sides(share)
        primal, send, change, weight, sigma = call(
            update_kernel,
            "update",
            [VMEM] * 5,
            (
                sds((SHARE, 128)),
                sds((CHIPS, SHARE, 128), f32 if last else bf16),
                sds((8, 128)),
                sds((8, 128)),
                sds((8, 128)),
            ),
            (VMEM,) * 5,
            limit=8,
        )(arrived, primal, cost, upper, weight)
        own, other = gathered(send)
        if not last:
            dual, image, share = call(
                middle_kernel,
                "middle_pass",
                [SMEM] * 3 + [VMEM] * 8,
                (sds((BLOCKS, TR)), sds((BLOCKS, TR)), sds((2, CHIPS, SHARE + 8, 128))),
                (VMEM,) * 3,
                (TABLE, ACC, SPREAD, OWNER),
            )(block_counts, tile_column, place, tiles, own, other, bounds, dual, image, change, sigma)
    primal_final, send = call(
        last_kernel,
        "last_pass",
        [SMEM] * 4 + [VMEM] * 8,
        (sds(wide), sds((4 * BLOCKS, 8, 128))),
        (VMEM,) * 2,
        (TABLE, ACC, OWNER, pltpu.VMEM((BLOCKS, TR), f32)),
    )(
        block_counts, tile_column, place, destination, tiles, own, other, bounds, dual, image,
        change, sigma,
    )
    arrived = lax.all_to_all(send, ALL, 0, 0, tiled=True)
    dual_final, weight = call(
        finish_kernel,
        "finish",
        [SMEM, VMEM, VMEM],
        (sds((BLOCKS, TR)), sds((8, 128))),
        (VMEM, VMEM),
        limit=8,
    )(place, arrived, weight)
    return (primal_final.reshape(-1), dual_final.reshape(-1), weight[0, 0:1])


def solution(mesh):
    split = Mesh(
        mesh.devices.reshape(mesh.shape["grp"], 4, 4, 2), ("grp", "dev_0", "dev_1", "dev_2")
    )
    return jax.shard_map(
        per_device,
        mesh=split,
        in_specs=(
            P(ALL, None, None),
            P(ALL),
            P(ALL),
            P(ALL),
            P(ALL),
            P(ALL),
            P(),
            P(),
            P(),
        ),
        out_specs=(P(), P(ALL), P()),
        check_vma=False,
    )
```

time: 312 us -> 224 us (0.72); the launches traced: 307 us -> 224 us
  matrix products: 71.7 us -> 0 us
  blocking collectives: 60.6 us -> 126 us
  waiting for transfers between devices: 75.1 us -> 10 us
  Pallas kernels: 0 us -> 50.1 us
  starting transfers between devices: 56.7 us -> 9.67 us
  other arithmetic: 12.3 us -> 0.33 us
  between operations: 6.81 us -> 0.76 us
  local copies, waits for them, and re-layouts: 24.1 us -> 27.3 us
    all_to_all x10 -> x0, waiting for transfers between devices: 75.1 us -> none  [the longest x6 42.7 us: copy_for_each(): lax.all_to_all(jnp.broadcast_to(array[None], (length, *array.shape)), axi...]
    dot_general x21 -> x0, matrix products: 71.7 us -> none  [the longest x4 39.3 us: row_products(): jnp.einsum('src,sc->sr', tile_set, picked, preferred_element_type=jnp.flo...]
    all_to_all x9 -> x7, blocking collectives: 60.6 us -> 126 us  [the longest x3 64.6 us: both_sides(): return lax.all_to_all(share[0] + other, CHIP, 0, 0, tiled=True)]
    all_to_all x10 -> x0, starting transfers between devices: 56.7 us -> none  [the longest x6 31 us: copy_for_each(): lax.all_to_all(jnp.broadcast_to(array[None], (length, *array.shape)), axi...]
    pallas_call x0 -> x8, Pallas kernels: none -> 50.1 us  [the longest x2 24.4 us: per_device(): call(middle_kernel, 'middle_pass', [SMEM] * 3 + [VMEM] * 8, (sds((BLOCKS,...]
    unnamed x17 -> x24, local copies, waits for them, and re-layouts: 2.3 us -> 26.6 us
    ppermute x0 -> x6, waiting for transfers between devices: none -> 10 us  [the longest x3 6.15 us: both_sides(): other = lax.ppermute(share[1], CORE, SWAP)]
    ppermute x0 -> x6, starting transfers between devices: none -> 9.67 us  [the longest x3 9.12 us: gathered(): return (own, lax.ppermute(own, CORE, SWAP))]
  transfers between devices with their start and end apart: 10 -> 6, of which waited for: 10 -> 6; matrix products, arithmetic and copies ran while one was open for 6% -> 0% of each run, Pallas kernels for 0% -> 0%
where the time goes in v1:
time: 224 us
  blocking collectives  126 us (56%)
  Pallas kernels  50.1 us (22%)
  local copies, waits for them, and re-layouts  27.3 us (12%)
  waiting for transfers between devices  10 us (4%)
  starting transfers between devices  9.67 us (4%)
    all_to_all x3, blocking collectives, both_sides(): return lax.all_to_all(share[0] + other, CHIP, 0, 0, tiled=True)  64.6 us
    all_to_all x3, blocking collectives, gathered(): own = lax.all_to_all(send, CHIP, 0, 0, tiled=True)  43.6 us
    unnamed x24, local copies, waits for them, and re-layouts  26.6 us
    pallas_call x2, Pallas kernels, per_device(): call(middle_kernel, 'middle_pass', [SMEM] * 3 + [VMEM] * 8, (sds((BLOCKS,...  24.4 us
    all_to_all x1, blocking collectives, per_device(): arrived = lax.all_to_all(send, ALL, 0, 0, tiled=True)  17.3 us
    pallas_call x1, Pallas kernels, per_device(): call(first_kernel, 'first_pass', [SMEM, SMEM, SMEM, ANY, VMEM, VMEM, ANY,...  13.1 us
    pallas_call x1, Pallas kernels, per_device(): call(last_kernel, 'last_pass', [SMEM] * 4 + [VMEM] * 8, (sds(wide), sds((...  9.78 us
    ppermute x3, starting transfers between devices, gathered(): return (own, lax.ppermute(own, CORE, SWAP))  9.12 us
  transfers between devices with their start and end apart: 6, of which 6 were waited for; matrix products, arithmetic and copies ran while one was open for 0% of the time, Pallas kernels for 0%

profile of v1, /device:TPU:1, one launch (start us, length us, event | category | flops | bytes accessed | tf_op | source)
XLA Modules:
  0.0 223.7 jit_solution(975978797893511924)
XLA Ops:
  0.6 0.1 pad_add_fusion.place_ref
  0.7 0.0 copy-start.3
  0.7 1.2 copy-done.3
  1.9 0.0 copy-start.4
  1.9 1.2 copy-done.4
  3.2 0.0 copy-start.5
  3.2 1.2 copy-done.5
  4.4 0.0 copy-start.7
  4.4 0.7 copy-done.7
  5.1 0.0 copy-start.9
  5.1 0.7 copy-done.9
  5.7 0.0 copy-start.10
  5.7 0.7 copy-done.10
  6.4 13.1 %first_pass.1 = (bf16[80,128,1024]{2,1,0:T(8,128)(2,1)S(1)}, f32[32,128]{1,0:T(8,128)S(1)}, f32[2,64,16,128]{3,2,1,0:T(8,128)S(1)}, f32[16,128]{1,0:T(8,128)S(1)...) custom-call(s32[32]{0:T(128)S(1)} %copy-done.9, s32[80]{0:T(128)S(1)} %copy-done.10, s32[3]{0:T(128)S(1)} %pad_add_fusion.place_ref, ...), custom_call_target="tpu_custom_call" | custom-call | tf_op jit(solution)/shard_map/first_pass/pallas_call | solution.py:365
  19.5 0.0 copy-start
  19.5 7.0 %copy-done = bf16[80,128,1024]{2,1,0:T(8,128)(2,1)} copy-done((bf16[80,128,1024]{2,1,0:T(8,128)(2,1)}, bf16[80,128,1024]{2,1,0:T(8,128)(2,1)S(1)}, u32[]{:S(2)}) %copy-start) | copy-done | bytes 20971544
  26.5 0.0 copy-start.6
  26.6 0.0 copy-start.8
  26.6 0.4 collective-permute-start
  27.0 1.6 collective-permute-done
  28.6 0.1 bitcast_add_fusion.2
  28.6 24.6 %all_to_all.35.arrived_ref = f32[64,16,128]{2,1,0:T(8,128)S(1)} all-to-all(f32[64,16,128]{2,1,0:T(8,128)S(1)} %bitcast_add_fusion.2), channel_id=1, replica_groups=mesh['grp'=4,'dev_0'=4,'dev_1'=4,'dev_2'=2] {'grp','dev_0','dev_1'}, dimensions={0} | all-to-all | bytes 1048576 | tf_op jit(solution)/shard_map/all_to_all | solution.py:338
  53.2 0.2 update.3
  53.5 13.9 %all_to_all.36.own_ref = bf16[64,16,128]{2,1,0:T(8,128)(2,1)S(1)} all-to-all(bf16[64,16,128]{2,1,0:T(8,128)(2,1)S(1)} %get-tuple-element.38), channel_id=1, replica_groups=mesh['grp'=4,'dev_0'=4,'dev_1'=4,'dev_2'=2] {'grp','dev_0','dev_1'}, dimensions={0} | all-to-all | bytes 524288 | tf_op jit(solution)/shard_map/all_to_all | solution.py:342
  67.4 3.3 %collective-permute-start.1 = (bf16[64,16,128]{2,1,0:T(8,128)(2,1)S(1)}, bf16[64,16,128]{2,1,0:T(8,128)(2,1)S(1)}, u32[]{:S(2)}, u32[]{:S(2)}) collective-permute-start(bf16[64,16,128]{2,1,0:T(8,128)(2,1)S(1)} %all_to_all.36.own_ref), channel_id=1, source_target_pairs={{0,1},{1,0},{2,3},{3,2},{4,5},{5,4},{6,7},{7,6},{8,9},{9,8},{10,11... | collective-permute-start | bytes 786440 | tf_op jit(solution)/shard_map/ppermute | solution.py:343
  70.6 1.2 collective-permute-done.1.other_ref
  71.8 0.0 copy-done.6
  71.8 0.0 copy-done.8
  71.8 0.0 copy-start.1
  71.8 7.0 %copy-done.1 = bf16[80,128,1024]{2,1,0:T(8,128)(2,1)S(1)} copy-done((bf16[80,128,1024]{2,1,0:T(8,128)(2,1)S(1)}, bf16[80,128,1024]{2,1,0:T(8,128)(2,1)}, u32[]{:S(2)}) %copy-start.1) | copy-done | bytes 20971544
  78.8 12.2 %middle_pass.2 = (f32[32,128]{1,0:T(8,128)S(1)}, f32[32,128]{1,0:T(8,128)S(1)}, f32[2,64,24,128]{3,2,1,0:T(8,128)S(1)}) custom-call(s32[32]{0:T(128)S(1)} %copy-done.9, s32[80]{0:T(128)S(1)} %copy-done.10, s32[3]{0:T(128)S(1)} %pad_add_fusion.place_ref, bf16[80,128,1024]{2,1,0:T(8,128)(2,1)S(1)} %copy-done.1, bf16[64,16,128]{2,1,0:T(8,128)(2,1)S(1)} %all_to_all.36.own_ref, ...), custom_call_target="tpu_custom_call" | custom-call | tf_op jit(solution)/shard_map/middle_pass/pallas_call | solution.py:406
  91.0 0.1 slice_bitcast_fusion.1
  91.0 0.1 collective-permute-start.2
  91.1 2.3 %collective-permute-done.2 = f32[64,24,128]{2,1,0:T(8,128)S(1)} collective-permute-done((f32[64,24,128]{2,1,0:T(8,128)S(1)}, f32[64,24,128]{2,1,0:T(8,128)S(1)}, u32[]{:S(2)}, u32[]{:S(2)}) %collective-permute-start.2) | collective-permute-done | bytes 786464 | tf_op jit(solution)/shard_map/ppermute | solution.py:337
  93.4 0.1 bitcast_add_fusion.1
  93.5 20.0 %all_to_all.37.arrived_ref = f32[64,24,128]{2,1,0:T(8,128)S(1)} all-to-all(f32[64,24,128]{2,1,0:T(8,128)S(1)} %bitcast_add_fusion.1), channel_id=1, replica_groups=mesh['grp'=4,'dev_0'=4,'dev_1'=4,'dev_2'=2] {'grp','dev_0','dev_1'}, dimensions={0} | all-to-all | bytes 1572864 | tf_op jit(solution)/shard_map/all_to_all | solution.py:338
  113.5 0.4 update.4
  113.9 13.9 %all_to_all.38.own_ref = bf16[64,16,128]{2,1,0:T(8,128)(2,1)S(1)} all-to-all(bf16[64,16,128]{2,1,0:T(8,128)(2,1)S(1)} %get-tuple-element.45), channel_id=1, replica_groups=mesh['grp'=4,'dev_0'=4,'dev_1'=4,'dev_2'=2] {'grp','dev_0','dev_1'}, dimensions={0} | all-to-all | bytes 524288 | tf_op jit(solution)/shard_map/all_to_all | solution.py:342
  127.8 3.0 %collective-permute-start.3 = (bf16[64,16,128]{2,1,0:T(8,128)(2,1)S(1)}, bf16[64,16,128]{2,1,0:T(8,128)(2,1)S(1)}, u32[]{:S(2)}, u32[]{:S(2)}) collective-permute-start(bf16[64,16,128]{2,1,0:T(8,128)(2,1)S(1)} %all_to_all.38.own_ref), channel_id=1, source_target_pairs={{0,1},{1,0},{2,3},{3,2},{4,5},{5,4},{6,7},{7,6},{8,9},{9,8},{10,11... | collective-permute-start | bytes 786440 | tf_op jit(solution)/shard_map/ppermute | solution.py:343
  130.7 1.2 collective-permute-done.3.other_ref
  131.9 0.0 copy-start.2
  131.9 7.0 %copy-done.2 = bf16[80,128,1024]{2,1,0:T(8,128)(2,1)S(1)} copy-done((bf16[80,128,1024]{2,1,0:T(8,128)(2,1)S(1)}, bf16[80,128,1024]{2,1,0:T(8,128)(2,1)}, u32[]{:S(2)}) %copy-start.2) | copy-done | bytes 20971544
  138.9 12.2 %middle_pass.3 = (f32[32,128]{1,0:T(8,128)S(1)}, f32[32,128]{1,0:T(8,128)S(1)}, f32[2,64,24,128]{3,2,1,0:T(8,128)S(1)}) custom-call(s32[32]{0:T(128)S(1)} %copy-done.9, s32[80]{0:T(128)S(1)} %copy-done.10, s32[3]{0:T(128)S(1)} %pad_add_fusion.place_ref, bf16[80,128,1024]{2,1,0:T(8,128)(2,1)S(1)} %copy-done.2, bf16[64,16,128]{2,1,0:T(8,128)(2,1)S(1)} %all_to_all.38.own_ref, ...), custom_call_target="tpu_custom_call" | custom-call | tf_op jit(solution)/shard_map/middle_pass/pallas_call | solution.py:406
  151.0 0.1 slice_bitcast_fusion
  151.1 0.1 collective-permute-start.4
  151.2 2.3 %collective-permute-done.4 = f32[64,24,128]{2,1,0:T(8,128)S(1)} collective-permute-done((f32[64,24,128]{2,1,0:T(8,128)S(1)}, f32[64,24,128]{2,1,0:T(8,128)S(1)}, u32[]{:S(2)}, u32[]{:S(2)}) %collective-permute-start.4) | collective-permute-done | bytes 786464 | tf_op jit(solution)/shard_map/ppermute | solution.py:337
  153.5 0.1 bitcast_add_fusion
  153.6 0.0 copy-start.11
  153.6 20.0 %all_to_all.39.arrived_ref = f32[64,24,128]{2,1,0:T(8,128)S(1)} all-to-all(f32[64,24,128]{2,1,0:T(8,128)S(1)} %bitcast_add_fusion), channel_id=1, replica_groups=mesh['grp'=4,'dev_0'=4,'dev_1'=4,'dev_2'=2] {'grp','dev_0','dev_1'}, dimensions={0} | all-to-all | bytes 1572864 | tf_op jit(solution)/shard_map/all_to_all | solution.py:338
  173.6 1.0 update.5
  174.6 15.8 %all_to_all.40.own_ref = f32[64,16,128]{2,1,0:T(8,128)S(1)} all-to-all(f32[64,16,128]{2,1,0:T(8,128)S(1)} %get-tuple-element.53), channel_id=1, replica_groups=mesh['grp'=4,'dev_0'=4,'dev_1'=4,'dev_2'=2] {'grp','dev_0','dev_1'}, dimensions={0} | all-to-all | bytes 1048576 | tf_op jit(solution)/shard_map/all_to_all | solution.py:342
  190.4 2.9 %collective-permute-start.5 = (f32[64,16,128]{2,1,0:T(8,128)S(1)}, f32[64,16,128]{2,1,0:T(8,128)S(1)}, u32[]{:S(2)}, u32[]{:S(2)}) collective-permute-start(f32[64,16,128]{2,1,0:T(8,128)S(1)} %all_to_all.40.own_ref), channel_id=1, source_target_pairs={{0,1},{1,0},{2,3},{3,2},{4,5},{5,4},{6,7},{7,6},{8,9},{9,8},{10,11... | collective-permute-start | bytes 1572872 | tf_op jit(solution)/shard_map/ppermute | solution.py:343
  193.2 1.5 collective-permute-done.5.other_ref
  194.8 0.0 copy-done.11
  194.8 9.8 %last_pass.1 = (f32[2048,128]{1,0:T(8,128)}, f32[128,8,128]{2,1,0:T(8,128)S(1)}) custom-call(s32[32]{0:T(128)S(1)} %copy-done.9, s32[80]{0:T(128)S(1)} %copy-done.10, s32[3]{0:T(128)S(1)} %pad_add_fusion.place_ref, s32[32]{0:T(128)S(1)} %copy-done.11, bf16[80,128,1024]{2,1,0:T(8,128)(2,1)S(1)} %copy-done.2, f32[64,16,128]{2,1,0:T(8,128)S(1)} %all_to_all.40.own_ref, ...), custom_call_target="tpu_custom_call" | custom-call | tf_op jit(solution)/shard_map/last_pass/pallas_call | solution.py:414
  204.6 17.3 %all_to_all.41.arrived_ref = f32[128,8,128]{2,1,0:T(8,128)S(1)} all-to-all(f32[128,8,128]{2,1,0:T(8,128)S(1)} %get-tuple-element.59), channel_id=1, replica_groups=mesh['grp'=4,'dev_0'=4,'dev_1'=4,'dev_2'=2] {'grp','dev_0','dev_1','dev_2'}, dimensions={0} | all-to-all | bytes 1048576 | tf_op jit(solution)/shard_map/all_to_all | solution.py:425
  221.9 1.3 finish.1
  223.2 0.5 slice.27
  (2 shorter events, 0.0 us)
Async XLA Ops:
  0.7 1.2 copy-start.3
  1.9 1.2 copy-start.4
  3.2 1.2 copy-start.5
  4.4 0.7 copy-start.7
  5.1 0.7 copy-start.9
  5.7 0.7 copy-start.10
  19.5 7.0 %copy-start = (bf16[80,128,1024]{2,1,0:T(8,128)(2,1)}, bf16[80,128,1024]{2,1,0:T(8,128)(2,1)S(1)}, u32[]{:S(2)}) copy-start(bf16[80,128,1024]{2,1,0:T(8,128)(2,1)S(1)} %get-tuple-element.33.tile_ref) | copy-start | bytes 62914564
  26.5 45.3 %copy-start.6 = (bf16[4096]{0:T(1024)(128)(2,1)S(1)}, bf16[4096]{0:T(1024)(128)(2,1)}, u32[]{:S(2)}) copy-start(bf16[4096]{0:T(1024)(128)(2,1)} %param.13) | copy-start | bytes 24580
  26.6 45.3 %copy-start.8 = (bf16[4096]{0:T(1024)(128)(2,1)S(1)}, bf16[4096]{0:T(1024)(128)(2,1)}, u32[]{:S(2)}) copy-start(bf16[4096]{0:T(1024)(128)(2,1)} %param.14) | copy-start | bytes 24580
  26.6 2.0 collective-permute-start
  67.4 4.4 %collective-permute-start.1 = (bf16[64,16,128]{2,1,0:T(8,128)(2,1)S(1)}, bf16[64,16,128]{2,1,0:T(8,128)(2,1)S(1)}, u32[]{:S(2)}, u32[]{:S(2)}) collective-permute-start(bf16[64,16,128]{2,1,0:T(8,128)(2,1)S(1)} %all_to_all.36.own_ref), channel_id=1, source_target_pairs={{0,1},{1,0},{2,3},{3,2},{4,5},{5,4},{6,7},{7,6},{8,9},{9,8},{10,11... | collective-permute-start | bytes 786440 | tf_op jit(solution)/shard_map/ppermute | solution.py:343
  71.8 7.0 %copy-start.1 = (bf16[80,128,1024]{2,1,0:T(8,128)(2,1)S(1)}, bf16[80,128,1024]{2,1,0:T(8,128)(2,1)}, u32[]{:S(2)}) copy-start(bf16[80,128,1024]{2,1,0:T(8,128)(2,1)} %copy-done) | copy-start | bytes 62914564
  91.0 2.4 %collective-permute-start.2 = (f32[64,24,128]{2,1,0:T(8,128)S(1)}, f32[64,24,128]{2,1,0:T(8,128)S(1)}, u32[]{:S(2)}, u32[]{:S(2)}) collective-permute-start(f32[64,24,128]{2,1,0:T(8,128)S(1)} %slice_bitcast_fusion.1), channel_id=1, source_target_pairs={{0,1},{1,0},{2,3},{3,2},{4,5},{5,4},{6,7},{7,6},{8,9},{9,8},{10,11... | collective-permute-start | bytes 2359304 | tf_op jit(solution)/shard_map/ppermute | solution.py:337
  127.8 4.1 %collective-permute-start.3 = (bf16[64,16,128]{2,1,0:T(8,128)(2,1)S(1)}, bf16[64,16,128]{2,1,0:T(8,128)(2,1)S(1)}, u32[]{:S(2)}, u32[]{:S(2)}) collective-permute-start(bf16[64,16,128]{2,1,0:T(8,128)(2,1)S(1)} %all_to_all.38.own_ref), channel_id=1, source_target_pairs={{0,1},{1,0},{2,3},{3,2},{4,5},{5,4},{6,7},{7,6},{8,9},{9,8},{10,11... | collective-permute-start | bytes 786440 | tf_op jit(solution)/shard_map/ppermute | solution.py:343
  131.9 7.0 %copy-start.2 = (bf16[80,128,1024]{2,1,0:T(8,128)(2,1)S(1)}, bf16[80,128,1024]{2,1,0:T(8,128)(2,1)}, u32[]{:S(2)}) copy-start(bf16[80,128,1024]{2,1,0:T(8,128)(2,1)} %copy-done) | copy-start | bytes 62914564
  151.1 2.4 %collective-permute-start.4 = (f32[64,24,128]{2,1,0:T(8,128)S(1)}, f32[64,24,128]{2,1,0:T(8,128)S(1)}, u32[]{:S(2)}, u32[]{:S(2)}) collective-permute-start(f32[64,24,128]{2,1,0:T(8,128)S(1)} %slice_bitcast_fusion), channel_id=1, source_target_pairs={{0,1},{1,0},{2,3},{3,2},{4,5},{5,4},{6,7},{7,6},{8,9},{9,8},{10,11... | collective-permute-start | bytes 2359304 | tf_op jit(solution)/shard_map/ppermute | solution.py:337
  153.6 41.2 %copy-start.11 = (s32[32]{0:T(128)S(1)}, s32[32]{0:T(128)}, u32[]{:S(2)}) copy-start(s32[32]{0:T(128)} %target_ref.1) | copy-start | bytes 388
  190.4 4.4 %collective-permute-start.5 = (f32[64,16,128]{2,1,0:T(8,128)S(1)}, f32[64,16,128]{2,1,0:T(8,128)S(1)}, u32[]{:S(2)}, u32[]{:S(2)}) collective-permute-start(f32[64,16,128]{2,1,0:T(8,128)S(1)} %all_to_all.40.own_ref), channel_id=1, source_target_pairs={{0,1},{1,0},{2,3},{3,2},{4,5},{5,4},{6,7},{7,6},{8,9},{9,8},{10,11... | collective-permute-start | bytes 1572872 | tf_op jit(solution)/shard_map/ppermute | solution.py:343

commit v2 on v1

v2 whole, which is shorter than its diff:
```python
import jax
import jax.numpy as jnp
from jax import lax
from jax.experimental import pallas as pl
from jax.experimental.pallas import tpu as pltpu
from jax.sharding import Mesh
from jax.sharding import PartitionSpec as P

ITERS = 3
STEP = 0.3
TINY = 1e-06
BLOCKS = 32
SLOTS = 80
TR = 128
CB = 1024
COL_BLOCKS = 256
ROWS_P = 2048
CHIPS = 64
SHARE = 16
CHUNK = 8
CHUNKS = SLOTS // CHUNK
ON_MXU = 2

CHIP = ("grp", "dev_0", "dev_1")
CORE = "dev_2"
ALL = ("grp", "dev_0", "dev_1", "dev_2")
SWAP = [(0, 1), (1, 0)]
MIB = 1 << 20
FIRST_LIMIT = 48
PASS_LIMIT = 48

f32 = jnp.float32
bf16 = jnp.bfloat16


def round_bf16(x):
    return x.astype(bf16).astype(f32)


def find_owners(count_ref, owner_ref):
    def clear(s, carry):
        owner_ref[s] = BLOCKS
        return carry

    def block(b, start):
        stop = start + count_ref[b]

        def slot(s, carry):
            owner_ref[s] = b
            return carry

        return lax.fori_loop(start, stop, slot, start) * 0 + stop

    lax.fori_loop(0, SLOTS, clear, 0)
    lax.fori_loop(0, BLOCKS, block, 0)


def row_tiles(slots, column_ref, owner_ref, tile_ref, table_ref, image_ref):
    results = []
    for u, s in enumerate(slots):
        col = column_ref[s]
        parts = [
            jnp.broadcast_to(table_ref[col, pl.ds(part, 1), :], (8, 128)) for part in range(8)
        ]
        if u < ON_MXU:
            left = jnp.concatenate(parts, axis=1).astype(bf16)
            r = 0.125 * lax.dot_general(
                left, tile_ref[s], (((1,), (1,)), ((), ())), preferred_element_type=f32
            )
        else:
            sums = []
            for g in range(TR // 8):
                rows = tile_ref[s, pl.ds(8 * g, 8), :].astype(f32)
                total = rows[:, 0:128] * parts[0]
                for part in range(1, 8):
                    total = total + rows[:, 128 * part : 128 * part + 128] * parts[part]
                sums.append(total)
            r = jnp.sum(jnp.concatenate(sums, axis=0).T.reshape(16, 8, 128), axis=0)
        results.append(r)
    for s, r in zip(slots, results):
        image_ref[owner_ref[s]] += r


def image_rows(image_ref):
    return jnp.concatenate(
        [jnp.sum(image_ref[b], axis=0, keepdims=True) for b in range(BLOCKS)], axis=0
    )


def column_tiles(slots, lefts, column_ref, tile_ref, sum_ref):
    sub = lax.broadcasted_iota(jnp.int32, (8, 128), 0)
    results = []
    for s, left in zip(slots, lefts):
        left = jnp.broadcast_to(left, (8, TR)).astype(bf16)
        out = jnp.dot(left, tile_ref[s], preferred_element_type=f32)
        r = out[:, 0:128]
        for part in range(1, 8):
            r = jnp.where(sub == part, out[:, 128 * part : 128 * part + 128], r)
        results.append(r)
    for s, r in zip(slots, results):
        sum_ref[column_ref[s]] += r


def clear_blocks(ref):
    n = ref.shape[0]

    def clear(i, carry):
        ref[i] = jnp.zeros((8, 128), f32)
        return carry

    lax.fori_loop(0, n, clear, 0, unroll=8 if n % 8 == 0 else 3)


def put_sums(sum_ref, core, own_ref, other_ref, scalars):
    def put(i, carry):
        for ref, side in ((own_ref, core), (other_ref, 1 - core)):
            at = side * (COL_BLOCKS // 2) + 2 * i
            ref[i, pl.ds(0, 8), :] = sum_ref[at]
            ref[i, pl.ds(8, 8), :] = sum_ref[at + 1]
            if scalars is not None:
                ref[i, pl.ds(SHARE, 8), :] = scalars
        return carry

    lax.fori_loop(0, CHIPS, put, 0, unroll=4)


def chunk_of(i):
    return [i * CHUNK + u for u in range(CHUNK)]


def tile_copies(tiles_hbm, tile_ref, sem):
    def chunk(i):
        return pltpu.make_async_copy(
            tiles_hbm.at[pl.ds(i * CHUNK, CHUNK)], tile_ref.at[pl.ds(i * CHUNK, CHUNK)], sem.at[i]
        )

    for i in range(CHUNKS):
        chunk(i).start()
    return chunk


def first_kernel(
    count_hbm, column_hbm, place_ref, tiles_hbm, dual_hbm, primal_hbm,
    owner_ref, image_out, own_ref, other_ref,
    count_ref, column_ref, dual_ref, wide_ref, table_ref, tile_ref, sum_ref, image_ref,
    tile_sem, side_sem,
):
    sides = [
        pltpu.make_async_copy(src, dst, side_sem.at[i])
        for i, (src, dst) in enumerate(
            (
                (count_hbm, count_ref),
                (column_hbm, column_ref),
                (dual_hbm, dual_ref),
                (primal_hbm, table_ref),
            )
        )
    ]
    for copy in sides:
        copy.start()
    arriving = tile_copies(tiles_hbm, tile_ref, tile_sem)
    clear_blocks(sum_ref)
    clear_blocks(image_ref)
    for copy in sides:
        copy.wait()
    find_owners(count_ref, owner_ref)
    wide_ref[pl.ds(0, BLOCKS), :] = dual_ref[...].astype(f32)
    wide_ref[pl.ds(BLOCKS, 8), :] = jnp.zeros((8, TR), f32)

    def fill(i, carry):
        table_ref[i] = round_bf16(table_ref[i])
        return carry

    lax.fori_loop(0, COL_BLOCKS, fill, 0, unroll=8)

    def step(i, carry):
        arriving(i).wait()
        slots = chunk_of(i)
        row_tiles(slots, column_ref, owner_ref, tile_ref, table_ref, image_ref)
        lefts = [wide_ref[pl.ds(owner_ref[s], 1), :] for s in slots]
        column_tiles(slots, lefts, column_ref, tile_ref, sum_ref)
        return carry

    lax.fori_loop(0, CHUNKS, step, 0)
    image_out[...] = image_rows(image_ref)
    put_sums(sum_ref, place_ref[0], own_ref, other_ref, None)


def merge_kernel(own_ref, other_ref, out_ref):
    def add(i, carry):
        out_ref[i] = own_ref[i] + other_ref[i]
        return carry

    lax.fori_loop(0, CHIPS, add, 0, unroll=8)


def fill_table(own_ref, other_ref, core, table_ref):
    def fill(i, carry):
        for ref, side in ((own_ref, core), (other_ref, 1 - core)):
            part = ref[i].astype(f32) if ref.dtype == bf16 else round_bf16(ref[i])
            at = side * (COL_BLOCKS // 2) + 2 * i
            table_ref[at] = part[0:8]
            table_ref[at + 1] = part[8:16]
        return carry

    lax.fori_loop(0, CHIPS, fill, 0, unroll=4)


def dual_step(bounds_ref, dual_in, image_before, image, change_in, sigma):
    bounds = bounds_ref[...]
    dual = jnp.maximum(
        dual_in[...] + sigma * (bounds - (2.0 * image - image_before)), 0.0
    )
    short = jnp.maximum(bounds - image, 0.0)
    violation = jnp.sum(short * short)
    lane = lax.broadcasted_iota(jnp.int32, (8, 128), 1)
    scalars = jnp.where(lane == 0, violation, jnp.where(lane == 1, change_in[...], 0.0))
    return dual, scalars


def middle_kernel(
    column_ref, owner_ref, place_ref, tiles_hbm, own_in, other_in, bounds_ref, dual_in,
    before_ref, change_in, sigma_in,
    dual_ref, image_out, own_ref, other_ref,
    table_ref, tile_ref, sum_ref, image_ref, tile_sem,
):
    core = place_ref[0]
    arriving = tile_copies(tiles_hbm, tile_ref, tile_sem)
    fill_table(own_in, other_in, core, table_ref)
    clear_blocks(sum_ref)
    clear_blocks(image_ref)
    sigma = sigma_in[0:1, :]

    def rows(i):
        arriving(i).wait()
        row_tiles(chunk_of(i), column_ref, owner_ref, tile_ref, table_ref, image_ref)

    def left(s):
        b = owner_ref[s]
        at = pl.ds(jnp.minimum(b, BLOCKS - 1), 1)
        image = jnp.sum(image_ref[b], axis=0, keepdims=True)
        move = bounds_ref[at, :] - (2.0 * image - before_ref[at, :])
        row = jnp.maximum(dual_in[at, :] + sigma * move, 0.0)
        return jnp.where(b < BLOCKS, row, 0.0)

    def columns(slots):
        column_tiles(slots, [left(s) for s in slots], column_ref, tile_ref, sum_ref)

    def early(i, carry):
        rows(i)
        return carry

    def step(i, carry):
        columns(chunk_of(i - 2))
        rows(i)
        return carry

    lax.fori_loop(0, 2, early, 0)
    lax.fori_loop(2, CHUNKS, step, 0)
    columns(chunk_of(CHUNKS - 2) + chunk_of(CHUNKS - 1))
    image = image_rows(image_ref)
    dual, scalars = dual_step(bounds_ref, dual_in, before_ref[...], image, change_in, sigma)
    image_out[...] = image
    dual_ref[...] = dual
    put_sums(sum_ref, core, own_ref, other_ref, scalars)


def last_kernel(
    column_ref, owner_ref, place_ref, target_ref, tiles_hbm, own_in, other_in, bounds_ref,
    dual_in, before_ref, change_in, sigma_in,
    primal_ref, send_ref,
    table_ref, tile_ref, image_ref, tile_sem,
):
    core = place_ref[0]
    arriving = tile_copies(tiles_hbm, tile_ref, tile_sem)
    fill_table(own_in, other_in, core, table_ref)
    clear_blocks(image_ref)

    def lay(i, carry):
        for ref, side in ((own_in, core), (other_in, 1 - core)):
            at = pl.multiple_of((side * CHIPS + i) * SHARE, SHARE)
            primal_ref[pl.ds(at, SHARE), :] = ref[i]
        return carry

    lax.fori_loop(0, CHIPS, lay, 0, unroll=4)

    def step(i, carry):
        arriving(i).wait()
        row_tiles(chunk_of(i), column_ref, owner_ref, tile_ref, table_ref, image_ref)
        return carry

    lax.fori_loop(0, CHUNKS, step, 0)
    dual, scalars = dual_step(
        bounds_ref, dual_in, before_ref[...], image_rows(image_ref), change_in, sigma_in[0:1, :]
    )

    def put(i, carry):
        send_ref[i] = scalars
        return carry

    lax.fori_loop(0, CHIPS, put, 0, unroll=8)
    first = place_ref[2] * (BLOCKS // 2)
    for b in range(BLOCKS):
        to = target_ref[b]
        send_ref[first + jnp.right_shift(to, 1), pl.ds(jnp.bitwise_and(to, 1), 1), :] = dual[
            b : b + 1, :
        ]


def next_weight(weight, scalars):
    lane = lax.broadcasted_iota(jnp.int32, (8, 128), 1)
    violation = jnp.sum(jnp.where(lane == 0, scalars, 0.0), axis=1, keepdims=True)
    change = jnp.sum(jnp.where(lane == 1, scalars, 0.0), axis=1, keepdims=True)
    ratio = jnp.broadcast_to((violation + TINY) / (change + TINY), (8, 128))
    return jnp.sqrt(weight * jnp.sqrt(ratio))


def update_kernel(first, *refs):
    if first:
        (arrived_ref, place_ref, primal_full, cost_full, upper_full,
         primal_ref, send_ref, change_ref, weight_ref, sigma_ref, cost_ref, upper_ref) = refs
        at = pl.ds(pl.multiple_of(place_ref[1] * SHARE, SHARE), SHARE)
        primal, cost, upper = primal_full[at, :], cost_full[at, :], upper_full[at, :]
        cost_ref[...] = cost
        upper_ref[...] = upper
    else:
        (arrived_ref, primal_in, cost_in, upper_in, weight_in,
         primal_ref, send_ref, change_ref, weight_ref, sigma_ref) = refs
        primal, cost, upper = primal_in[...], cost_in[...], upper_in[...]
    rows = arrived_ref.shape[1]

    def add(i, total):
        return total + arrived_ref[i]

    total = lax.fori_loop(0, CHIPS, add, jnp.zeros((rows, 128), f32), unroll=8)
    if first:
        weight = jnp.ones((8, 128), f32)
    else:
        weight = next_weight(weight_in[...], total[SHARE:, :])
    tau = STEP / weight[0:1, :]
    new = jnp.clip(primal - tau * (cost - total[:SHARE, :]), 0.0, upper)
    primal_ref[...] = new
    moved = new - primal
    change_ref[...] = jnp.full((8, 128), jnp.sum(moved * moved), f32)
    weight_ref[...] = weight
    sigma_ref[...] = STEP * weight
    out = new.astype(send_ref.dtype)

    def put(i, carry):
        send_ref[i] = out
        return carry

    lax.fori_loop(0, CHIPS, put, 0, unroll=8)


def finish_kernel(place_ref, same_ref, cross_ref, weight_in, dual_ref, weight_ref):
    def add(i, total):
        return total + (same_ref[i] + cross_ref[i])

    total = lax.fori_loop(0, CHIPS, add, jnp.zeros((8, 128), f32), unroll=8)
    total = jnp.broadcast_to(total[2:3, :], (8, 128))
    weight_ref[...] = next_weight(weight_in[...], total)
    core = place_ref[0]
    first = place_ref[2] * (BLOCKS // 2)
    for chip in range(BLOCKS // 2):
        same = same_ref[first + chip, pl.ds(core, 1), :]
        cross = cross_ref[first + chip, pl.ds(core, 1), :]
        dual_ref[pl.ds(2 * chip + core, 1), :] = same
        dual_ref[pl.ds(2 * chip + 1 - core, 1), :] = cross


SMEM = pl.BlockSpec(memory_space=pltpu.SMEM)
VMEM = pl.BlockSpec(memory_space=pltpu.VMEM)
ANY = pl.BlockSpec(memory_space=pl.ANY)


def sds(shape, dtype=f32):
    return jax.ShapeDtypeStruct(shape, dtype)


def call(kernel, name, in_specs, out_shape, out_specs, scratch=(), limit=8):
    return pl.pallas_call(
        kernel,
        name=name,
        in_specs=in_specs,
        out_specs=out_specs,
        out_shape=out_shape,
        scratch_shapes=list(scratch),
        compiler_params=pltpu.CompilerParams(vmem_limit_bytes=limit * MIB),
    )


TILE = pltpu.VMEM((SLOTS, TR, CB), bf16)
TABLE = pltpu.VMEM((COL_BLOCKS, 8, 128), f32)
IMAGE = pltpu.VMEM((BLOCKS + 1, 8, 128), f32)
DMA = pltpu.SemaphoreType.DMA


def summed(own, other):
    crossed = lax.ppermute(other, CORE, SWAP)
    merged = call(merge_kernel, "merge", [VMEM] * 2, sds(own.shape), VMEM, limit=4)(own, crossed)
    return lax.all_to_all(merged, CHIP, 0, 0, tiled=True)


def gathered(send):
    own = lax.all_to_all(send, CHIP, 0, 0, tiled=True)
    return own, lax.ppermute(own, CORE, SWAP)


def per_device(
    matrix_tiles,
    tile_column,
    block_counts,
    destination,
    row_bounds,
    dual_start,
    primal_start,
    cost_vector,
    upper_bound,
):
    core = lax.axis_index(CORE)
    place = jnp.stack(
        [core, core * CHIPS + lax.axis_index(CHIP), lax.axis_index("grp")]
    ).astype(jnp.int32)
    bounds = row_bounds.astype(f32).reshape(BLOCKS, TR)
    dual_bf = dual_start.reshape(BLOCKS, TR)
    dual = dual_bf.astype(f32)
    wide = (ROWS_P, 128)
    part = sds((SHARE, 128))
    tiny = sds((8, 128))

    owners, before, own, other = call(
        first_kernel,
        "first_pass",
        [ANY, ANY, SMEM, ANY, ANY, ANY],
        (
            sds((SLOTS,), jnp.int32),
            sds((BLOCKS, TR)),
            sds((CHIPS, SHARE, 128)),
            sds((CHIPS, SHARE, 128)),
        ),
        (SMEM, VMEM, VMEM, VMEM),
        (
            pltpu.SMEM((BLOCKS,), jnp.int32),
            pltpu.SMEM((SLOTS,), jnp.int32),
            pltpu.VMEM((BLOCKS, TR), bf16),
            pltpu.VMEM((BLOCKS + 8, TR), f32),
            TABLE,
            TILE,
            TABLE,
            IMAGE,
            DMA((CHUNKS,)),
            DMA((4,)),
        ),
        limit=FIRST_LIMIT,
    )(
        block_counts, tile_column, place, matrix_tiles, dual_bf,
        primal_start.reshape(COL_BLOCKS, 8, 128),
    )

    for iteration in range(ITERS):
        first, last = iteration == 0, iteration == ITERS - 1
        arrived = summed(own, other)
        send_shape = sds((CHIPS, SHARE, 128), f32 if last else bf16)
        if first:
            primal, send, change, weight, sigma, cost, upper = call(
                lambda *refs: update_kernel(True, *refs),
                "update",
                [VMEM, SMEM] + [VMEM] * 3,
                (part, send_shape, tiny, tiny, tiny, part, part),
                (VMEM,) * 7,
                limit=4,
            )(
                arrived, place, primal_start.reshape(wide), cost_vector.reshape(wide),
                upper_bound.reshape(wide),
            )
        else:
            primal, send, change, weight, sigma = call(
                lambda *refs: update_kernel(False, *refs),
                "update",
                [VMEM] * 5,
                (part, send_shape, tiny, tiny, tiny),
                (VMEM,) * 5,
                limit=4,
            )(arrived, primal, cost, upper, weight)
        near, far = gathered(send)
        if last:
            break
        dual, before, own, other = call(
            middle_kernel,
            "middle_pass",
            [SMEM] * 3 + [ANY] + [VMEM] * 7,
            (sds((BLOCKS, TR)), sds((BLOCKS, TR)))
            + (sds((CHIPS, SHARE + 8, 128)),) * 2,
            (VMEM,) * 4,
            (TABLE, TILE, TABLE, IMAGE, DMA((CHUNKS,))),
            limit=PASS_LIMIT,
        )(
            tile_column, owners, place, matrix_tiles, near, far, bounds, dual, before, change,
            sigma,
        )
    primal_final, send = call(
        last_kernel,
        "last_pass",
        [SMEM] * 4 + [ANY] + [VMEM] * 7,
        (sds(wide), sds((CHIPS, 8, 128))),
        (VMEM,) * 2,
        (TABLE, TILE, IMAGE, DMA((CHUNKS,))),
        limit=PASS_LIMIT,
    )(
        tile_column, owners, place, destination, matrix_tiles, near, far, bounds, dual, before, change,
        sigma,
    )
    same, cross = gathered(send)
    dual_final, weight = call(
        finish_kernel,
        "finish",
        [SMEM, VMEM, VMEM, VMEM],
        (sds((BLOCKS, TR)), tiny),
        (VMEM, VMEM),
        limit=4,
    )(place, same, cross, weight)
    return (primal_final.reshape(-1), dual_final.reshape(-1), weight[0, 0:1])


def solution(mesh):
    split = Mesh(
        mesh.devices.reshape(mesh.shape["grp"], 4, 4, 2), ("grp", "dev_0", "dev_1", "dev_2")
    )
    return jax.shard_map(
        per_device,
        mesh=split,
        in_specs=(
            P(ALL, None, None),
            P(ALL),
            P(ALL),
            P(ALL),
            P(ALL),
            P(ALL),
            P(),
            P(),
            P(),
        ),
        out_specs=(P(), P(ALL), P()),
        check_vma=False,
    )
```

time: 224 us -> 193 us (0.86)
  local copies, waits for them, and re-layouts: 27.3 us -> 3.76 us
  blocking collectives: 126 us -> 120 us
  Pallas kernels: 50.1 us -> 44.3 us
  starting transfers between devices: 9.67 us -> 13.5 us
    unnamed x24 -> x16, local copies, waits for them, and re-layouts: 26.6 us -> 3.25 us
    all_to_all x4 -> x3, blocking collectives: 81.9 us -> 61.7 us  [summed(): return lax.all_to_all(merged, CHIP, 0, 0, tiled=True)]
    all_to_all x3 -> x4, blocking collectives: 43.6 us -> 57.9 us  [gathered(): own = lax.all_to_all(send, CHIP, 0, 0, tiled=True)]
    pallas_call x8 -> x11, Pallas kernels: 50.1 us -> 44.3 us  [the longest x2 21.1 us: per_device(): call(middle_kernel, 'middle_pass', [SMEM] * 3 + [ANY] + [VMEM] * 7, (sds(...]
    ppermute x3 -> x4, starting transfers between devices: 9.12 us -> 11 us  [gathered(): return (own, lax.ppermute(own, CORE, SWAP))]
    ppermute x3 -> x4, waiting for transfers between devices: 3.86 us -> 5.01 us  [gathered(): return (own, lax.ppermute(own, CORE, SWAP))]
  transfers between devices with their start and end apart: 6 -> 7, of which waited for: 6 -> 7; matrix products, arithmetic and copies ran while one was open for 0% -> 0% of each run, Pallas kernels for 0% -> 0%
where the time goes in v2:
time: 193 us; the launch traced here: 192 us
  blocking collectives  120 us (62%)
  Pallas kernels  44.3 us (23%)
  starting transfers between devices  13.5 us (7%)
  waiting for transfers between devices  10.4 us (5%)
  local copies, waits for them, and re-layouts  3.76 us (2%)
    all_to_all x3, blocking collectives, summed(): return lax.all_to_all(merged, CHIP, 0, 0, tiled=True)  61.7 us
    all_to_all x4, blocking collectives, gathered(): own = lax.all_to_all(send, CHIP, 0, 0, tiled=True)  57.9 us
    pallas_call x2, Pallas kernels, per_device(): call(middle_kernel, 'middle_pass', [SMEM] * 3 + [ANY] + [VMEM] * 7, (sds(...  21.1 us
    ppermute x4, starting transfers between devices, gathered(): return (own, lax.ppermute(own, CORE, SWAP))  11 us
    pallas_call x1, Pallas kernels, per_device(): call(first_kernel, 'first_pass', [ANY, ANY, SMEM, ANY, ANY, ANY], (sds((S...  10.2 us
    pallas_call x1, Pallas kernels, per_device(): call(last_kernel, 'last_pass', [SMEM] * 4 + [ANY] + [VMEM] * 7, (sds(wide...  9.34 us
    ppermute x3, waiting for transfers between devices, summed(): crossed = lax.ppermute(other, CORE, SWAP)  5.36 us
    ppermute x4, waiting for transfers between devices, gathered(): return (own, lax.ppermute(own, CORE, SWAP))  5.01 us
  transfers between devices with their start and end apart: 7, of which 7 were waited for; matrix products, arithmetic and copies ran while one was open for 0% of the time, Pallas kernels for 0%

profile of v2, /device:TPU:1, one launch (start us, length us, event | category | flops | bytes accessed | tf_op | source)
XLA Modules:
  0.0 192.4 jit_solution(12957825365375838481)
XLA Ops:
  0.6 0.0 copy-start.7
  0.6 0.1 pad_add_fusion.place_ref.refs_1_
  0.7 0.0 copy-start
  0.7 1.2 copy-done
  2.0 0.0 copy-start.3
  2.0 0.7 copy-done.3
  2.7 0.0 copy-start.4
  2.7 0.7 copy-done.4
  3.3 0.0 copy-start.6
  3.3 0.7 copy-done.6
  4.0 0.0 copy-start.1
  4.0 0.0 copy-start.2
  4.0 10.2 %first_pass.1 = (s32[80]{0:T(128)S(1)}, f32[32,128]{1,0:T(8,128)S(1)}, f32[64,16,128]{2,1,0:T(8,128)S(1)}, f32[64,16,128]{2,1,0:T(8,128)S(1)}) custom-call(s32[32]{0:T(128)S(1)} %copy-done.6, s32[80]{0:T(128)S(1)} %copy-done.4, s32[3]{0:T(128)S(1)} %pad_add_fusion.place_ref.refs_1_, bf16[80,128,1024]{2,1,0:T(8,128)(2,1)} %tiles_hbm.7, ...), custom_call_target="tpu_custom_call" | custom-call | tf_op jit(solution)/shard_map/first_pass/pallas_call | solution.py:432
  14.2 1.5 collective-permute-start
  15.7 1.5 collective-permute-done.other_ref
  17.3 0.1 merge.3
  17.3 23.0 %all_to_all.35.refs_0_ = f32[64,16,128]{2,1,0:T(8,128)S(1)} all-to-all(f32[64,16,128]{2,1,0:T(8,128)S(1)} %merge.3), channel_id=1, replica_groups=mesh['grp'=4,'dev_0'=4,'dev_1'=4,'dev_2'=2] {'grp','dev_0','dev_1'}, dimensions={0} | all-to-all | bytes 1048576 | tf_op jit(solution)/shard_map/all_to_all | solution.py:402
  40.4 0.0 copy-done.1
  40.4 0.0 copy-done.2
  40.4 0.8 update.3
  41.2 13.9 %all_to_all.36.own_in = bf16[64,16,128]{2,1,0:T(8,128)(2,1)S(1)} all-to-all(bf16[64,16,128]{2,1,0:T(8,128)(2,1)S(1)} %get-tuple-element.38), channel_id=1, replica_groups=mesh['grp'=4,'dev_0'=4,'dev_1'=4,'dev_2'=2] {'grp','dev_0','dev_1'}, dimensions={0} | all-to-all | bytes 524288 | tf_op jit(solution)/shard_map/all_to_all | solution.py:406
  55.1 3.3 %collective-permute-start.1 = (bf16[64,16,128]{2,1,0:T(8,128)(2,1)S(1)}, bf16[64,16,128]{2,1,0:T(8,128)(2,1)S(1)}, u32[]{:S(2)}, u32[]{:S(2)}) collective-permute-start(bf16[64,16,128]{2,1,0:T(8,128)(2,1)S(1)} %all_to_all.36.own_in), channel_id=1, source_target_pairs={{0,1},{1,0},{2,3},{3,2},{4,5},{5,4},{6,7},{7,6},{8,9},{9,8},{10,11... | collective-permute-start | bytes 786440 | tf_op jit(solution)/shard_map/ppermute | solution.py:407
  58.3 0.0 copy-done.7
  58.3 1.2 collective-permute-done.1.other_in
  59.5 10.5 %middle_pass.2 = (f32[32,128]{1,0:T(8,128)S(1)}, f32[32,128]{1,0:T(8,128)S(1)}, f32[64,24,128]{2,1,0:T(8,128)S(1)}, f32[64,24,128]{2,1,0:T(8,128)S(1)}) custom-call(s32[80]{0:T(128)S(1)} %copy-done.4, s32[80]{0:T(128)S(1)} %get-tuple-element.35.owner_ref, s32[3]{0:T(128)S(1)} %pad_add_fusion.place_ref.refs_1_, bf16[80,128,1024]{2,1,0:T(8,128)(2,1)} %tiles_hbm.7, ...), custom_call_target="tpu_custom_call" | custom-call | tf_op jit(solution)/shard_map/middle_pass/pallas_call | solution.py:489
  70.0 0.0 copy-start.5
  70.0 0.5 collective-permute-start.2
  70.5 1.9 collective-permute-done.2.other_ref
  72.4 0.1 merge.4
  72.5 19.4 %all_to_all.37.refs_0_ = f32[64,24,128]{2,1,0:T(8,128)S(1)} all-to-all(f32[64,24,128]{2,1,0:T(8,128)S(1)} %merge.4), channel_id=1, replica_groups=mesh['grp'=4,'dev_0'=4,'dev_1'=4,'dev_2'=2] {'grp','dev_0','dev_1'}, dimensions={0} | all-to-all | bytes 1572864 | tf_op jit(solution)/shard_map/all_to_all | solution.py:402
  91.9 0.4 update.4
  92.2 14.1 %all_to_all.38.own_in = bf16[64,16,128]{2,1,0:T(8,128)(2,1)S(1)} all-to-all(bf16[64,16,128]{2,1,0:T(8,128)(2,1)S(1)} %get-tuple-element.48), channel_id=1, replica_groups=mesh['grp'=4,'dev_0'=4,'dev_1'=4,'dev_2'=2] {'grp','dev_0','dev_1'}, dimensions={0} | all-to-all | bytes 524288 | tf_op jit(solution)/shard_map/all_to_all | solution.py:406
  106.3 3.1 %collective-permute-start.3 = (bf16[64,16,128]{2,1,0:T(8,128)(2,1)S(1)}, bf16[64,16,128]{2,1,0:T(8,128)(2,1)S(1)}, u32[]{:S(2)}, u32[]{:S(2)}) collective-permute-start(bf16[64,16,128]{2,1,0:T(8,128)(2,1)S(1)} %all_to_all.38.own_in), channel_id=1, source_target_pairs={{0,1},{1,0},{2,3},{3,2},{4,5},{5,4},{6,7},{7,6},{8,9},{9,8},{10,11... | collective-permute-start | bytes 786440 | tf_op jit(solution)/shard_map/ppermute | solution.py:407
  109.4 1.2 collective-permute-done.3.other_in
  110.5 10.5 %middle_pass.3 = (f32[32,128]{1,0:T(8,128)S(1)}, f32[32,128]{1,0:T(8,128)S(1)}, f32[64,24,128]{2,1,0:T(8,128)S(1)}, f32[64,24,128]{2,1,0:T(8,128)S(1)}) custom-call(s32[80]{0:T(128)S(1)} %copy-done.4, s32[80]{0:T(128)S(1)} %get-tuple-element.35.owner_ref, s32[3]{0:T(128)S(1)} %pad_add_fusion.place_ref.refs_1_, bf16[80,128,1024]{2,1,0:T(8,128)(2,1)} %tiles_hbm.7, ...), custom_call_target="tpu_custom_call" | custom-call | tf_op jit(solution)/shard_map/middle_pass/pallas_call | solution.py:489
  121.1 0.5 collective-permute-start.4
  121.5 1.9 collective-permute-done.4.other_ref
  123.4 0.1 merge.5
  123.5 19.3 %all_to_all.39.refs_0_ = f32[64,24,128]{2,1,0:T(8,128)S(1)} all-to-all(f32[64,24,128]{2,1,0:T(8,128)S(1)} %merge.5), channel_id=1, replica_groups=mesh['grp'=4,'dev_0'=4,'dev_1'=4,'dev_2'=2] {'grp','dev_0','dev_1'}, dimensions={0} | all-to-all | bytes 1572864 | tf_op jit(solution)/shard_map/all_to_all | solution.py:402
  142.9 1.0 update.5
  143.9 15.7 %all_to_all.40.own_in = f32[64,16,128]{2,1,0:T(8,128)S(1)} all-to-all(f32[64,16,128]{2,1,0:T(8,128)S(1)} %get-tuple-element.57), channel_id=1, replica_groups=mesh['grp'=4,'dev_0'=4,'dev_1'=4,'dev_2'=2] {'grp','dev_0','dev_1'}, dimensions={0} | all-to-all | bytes 1048576 | tf_op jit(solution)/shard_map/all_to_all | solution.py:406
  159.6 3.1 %collective-permute-start.5 = (f32[64,16,128]{2,1,0:T(8,128)S(1)}, f32[64,16,128]{2,1,0:T(8,128)S(1)}, u32[]{:S(2)}, u32[]{:S(2)}) collective-permute-start(f32[64,16,128]{2,1,0:T(8,128)S(1)} %all_to_all.40.own_in), channel_id=1, source_target_pairs={{0,1},{1,0},{2,3},{3,2},{4,5},{5,4},{6,7},{7,6},{8,9},{9,8},{10,11... | collective-permute-start | bytes 1572872 | tf_op jit(solution)/shard_map/ppermute | solution.py:407
  162.7 1.5 collective-permute-done.5.other_in
  164.2 0.0 copy-done.5
  164.2 9.3 %last_pass.1 = (f32[2048,128]{1,0:T(8,128)}, f32[64,8,128]{2,1,0:T(8,128)S(1)}) custom-call(s32[80]{0:T(128)S(1)} %copy-done.4, s32[80]{0:T(128)S(1)} %get-tuple-element.35.owner_ref, s32[3]{0:T(128)S(1)} %pad_add_fusion.place_ref.refs_1_, s32[32]{0:T(128)S(1)} %copy-done.5, bf16[80,128,1024]{2,1,0:T(8,128)(2,1)} %tiles_hbm.7, ...), custom_call_target="tpu_custom_call" | custom-call | tf_op jit(solution)/shard_map/last_pass/pallas_call | solution.py:502
  173.6 14.3 %all_to_all.41.same_ref = f32[64,8,128]{2,1,0:T(8,128)S(1)} all-to-all(f32[64,8,128]{2,1,0:T(8,128)S(1)} %get-tuple-element.63), channel_id=1, replica_groups=mesh['grp'=4,'dev_0'=4,'dev_1'=4,'dev_2'=2] {'grp','dev_0','dev_1'}, dimensions={0} | all-to-all | bytes 524288 | tf_op jit(solution)/shard_map/all_to_all | solution.py:406
  187.8 1.6 collective-permute-start.6
  189.4 1.2 collective-permute-done.6.cross_ref
  190.6 1.3 finish.1
  191.9 0.5 slice.3
  (2 shorter events, 0.0 us)
Async XLA Ops:
  0.6 57.7 %copy-start.7 = (bf16[4096]{0:T(1024)(128)(2,1)S(1)}, bf16[4096]{0:T(1024)(128)(2,1)}, u32[]{:S(2)}) copy-start(bf16[4096]{0:T(1024)(128)(2,1)} %param.13) | copy-start | bytes 24580
  0.7 1.2 copy-start
  2.0 0.7 copy-start.3
  2.7 0.7 copy-start.4
  3.3 0.7 copy-start.6
  4.0 36.4 %copy-start.1 = (f32[262144]{0:T(1024)S(1)}, f32[262144]{0:T(1024)}, u32[]{:S(2)}) copy-start(f32[262144]{0:T(1024)} %param.16) | copy-start | bytes 3145732
  4.0 36.4 %copy-start.2 = (f32[262144]{0:T(1024)S(1)}, f32[262144]{0:T(1024)}, u32[]{:S(2)}) copy-start(f32[262144]{0:T(1024)} %param.17) | copy-start | bytes 3145732
  14.2 3.0 %collective-permute-start = (f32[64,16,128]{2,1,0:T(8,128)S(1)}, f32[64,16,128]{2,1,0:T(8,128)S(1)}, u32[]{:S(2)}, u32[]{:S(2)}) collective-permute-start(f32[64,16,128]{2,1,0:T(8,128)S(1)} %get-tuple-element.37), channel_id=1, source_target_pairs={{0,1},{1,0},{2,3},{3,2},{4,5},{5,4},{6,7},{7,6},{8,9},{9,8},{10,11... | collective-permute-start | bytes 1572872 | tf_op jit(solution)/shard_map/ppermute | solution.py:400
  55.1 4.4 %collective-permute-start.1 = (bf16[64,16,128]{2,1,0:T(8,128)(2,1)S(1)}, bf16[64,16,128]{2,1,0:T(8,128)(2,1)S(1)}, u32[]{:S(2)}, u32[]{:S(2)}) collective-permute-start(bf16[64,16,128]{2,1,0:T(8,128)(2,1)S(1)} %all_to_all.36.own_in), channel_id=1, source_target_pairs={{0,1},{1,0},{2,3},{3,2},{4,5},{5,4},{6,7},{7,6},{8,9},{9,8},{10,11... | collective-permute-start | bytes 786440 | tf_op jit(solution)/shard_map/ppermute | solution.py:407
  70.0 94.2 %copy-start.5 = (s32[32]{0:T(128)S(1)}, s32[32]{0:T(128)}, u32[]{:S(2)}) copy-start(s32[32]{0:T(128)} %target_ref.1) | copy-start | bytes 388
  70.0 2.4 %collective-permute-start.2 = (f32[64,24,128]{2,1,0:T(8,128)S(1)}, f32[64,24,128]{2,1,0:T(8,128)S(1)}, u32[]{:S(2)}, u32[]{:S(2)}) collective-permute-start(f32[64,24,128]{2,1,0:T(8,128)S(1)} %get-tuple-element.43), channel_id=1, source_target_pairs={{0,1},{1,0},{2,3},{3,2},{4,5},{5,4},{6,7},{7,6},{8,9},{9,8},{10,11... | collective-permute-start | bytes 2359304 | tf_op jit(solution)/shard_map/ppermute | solution.py:400
  106.3 4.2 %collective-permute-start.3 = (bf16[64,16,128]{2,1,0:T(8,128)(2,1)S(1)}, bf16[64,16,128]{2,1,0:T(8,128)(2,1)S(1)}, u32[]{:S(2)}, u32[]{:S(2)}) collective-permute-start(bf16[64,16,128]{2,1,0:T(8,128)(2,1)S(1)} %all_to_all.38.own_in), channel_id=1, source_target_pairs={{0,1},{1,0},{2,3},{3,2},{4,5},{5,4},{6,7},{7,6},{8,9},{9,8},{10,11... | collective-permute-start | bytes 786440 | tf_op jit(solution)/shard_map/ppermute | solution.py:407
  121.1 2.4 %collective-permute-start.4 = (f32[64,24,128]{2,1,0:T(8,128)S(1)}, f32[64,24,128]{2,1,0:T(8,128)S(1)}, u32[]{:S(2)}, u32[]{:S(2)}) collective-permute-start(f32[64,24,128]{2,1,0:T(8,128)S(1)} %get-tuple-element.54), channel_id=1, source_target_pairs={{0,1},{1,0},{2,3},{3,2},{4,5},{5,4},{6,7},{7,6},{8,9},{9,8},{10,11... | collective-permute-start | bytes 2359304 | tf_op jit(solution)/shard_map/ppermute | solution.py:400
  159.6 4.7 %collective-permute-start.5 = (f32[64,16,128]{2,1,0:T(8,128)S(1)}, f32[64,16,128]{2,1,0:T(8,128)S(1)}, u32[]{:S(2)}, u32[]{:S(2)}) collective-permute-start(f32[64,16,128]{2,1,0:T(8,128)S(1)} %all_to_all.40.own_in), channel_id=1, source_target_pairs={{0,1},{1,0},{2,3},{3,2},{4,5},{5,4},{6,7},{7,6},{8,9},{9,8},{10,11... | collective-permute-start | bytes 1572872 | tf_op jit(solution)/shard_map/ppermute | solution.py:407
  187.8 2.8 %collective-permute-start.6 = (f32[64,8,128]{2,1,0:T(8,128)S(1)}, f32[64,8,128]{2,1,0:T(8,128)S(1)}, u32[]{:S(2)}, u32[]{:S(2)}) collective-permute-start(f32[64,8,128]{2,1,0:T(8,128)S(1)} %all_to_all.41.same_ref), channel_id=1, source_target_pairs={{0,1},{1,0},{2,3},{3,2},{4,5},{5,4},{6,7},{7,6},{8,9},{9,8},{10,11... | collective-permute-start | bytes 786440 | tf_op jit(solution)/shard_map/ppermute | solution.py:407

commit v3 on v2

--- a/solution.py
+++ b/solution.py
@@ -26,7 +26,6 @@
 ALL = ("grp", "dev_0", "dev_1", "dev_2")
 SWAP = [(0, 1), (1, 0)]
 MIB = 1 << 20
-FIRST_LIMIT = 48
 PASS_LIMIT = 48
 
 f32 = jnp.float32
@@ -55,29 +54,28 @@
     lax.fori_loop(0, BLOCKS, block, 0)
 
 
-def row_tiles(slots, column_ref, owner_ref, tile_ref, table_ref, image_ref):
-    results = []
-    for u, s in enumerate(slots):
-        col = column_ref[s]
-        parts = [
-            jnp.broadcast_to(table_ref[col, pl.ds(part, 1), :], (8, 128)) for part in range(8)
-        ]
-        if u < ON_MXU:
-            left = jnp.concatenate(parts, axis=1).astype(bf16)
-            r = 0.125 * lax.dot_general(
-                left, tile_ref[s], (((1,), (1,)), ((), ())), preferred_element_type=f32
-            )
-        else:
-            sums = []
-            for g in range(TR // 8):
-                rows = tile_ref[s, pl.ds(8 * g, 8), :].astype(f32)
-                total = rows[:, 0:128] * parts[0]
-                for part in range(1, 8):
-                    total = total + rows[:, 128 * part : 128 * part + 128] * parts[part]
-                sums.append(total)
-            r = jnp.sum(jnp.concatenate(sums, axis=0).T.reshape(16, 8, 128), axis=0)
-        results.append(r)
-    for s, r in zip(slots, results):
+def row_tile(u, s, column_ref, tiles, table_ref):
+    col = column_ref[s]
+    parts = [jnp.broadcast_to(table_ref[col, pl.ds(part, 1), :], (8, 128)) for part in range(8)]
+    if u < ON_MXU:
+        left = jnp.concatenate(parts, axis=1).astype(bf16)
+        return 0.125 * lax.dot_general(
+            left, tiles[s], (((1,), (1,)), ((), ())), preferred_element_type=f32
+        )
+    sums = []
+    for g in range(TR // 8):
+        rows = tiles[s, pl.ds(8 * g, 8), slice(None)].astype(f32)
+        total = rows[:, 0:128] * parts[0]
+        for part in range(1, 8):
+            total = total + rows[:, 128 * part : 128 * part + 128] * parts[part]
+        sums.append(total)
+    return jnp.sum(jnp.concatenate(sums, axis=0).T.reshape(16, 8, 128), axis=0)
+
+
+def row_chunk(i, arrive, column_ref, owner_ref, tiles, table_ref, image_ref):
+    arrive(i)
+    results = [row_tile(u, s, column_ref, tiles, table_ref) for u, s in enumerate(chunk_of(i))]
+    for s, r in zip(chunk_of(i), results):
         image_ref[owner_ref[s]] += r
 
 
@@ -87,12 +85,12 @@
     )
 
 
-def column_tiles(slots, lefts, column_ref, tile_ref, sum_ref):
+def column_tiles(slots, lefts, column_ref, tiles, sum_ref):
     sub = lax.broadcasted_iota(jnp.int32, (8, 128), 0)
     results = []
     for s, left in zip(slots, lefts):
         left = jnp.broadcast_to(left, (8, TR)).astype(bf16)
-        out = jnp.dot(left, tile_ref[s], preferred_element_type=f32)
+        out = jnp.dot(left, tiles[s], preferred_element_type=f32)
         r = out[:, 0:128]
         for part in range(1, 8):
             r = jnp.where(sub == part, out[:, 128 * part : 128 * part + 128], r)
@@ -128,20 +126,34 @@
     return [i * CHUNK + u for u in range(CHUNK)]
 
 
-def tile_copies(tiles_hbm, tile_ref, sem):
-    def chunk(i):
-        return pltpu.make_async_copy(
-            tiles_hbm.at[pl.ds(i * CHUNK, CHUNK)], tile_ref.at[pl.ds(i * CHUNK, CHUNK)], sem.at[i]
-        )
-
-    for i in range(CHUNKS):
-        chunk(i).start()
-    return chunk
+def start_tiles(tiles_hbm, kept_ref, tile_ref, sem, first):
+    copies = {}
+    for i in range(0 if first else 1, CHUNKS):
+        to = kept_ref if i == 0 else tile_ref.at[pl.ds((i - 1) * CHUNK, CHUNK)]
+        copies[i] = pltpu.make_async_copy(tiles_hbm.at[pl.ds(i * CHUNK, CHUNK)], to, sem.at[i])
+        copies[i].start()
+
+    def arrive(i):
+        if i in copies:
+            copies[i].wait()
+
+    return arrive
+
+
+class Tiles:
+    def __init__(self, kept_ref, tile_ref):
+        self.refs = kept_ref, tile_ref
+
+    def __getitem__(self, at):
+        s = at[0] if isinstance(at, tuple) else at
+        rest = at[1:] if isinstance(at, tuple) else ()
+        ref, base = (self.refs[0], 0) if s < CHUNK else (self.refs[1], CHUNK)
+        return ref[(s - base, *rest)]
 
 
 def first_kernel(
     count_hbm, column_hbm, place_ref, tiles_hbm, dual_hbm, primal_hbm,
-    owner_ref, image_out, own_ref, other_ref,
+    owner_ref, image_out, own_ref, other_ref, kept_ref,
     count_ref, column_ref, dual_ref, wide_ref, table_ref, tile_ref, sum_ref, image_ref,
     tile_sem, side_sem,
 ):
@@ -158,7 +170,8 @@
     ]
     for copy in sides:
         copy.start()
-    arriving = tile_copies(tiles_hbm, tile_ref, tile_sem)
+    arrive = start_tiles(tiles_hbm, kept_ref, tile_ref, tile_sem, True)
+    tiles = Tiles(kept_ref, tile_ref)
     clear_blocks(sum_ref)
     clear_blocks(image_ref)
     for copy in sides:
@@ -173,22 +186,31 @@
 
     lax.fori_loop(0, COL_BLOCKS, fill, 0, unroll=8)
 
-    def step(i, carry):
-        arriving(i).wait()
-        slots = chunk_of(i)
-        row_tiles(slots, column_ref, owner_ref, tile_ref, table_ref, image_ref)
-        lefts = [wide_ref[pl.ds(owner_ref[s], 1), :] for s in slots]
-        column_tiles(slots, lefts, column_ref, tile_ref, sum_ref)
-        return carry
-
-    lax.fori_loop(0, CHUNKS, step, 0)
+    for i in range(CHUNKS):
+        row_chunk(i, arrive, column_ref, owner_ref, tiles, table_ref, image_ref)
+        lefts = [wide_ref[pl.ds(owner_ref[s], 1), :] for s in chunk_of(i)]
+        column_tiles(chunk_of(i), lefts, column_ref, tiles, sum_ref)
     image_out[...] = image_rows(image_ref)
     put_sums(sum_ref, place_ref[0], own_ref, other_ref, None)
 
 
 def merge_kernel(own_ref, other_ref, out_ref):
+    rows = own_ref.shape[1]
+    if rows > SHARE:
+        rest = own_ref[0, pl.ds(SHARE, 8), :] + other_ref[0, pl.ds(SHARE, 8), :]
+        sub = lax.broadcasted_iota(jnp.int32, (8, 128), 0)
+        parts = jnp.zeros((8, 128), f32)
+        for p in range(3):
+            head = round_bf16(rest)
+            parts = jnp.where(sub == p, head, parts)
+            rest = rest - head
+        parts = parts.astype(bf16)
+
     def add(i, carry):
-        out_ref[i] = own_ref[i] + other_ref[i]
+        data = pl.ds(0, SHARE)
+        out_ref[i, data, :] = (own_ref[i, data, :] + other_ref[i, data, :]).astype(bf16)
+        if rows > SHARE:
+            out_ref[i, pl.ds(SHARE, 8), :] = parts
         return carry
 
     lax.fori_loop(0, CHIPS, add, 0, unroll=8)
@@ -219,21 +241,18 @@
 
 
 def middle_kernel(
-    column_ref, owner_ref, place_ref, tiles_hbm, own_in, other_in, bounds_ref, dual_in,
+    column_ref, owner_ref, place_ref, tiles_hbm, kept_ref, own_in, other_in, bounds_ref, dual_in,
     before_ref, change_in, sigma_in,
     dual_ref, image_out, own_ref, other_ref,
     table_ref, tile_ref, sum_ref, image_ref, tile_sem,
 ):
     core = place_ref[0]
-    arriving = tile_copies(tiles_hbm, tile_ref, tile_sem)
+    arrive = start_tiles(tiles_hbm, kept_ref, tile_ref, tile_sem, False)
+    tiles = Tiles(kept_ref, tile_ref)
     fill_table(own_in, other_in, core, table_ref)
     clear_blocks(sum_ref)
     clear_blocks(image_ref)
     sigma = sigma_in[0:1, :]
-
-    def rows(i):
-        arriving(i).wait()
-        row_tiles(chunk_of(i), column_ref, owner_ref, tile_ref, table_ref, image_ref)
 
     def left(s):
         b = owner_ref[s]
@@ -243,21 +262,15 @@
         row = jnp.maximum(dual_in[at, :] + sigma * move, 0.0)
         return jnp.where(b < BLOCKS, row, 0.0)
 
-    def columns(slots):
-        column_tiles(slots, [left(s) for s in slots], column_ref, tile_ref, sum_ref)
-
-    def early(i, carry):
-        rows(i)
-        return carry
-
-    def step(i, carry):
-        columns(chunk_of(i - 2))
-        rows(i)
-        return carry
-
-    lax.fori_loop(0, 2, early, 0)
-    lax.fori_loop(2, CHUNKS, step, 0)
-    columns(chunk_of(CHUNKS - 2) + chunk_of(CHUNKS - 1))
+    done = 0
+    for i in range(CHUNKS + 1):
+        ready = SLOTS if i == CHUNKS else max(i * CHUNK - 4, 0)
+        slots = range(done, ready)
+        lefts = [left(s) for s in slots]
+        if i < CHUNKS:
+            row_chunk(i, arrive, column_ref, owner_ref, tiles, table_ref, image_ref)
+        column_tiles(slots, lefts, column_ref, tiles, sum_ref)
+        done = ready
     image = image_rows(image_ref)
     dual, scalars = dual_step(bounds_ref, dual_in, before_ref[...], image, change_in, sigma)
     image_out[...] = image
@@ -266,13 +279,14 @@
 
 
 def last_kernel(
-    column_ref, owner_ref, place_ref, target_ref, tiles_hbm, own_in, other_in, bounds_ref,
+    column_ref, owner_ref, place_ref, target_ref, tiles_hbm, kept_ref, own_in, other_in, bounds_ref,
     dual_in, before_ref, change_in, sigma_in,
     primal_ref, send_ref,
     table_ref, tile_ref, image_ref, tile_sem,
 ):
     core = place_ref[0]
-    arriving = tile_copies(tiles_hbm, tile_ref, tile_sem)
+    arrive = start_tiles(tiles_hbm, kept_ref, tile_ref, tile_sem, False)
+    tiles = Tiles(kept_ref, tile_ref)
     fill_table(own_in, other_in, core, table_ref)
     clear_blocks(image_ref)
 
@@ -284,12 +298,8 @@
 
     lax.fori_loop(0, CHIPS, lay, 0, unroll=4)
 
-    def step(i, carry):
-        arriving(i).wait()
-        row_tiles(chunk_of(i), column_ref, owner_ref, tile_ref, table_ref, image_ref)
-        return carry
-
-    lax.fori_loop(0, CHUNKS, step, 0)
+    for i in range(CHUNKS):
+        row_chunk(i, arrive, column_ref, owner_ref, tiles, table_ref, image_ref)
     dual, scalars = dual_step(
         bounds_ref, dual_in, before_ref[...], image_rows(image_ref), change_in, sigma_in[0:1, :]
     )
@@ -330,13 +340,15 @@
     rows = arrived_ref.shape[1]
 
     def add(i, total):
-        return total + arrived_ref[i]
+        return total + arrived_ref[i].astype(f32)
 
     total = lax.fori_loop(0, CHIPS, add, jnp.zeros((rows, 128), f32), unroll=8)
     if first:
         weight = jnp.ones((8, 128), f32)
     else:
-        weight = next_weight(weight_in[...], total[SHARE:, :])
+        scalars = total[SHARE : SHARE + 1, :] + total[SHARE + 1 : SHARE + 2, :]
+        scalars = scalars + total[SHARE + 2 : SHARE + 3, :]
+        weight = next_weight(weight_in[...], jnp.broadcast_to(scalars, (8, 128)))
     tau = STEP / weight[0:1, :]
     new = jnp.clip(primal - tau * (cost - total[:SHARE, :]), 0.0, upper)
     primal_ref[...] = new
@@ -359,7 +371,7 @@
 
     total = lax.fori_loop(0, CHIPS, add, jnp.zeros((8, 128), f32), unroll=8)
     total = jnp.broadcast_to(total[2:3, :], (8, 128))
-    weight_ref[...] = next_weight(weight_in[...], total)
+    weight_ref[0] = next_weight(weight_in[...], total)[0, 0]
     core = place_ref[0]
     first = place_ref[2] * (BLOCKS // 2)
     for chip in range(BLOCKS // 2):
@@ -390,15 +402,70 @@
     )
 
 
-TILE = pltpu.VMEM((SLOTS, TR, CB), bf16)
+TILE = pltpu.VMEM((SLOTS - CHUNK, TR, CB), bf16)
 TABLE = pltpu.VMEM((COL_BLOCKS, 8, 128), f32)
 IMAGE = pltpu.VMEM((BLOCKS + 1, 8, 128), f32)
 DMA = pltpu.SemaphoreType.DMA
 
 
+def first_call(*args):
+    return call(
+        first_kernel,
+        "first_pass",
+        [ANY, ANY, SMEM, ANY, ANY, ANY],
+        (
+            sds((SLOTS,), jnp.int32),
+            sds((BLOCKS, TR)),
+            sds((CHIPS, SHARE, 128)),
+            sds((CHIPS, SHARE, 128)),
+            sds((CHUNK, TR, CB), bf16),
+        ),
+        (SMEM, VMEM, VMEM, VMEM, VMEM),
+        (
+            pltpu.SMEM((BLOCKS,), jnp.int32),
+            pltpu.SMEM((SLOTS,), jnp.int32),
+            pltpu.VMEM((BLOCKS, TR), bf16),
+            pltpu.VMEM((BLOCKS + 8, TR), f32),
+            TABLE,
+            TILE,
+            TABLE,
+            IMAGE,
+            DMA((CHUNKS,)),
+            DMA((4,)),
+        ),
+        limit=PASS_LIMIT,
+    )(*args)
+
+
+def middle_call(*args):
+    return call(
+        middle_kernel,
+        "middle_pass",
+        [SMEM] * 3 + [ANY] + [VMEM] * 8,
+        (sds((BLOCKS, TR)), sds((BLOCKS, TR))) + (sds((CHIPS, SHARE + 8, 128)),) * 2,
+        (VMEM,) * 4,
+        (TABLE, TILE, TABLE, IMAGE, DMA((CHUNKS,))),
+        limit=PASS_LIMIT,
+    )(*args)
+
+
+def last_call(*args):
+    return call(
+        last_kernel,
+        "last_pass",
+        [SMEM] * 4 + [ANY] + [VMEM] * 8,
+        (sds((ROWS_P, 128)), sds((CHIPS, 8, 128))),
+        (VMEM,) * 2,
+        (TABLE, TILE, IMAGE, DMA((CHUNKS,))),
+        limit=PASS_LIMIT,
+    )(*args)
+
+
 def summed(own, other):
     crossed = lax.ppermute(other, CORE, SWAP)
-    merged = call(merge_kernel, "merge", [VMEM] * 2, sds(own.shape), VMEM, limit=4)(own, crossed)
+    merged = call(merge_kernel, "merge", [VMEM] * 2, sds(own.shape, bf16), VMEM, limit=4)(
+        own, crossed
+    )
     return lax.all_to_all(merged, CHIP, 0, 0, tiled=True)
 
 
@@ -429,31 +496,7 @@
     part = sds((SHARE, 128))
     tiny = sds((8, 128))
 
-    owners, before, own, other = call(
-        first_kernel,
-        "first_pass",
-        [ANY, ANY, SMEM, ANY, ANY, ANY],
-        (
-            sds((SLOTS,), jnp.int32),
-            sds((BLOCKS, TR)),
-            sds((CHIPS, SHARE, 128)),
-            sds((CHIPS, SHARE, 128)),
-        ),
-        (SMEM, VMEM, VMEM, VMEM),
-        (
-            pltpu.SMEM((BLOCKS,), jnp.int32),
-            pltpu.SMEM((SLOTS,), jnp.int32),
-            pltpu.VMEM((BLOCKS, TR), bf16),
-            pltpu.VMEM((BLOCKS + 8, TR), f32),
-            TABLE,
-            TILE,
-            TABLE,
-            IMAGE,
-            DMA((CHUNKS,)),
-            DMA((4,)),
-        ),
-        limit=FIRST_LIMIT,
-    )(
+    owners, before, own, other, kept = first_call(
         block_counts, tile_column, place, matrix_tiles, dual_bf,
         primal_start.reshape(COL_BLOCKS, 8, 128),
     )
@@ -486,29 +529,12 @@
         near, far = gathered(send)
         if last:
             break
-        dual, before, own, other = call(
-            middle_kernel,
-            "middle_pass",
-            [SMEM] * 3 + [ANY] + [VMEM] * 7,
-            (sds((BLOCKS, TR)), sds((BLOCKS, TR)))
-            + (sds((CHIPS, SHARE + 8, 128)),) * 2,
-            (VMEM,) * 4,
-            (TABLE, TILE, TABLE, IMAGE, DMA((CHUNKS,))),
-            limit=PASS_LIMIT,
-        )(
-            tile_column, owners, place, matrix_tiles, near, far, bounds, dual, before, change,
+        dual, before, own, other = middle_call(
+            tile_column, owners, place, matrix_tiles, kept, near, far, bounds, dual, before, change,
             sigma,
         )
-    primal_final, send = call(
-        last_kernel,
-        "last_pass",
-        [SMEM] * 4 + [ANY] + [VMEM] * 7,
-        (sds(wide), sds((CHIPS, 8, 128))),
-        (VMEM,) * 2,
-        (TABLE, TILE, IMAGE, DMA((CHUNKS,))),
-        limit=PASS_LIMIT,
-    )(
-        tile_column, owners, place, destination, matrix_tiles, near, far, bounds, dual, before, change,
+    primal_final, send = last_call(
+        tile_column, owners, place, destination, matrix_tiles, kept, near, far, bounds, dual, before, change,
         sigma,
     )
     same, cross = gathered(send)
@@ -516,11 +542,11 @@
         finish_kernel,
         "finish",
         [SMEM, VMEM, VMEM, VMEM],
-        (sds((BLOCKS, TR)), tiny),
-        (VMEM, VMEM),
+        (sds((BLOCKS, TR)), sds((1,))),
+        (VMEM, SMEM),
         limit=4,
     )(place, same, cross, weight)
-    return (primal_final.reshape(-1), dual_final.reshape(-1), weight[0, 0:1])
+    return (primal_final.reshape(-1), dual_final.reshape(-1), weight)
 
 
 def solution(mesh):

time: 193 us -> 178 us (0.922)
  blocking collectives: 120 us -> 109 us
  Pallas kernels: 44.3 us -> 40.3 us
    all_to_all x3, blocking collectives: 61.7 us -> 51.5 us  [summed(): return lax.all_to_all(merged, CHIP, 0, 0, tiled=True)]
    pallas_call x7, Pallas kernels: 40.9 us -> 36.8 us  [the longest x2 17.8 us: middle_call(): call(middle_kernel, 'middle_pass', [SMEM] * 3 + [ANY] + [VMEM] * 8, (sds(...]
where the time goes in v3:
time: 178 us
  blocking collectives  109 us (61%)
  Pallas kernels  40.3 us (23%)
  starting transfers between devices  13.7 us (8%)
  waiting for transfers between devices  10.4 us (6%)
  local copies, waits for them, and re-layouts  3.25 us (2%)
    all_to_all x4, blocking collectives, gathered(): own = lax.all_to_all(send, CHIP, 0, 0, tiled=True)  57.5 us
    all_to_all x3, blocking collectives, summed(): return lax.all_to_all(merged, CHIP, 0, 0, tiled=True)  51.5 us
    pallas_call x2, Pallas kernels, middle_call(): call(middle_kernel, 'middle_pass', [SMEM] * 3 + [ANY] + [VMEM] * 8, (sds(...  17.8 us
    ppermute x4, starting transfers between devices, gathered(): return (own, lax.ppermute(own, CORE, SWAP))  11.1 us
    pallas_call x1, Pallas kernels, first_call(): call(first_kernel, 'first_pass', [ANY, ANY, SMEM, ANY, ANY, ANY], (sds((S...  9.96 us
    pallas_call x1, Pallas kernels, last_call(): call(last_kernel, 'last_pass', [SMEM] * 4 + [ANY] + [VMEM] * 8, (sds((ROW...  8.74 us
    ppermute x3, waiting for transfers between devices, summed(): crossed = lax.ppermute(other, CORE, SWAP)  5.36 us
    ppermute x4, waiting for transfers between devices, gathered(): return (own, lax.ppermute(own, CORE, SWAP))  5.01 us
  transfers between devices with their start and end apart: 7, of which 7 were waited for; matrix products, arithmetic and copies ran while one was open for 0% of the time, Pallas kernels for 0%

profile of v3, /device:TPU:1, one launch (start us, length us, event | category | flops | bytes accessed | tf_op | source)
XLA Modules:
  0.0 177.6 jit_solution(17893381468708995157)
XLA Ops:
  0.6 0.0 copy-start.7
  0.6 0.1 pad_add_fusion.place_ref.refs_1_
  0.7 0.0 copy-start
  0.7 1.2 copy-done
  2.0 0.0 copy-start.3
  2.0 0.7 copy-done.3
  2.7 0.0 copy-start.4
  2.7 0.7 copy-done.4
  3.3 0.0 copy-start.6
  3.3 0.7 copy-done.6
  4.0 0.0 copy-start.1
  4.0 0.0 copy-start.2
  4.0 10.0 %first_pass.1 = (s32[80]{0:T(128)S(1)}, f32[32,128]{1,0:T(8,128)S(1)}, f32[64,16,128]{2,1,0:T(8,128)S(1)}, f32[64,16,128]{2,1,0:T(8,128)S(1)}, bf16[8,128,1024]{2,1,0:T(8,128)(2,1)S(1)}) custom-call(s32[32]{0:T(128)S(1)} %copy-done.6, s32[80]{0:T(128)S(1)} %copy-done.4, s32[3]{0:T(128)S(1)} %pad_add_fusion.place_ref.refs_1_, ...), custom_call_target="tpu_custom_call" | custom-call | tf_op jit(solution)/shard_map/first_pass/pallas_call | solution.py:412
  13.9 1.7 collective-permute-start
  15.6 1.5 collective-permute-done.other_ref
  17.1 0.1 merge.3
  17.2 20.8 %all_to_all.35.refs_0_ = bf16[64,16,128]{2,1,0:T(8,128)(2,1)S(1)} all-to-all(bf16[64,16,128]{2,1,0:T(8,128)(2,1)S(1)} %merge.3), channel_id=1, replica_groups=mesh['grp'=4,'dev_0'=4,'dev_1'=4,'dev_2'=2] {'grp','dev_0','dev_1'}, dimensions={0} | all-to-all | bytes 524288 | tf_op jit(solution)/shard_map/all_to_all | solution.py:469
  38.0 0.0 copy-done.1
  38.0 0.0 copy-done.2
  38.0 0.8 update.3
  38.8 13.8 %all_to_all.36.own_in = bf16[64,16,128]{2,1,0:T(8,128)(2,1)S(1)} all-to-all(bf16[64,16,128]{2,1,0:T(8,128)(2,1)S(1)} %get-tuple-element.40), channel_id=1, replica_groups=mesh['grp'=4,'dev_0'=4,'dev_1'=4,'dev_2'=2] {'grp','dev_0','dev_1'}, dimensions={0} | all-to-all | bytes 524288 | tf_op jit(solution)/shard_map/all_to_all | solution.py:473
  52.6 3.1 %collective-permute-start.1 = (bf16[64,16,128]{2,1,0:T(8,128)(2,1)S(1)}, bf16[64,16,128]{2,1,0:T(8,128)(2,1)S(1)}, u32[]{:S(2)}, u32[]{:S(2)}) collective-permute-start(bf16[64,16,128]{2,1,0:T(8,128)(2,1)S(1)} %all_to_all.36.own_in), channel_id=1, source_target_pairs={{0,1},{1,0},{2,3},{3,2},{4,5},{5,4},{6,7},{7,6},{8,9},{9,8},{10,11... | collective-permute-start | bytes 786440 | tf_op jit(solution)/shard_map/ppermute | solution.py:474
  55.7 0.0 copy-done.7
  55.7 1.2 collective-permute-done.1.other_in
  56.8 8.9 %middle_pass.2 = (f32[32,128]{1,0:T(8,128)S(1)}, f32[32,128]{1,0:T(8,128)S(1)}, f32[64,24,128]{2,1,0:T(8,128)S(1)}, f32[64,24,128]{2,1,0:T(8,128)S(1)}) custom-call(s32[80]{0:T(128)S(1)} %copy-done.4, s32[80]{0:T(128)S(1)} %get-tuple-element.36.owner_ref, s32[3]{0:T(128)S(1)} %pad_add_fusion.place_ref.refs_1_, bf16[80,128,1024]{2,1,0:T(8,128)(2,1)} %tiles_hbm.7, ...), custom_call_target="tpu_custom_call" | custom-call | tf_op jit(solution)/shard_map/middle_pass/pallas_call | solution.py:441
  65.8 0.0 copy-start.5
  65.8 0.5 collective-permute-start.2
  66.3 1.9 %collective-permute-done.2.other_ref = f32[64,24,128]{2,1,0:T(8,128)S(1)} collective-permute-done((f32[64,24,128]{2,1,0:T(8,128)S(1)}, f32[64,24,128]{2,1,0:T(8,128)S(1)}, u32[]{:S(2)}, u32[]{:S(2)}) %collective-permute-start.2) | collective-permute-done | bytes 786464 | tf_op jit(solution)/shard_map/ppermute | solution.py:465
  68.2 0.1 merge.4
  68.3 15.3 %all_to_all.37.refs_0_ = bf16[64,24,128]{2,1,0:T(8,128)(2,1)S(1)} all-to-all(bf16[64,24,128]{2,1,0:T(8,128)(2,1)S(1)} %merge.4), channel_id=1, replica_groups=mesh['grp'=4,'dev_0'=4,'dev_1'=4,'dev_2'=2] {'grp','dev_0','dev_1'}, dimensions={0} | all-to-all | bytes 786432 | tf_op jit(solution)/shard_map/all_to_all | solution.py:469
  83.6 0.4 update.4
  84.0 14.0 %all_to_all.38.own_in = bf16[64,16,128]{2,1,0:T(8,128)(2,1)S(1)} all-to-all(bf16[64,16,128]{2,1,0:T(8,128)(2,1)S(1)} %get-tuple-element.50), channel_id=1, replica_groups=mesh['grp'=4,'dev_0'=4,'dev_1'=4,'dev_2'=2] {'grp','dev_0','dev_1'}, dimensions={0} | all-to-all | bytes 524288 | tf_op jit(solution)/shard_map/all_to_all | solution.py:473
  98.0 3.2 %collective-permute-start.3 = (bf16[64,16,128]{2,1,0:T(8,128)(2,1)S(1)}, bf16[64,16,128]{2,1,0:T(8,128)(2,1)S(1)}, u32[]{:S(2)}, u32[]{:S(2)}) collective-permute-start(bf16[64,16,128]{2,1,0:T(8,128)(2,1)S(1)} %all_to_all.38.own_in), channel_id=1, source_target_pairs={{0,1},{1,0},{2,3},{3,2},{4,5},{5,4},{6,7},{7,6},{8,9},{9,8},{10,11... | collective-permute-start | bytes 786440 | tf_op jit(solution)/shard_map/ppermute | solution.py:474
  101.2 1.2 collective-permute-done.3.other_in
  102.3 8.9 %middle_pass.3 = (f32[32,128]{1,0:T(8,128)S(1)}, f32[32,128]{1,0:T(8,128)S(1)}, f32[64,24,128]{2,1,0:T(8,128)S(1)}, f32[64,24,128]{2,1,0:T(8,128)S(1)}) custom-call(s32[80]{0:T(128)S(1)} %copy-done.4, s32[80]{0:T(128)S(1)} %get-tuple-element.36.owner_ref, s32[3]{0:T(128)S(1)} %pad_add_fusion.place_ref.refs_1_, bf16[80,128,1024]{2,1,0:T(8,128)(2,1)} %tiles_hbm.7, ...), custom_call_target="tpu_custom_call" | custom-call | tf_op jit(solution)/shard_map/middle_pass/pallas_call | solution.py:441
  111.3 0.5 collective-permute-start.4
  111.7 1.9 %collective-permute-done.4.other_ref = f32[64,24,128]{2,1,0:T(8,128)S(1)} collective-permute-done((f32[64,24,128]{2,1,0:T(8,128)S(1)}, f32[64,24,128]{2,1,0:T(8,128)S(1)}, u32[]{:S(2)}, u32[]{:S(2)}) %collective-permute-start.4) | collective-permute-done | bytes 786464 | tf_op jit(solution)/shard_map/ppermute | solution.py:465
  113.6 0.1 merge.5
  113.8 15.3 %all_to_all.39.refs_0_ = bf16[64,24,128]{2,1,0:T(8,128)(2,1)S(1)} all-to-all(bf16[64,24,128]{2,1,0:T(8,128)(2,1)S(1)} %merge.5), channel_id=1, replica_groups=mesh['grp'=4,'dev_0'=4,'dev_1'=4,'dev_2'=2] {'grp','dev_0','dev_1'}, dimensions={0} | all-to-all | bytes 786432 | tf_op jit(solution)/shard_map/all_to_all | solution.py:469
  129.1 1.0 update.5
  130.1 15.6 %all_to_all.40.own_in = f32[64,16,128]{2,1,0:T(8,128)S(1)} all-to-all(f32[64,16,128]{2,1,0:T(8,128)S(1)} %get-tuple-element.59), channel_id=1, replica_groups=mesh['grp'=4,'dev_0'=4,'dev_1'=4,'dev_2'=2] {'grp','dev_0','dev_1'}, dimensions={0} | all-to-all | bytes 1048576 | tf_op jit(solution)/shard_map/all_to_all | solution.py:473
  145.6 3.2 %collective-permute-start.5 = (f32[64,16,128]{2,1,0:T(8,128)S(1)}, f32[64,16,128]{2,1,0:T(8,128)S(1)}, u32[]{:S(2)}, u32[]{:S(2)}) collective-permute-start(f32[64,16,128]{2,1,0:T(8,128)S(1)} %all_to_all.40.own_in), channel_id=1, source_target_pairs={{0,1},{1,0},{2,3},{3,2},{4,5},{5,4},{6,7},{7,6},{8,9},{9,8},{10,11... | collective-permute-start | bytes 1572872 | tf_op jit(solution)/shard_map/ppermute | solution.py:474
  148.8 1.5 collective-permute-done.5.other_in
  150.4 0.0 copy-done.5
  150.4 8.7 %last_pass.1 = (f32[2048,128]{1,0:T(8,128)}, f32[64,8,128]{2,1,0:T(8,128)S(1)}) custom-call(s32[80]{0:T(128)S(1)} %copy-done.4, s32[80]{0:T(128)S(1)} %get-tuple-element.36.owner_ref, s32[3]{0:T(128)S(1)} %pad_add_fusion.place_ref.refs_1_, s32[32]{0:T(128)S(1)} %copy-done.5, bf16[80,128,1024]{2,1,0:T(8,128)(2,1)} %tiles_hbm.7, ...), custom_call_target="tpu_custom_call" | custom-call | tf_op jit(solution)/shard_map/last_pass/pallas_call | solution.py:453
  159.1 14.2 %all_to_all.41.same_ref = f32[64,8,128]{2,1,0:T(8,128)S(1)} all-to-all(f32[64,8,128]{2,1,0:T(8,128)S(1)} %get-tuple-element.65), channel_id=1, replica_groups=mesh['grp'=4,'dev_0'=4,'dev_1'=4,'dev_2'=2] {'grp','dev_0','dev_1'}, dimensions={0} | all-to-all | bytes 524288 | tf_op jit(solution)/shard_map/all_to_all | solution.py:473
  173.4 1.6 collective-permute-start.6
  175.0 1.2 collective-permute-done.6.cross_ref
  176.1 1.3 finish.1
  (2 shorter events, 0.0 us)
Async XLA Ops:
  0.6 55.1 %copy-start.7 = (bf16[4096]{0:T(1024)(128)(2,1)S(1)}, bf16[4096]{0:T(1024)(128)(2,1)}, u32[]{:S(2)}) copy-start(bf16[4096]{0:T(1024)(128)(2,1)} %param.13) | copy-start | bytes 24580
  0.7 1.2 copy-start
  2.0 0.7 copy-start.3
  2.7 0.7 copy-start.4
  3.3 0.7 copy-start.6
  4.0 34.0 %copy-start.1 = (f32[262144]{0:T(1024)S(1)}, f32[262144]{0:T(1024)}, u32[]{:S(2)}) copy-start(f32[262144]{0:T(1024)} %param.16) | copy-start | bytes 3145732
  4.0 34.0 %copy-start.2 = (f32[262144]{0:T(1024)S(1)}, f32[262144]{0:T(1024)}, u32[]{:S(2)}) copy-start(f32[262144]{0:T(1024)} %param.17) | copy-start | bytes 3145732
  13.9 3.2 %collective-permute-start = (f32[64,16,128]{2,1,0:T(8,128)S(1)}, f32[64,16,128]{2,1,0:T(8,128)S(1)}, u32[]{:S(2)}, u32[]{:S(2)}) collective-permute-start(f32[64,16,128]{2,1,0:T(8,128)S(1)} %get-tuple-element.39), channel_id=1, source_target_pairs={{0,1},{1,0},{2,3},{3,2},{4,5},{5,4},{6,7},{7,6},{8,9},{9,8},{10,11... | collective-permute-start | bytes 1572872 | tf_op jit(solution)/shard_map/ppermute | solution.py:465
  52.6 4.2 %collective-permute-start.1 = (bf16[64,16,128]{2,1,0:T(8,128)(2,1)S(1)}, bf16[64,16,128]{2,1,0:T(8,128)(2,1)S(1)}, u32[]{:S(2)}, u32[]{:S(2)}) collective-permute-start(bf16[64,16,128]{2,1,0:T(8,128)(2,1)S(1)} %all_to_all.36.own_in), channel_id=1, source_target_pairs={{0,1},{1,0},{2,3},{3,2},{4,5},{5,4},{6,7},{7,6},{8,9},{9,8},{10,11... | collective-permute-start | bytes 786440 | tf_op jit(solution)/shard_map/ppermute | solution.py:474
  65.8 84.6 %copy-start.5 = (s32[32]{0:T(128)S(1)}, s32[32]{0:T(128)}, u32[]{:S(2)}) copy-start(s32[32]{0:T(128)} %target_ref.1) | copy-start | bytes 388
  65.8 2.4 %collective-permute-start.2 = (f32[64,24,128]{2,1,0:T(8,128)S(1)}, f32[64,24,128]{2,1,0:T(8,128)S(1)}, u32[]{:S(2)}, u32[]{:S(2)}) collective-permute-start(f32[64,24,128]{2,1,0:T(8,128)S(1)} %get-tuple-element.45), channel_id=1, source_target_pairs={{0,1},{1,0},{2,3},{3,2},{4,5},{5,4},{6,7},{7,6},{8,9},{9,8},{10,11... | collective-permute-start | bytes 2359304 | tf_op jit(solution)/shard_map/ppermute | solution.py:465
  98.0 4.4 %collective-permute-start.3 = (bf16[64,16,128]{2,1,0:T(8,128)(2,1)S(1)}, bf16[64,16,128]{2,1,0:T(8,128)(2,1)S(1)}, u32[]{:S(2)}, u32[]{:S(2)}) collective-permute-start(bf16[64,16,128]{2,1,0:T(8,128)(2,1)S(1)} %all_to_all.38.own_in), channel_id=1, source_target_pairs={{0,1},{1,0},{2,3},{3,2},{4,5},{5,4},{6,7},{7,6},{8,9},{9,8},{10,11... | collective-permute-start | bytes 786440 | tf_op jit(solution)/shard_map/ppermute | solution.py:474
  111.3 2.4 %collective-permute-start.4 = (f32[64,24,128]{2,1,0:T(8,128)S(1)}, f32[64,24,128]{2,1,0:T(8,128)S(1)}, u32[]{:S(2)}, u32[]{:S(2)}) collective-permute-start(f32[64,24,128]{2,1,0:T(8,128)S(1)} %get-tuple-element.56), channel_id=1, source_target_pairs={{0,1},{1,0},{2,3},{3,2},{4,5},{5,4},{6,7},{7,6},{8,9},{9,8},{10,11... | collective-permute-start | bytes 2359304 | tf_op jit(solution)/shard_map/ppermute | solution.py:465
  145.6 4.7 %collective-permute-start.5 = (f32[64,16,128]{2,1,0:T(8,128)S(1)}, f32[64,16,128]{2,1,0:T(8,128)S(1)}, u32[]{:S(2)}, u32[]{:S(2)}) collective-permute-start(f32[64,16,128]{2,1,0:T(8,128)S(1)} %all_to_all.40.own_in), channel_id=1, source_target_pairs={{0,1},{1,0},{2,3},{3,2},{4,5},{5,4},{6,7},{7,6},{8,9},{9,8},{10,11... | collective-permute-start | bytes 1572872 | tf_op jit(solution)/shard_map/ppermute | solution.py:474
  173.4 2.8 %collective-permute-start.6 = (f32[64,8,128]{2,1,0:T(8,128)S(1)}, f32[64,8,128]{2,1,0:T(8,128)S(1)}, u32[]{:S(2)}, u32[]{:S(2)}) collective-permute-start(f32[64,8,128]{2,1,0:T(8,128)S(1)} %all_to_all.41.same_ref), channel_id=1, source_target_pairs={{0,1},{1,0},{2,3},{3,2},{4,5},{5,4},{6,7},{7,6},{8,9},{9,8},{10,11... | collective-permute-start | bytes 786440 | tf_op jit(solution)/shard_map/ppermute | solution.py:474

commit v4 on v3

--- a/solution.py
+++ b/solution.py
@@ -10,6 +10,12 @@
 STEP = 0.3
 TINY = 1e-06
 BLOCKS = 32
+MAXC = 4
+AT_OWNER = 0
+AT_COLUMN = 96
+AT_TARGET = AT_COLUMN + 80
+AT_PLACE = AT_TARGET + 32
+INDEX = 256
 SLOTS = 80
 TR = 128
 CB = 1024
@@ -17,9 +23,10 @@
 ROWS_P = 2048
 CHIPS = 64
 SHARE = 16
-CHUNK = 8
-CHUNKS = SLOTS // CHUNK
-ON_MXU = 2
+KEPT = 12
+STOPS = (8, 12, 20, 28, 36, 44, 52, 60, 68, 76, 80)
+STARTS = (0,) + STOPS[:-1]
+CHUNKS = len(STOPS)
 
 CHIP = ("grp", "dev_0", "dev_1")
 CORE = "dev_2"
@@ -36,32 +43,37 @@
     return x.astype(bf16).astype(f32)
 
 
-def find_owners(count_ref, owner_ref):
-    def clear(s, carry):
-        owner_ref[s] = BLOCKS
-        return carry
-
-    def block(b, start):
-        stop = start + count_ref[b]
-
-        def slot(s, carry):
-            owner_ref[s] = b
-            return carry
-
-        return lax.fori_loop(start, stop, slot, start) * 0 + stop
-
-    lax.fori_loop(0, SLOTS, clear, 0)
-    lax.fori_loop(0, BLOCKS, block, 0)
-
-
-def row_tile(u, s, column_ref, tiles, table_ref):
+class View:
+    def __init__(self, ref, base):
+        self.ref, self.base = ref, base
+
+    def __getitem__(self, i):
+        return self.ref[self.base + i]
+
+
+def views(index_ref):
+    return tuple(View(index_ref, base) for base in (AT_COLUMN, AT_OWNER, AT_PLACE, AT_TARGET))
+
+
+def fill_index(raw_ref, index_ref):
+    for s in range(SLOTS):
+        index_ref[AT_OWNER + s] = BLOCKS
+    at = jnp.int32(AT_OWNER)
+    for b in range(BLOCKS):
+        for k in range(MAXC):
+            index_ref[at + k] = b
+        at = at + raw_ref[b]
+    for k in range(MAXC):
+        index_ref[at + k] = BLOCKS
+    for i in range(SLOTS + BLOCKS + 3):
+        index_ref[AT_COLUMN + i] = raw_ref[BLOCKS + i]
+
+
+def row_tile(s, column_ref, tiles, table_ref, rough):
     col = column_ref[s]
     parts = [jnp.broadcast_to(table_ref[col, pl.ds(part, 1), :], (8, 128)) for part in range(8)]
-    if u < ON_MXU:
-        left = jnp.concatenate(parts, axis=1).astype(bf16)
-        return 0.125 * lax.dot_general(
-            left, tiles[s], (((1,), (1,)), ((), ())), preferred_element_type=f32
-        )
+    if rough:
+        parts = [round_bf16(p) for p in parts]
     sums = []
     for g in range(TR // 8):
         rows = tiles[s, pl.ds(8 * g, 8), slice(None)].astype(f32)
@@ -72,9 +84,9 @@
     return jnp.sum(jnp.concatenate(sums, axis=0).T.reshape(16, 8, 128), axis=0)
 
 
-def row_chunk(i, arrive, column_ref, owner_ref, tiles, table_ref, image_ref):
+def row_chunk(i, arrive, column_ref, owner_ref, tiles, table_ref, image_ref, rough=False):
     arrive(i)
-    results = [row_tile(u, s, column_ref, tiles, table_ref) for u, s in enumerate(chunk_of(i))]
+    results = [row_tile(s, column_ref, tiles, table_ref, rough) for s in chunk_of(i)]
     for s, r in zip(chunk_of(i), results):
         image_ref[owner_ref[s]] += r
 
@@ -123,14 +135,19 @@
 
 
 def chunk_of(i):
-    return [i * CHUNK + u for u in range(CHUNK)]
+    return range(STARTS[i], STOPS[i])
 
 
 def start_tiles(tiles_hbm, kept_ref, tile_ref, sem, first):
     copies = {}
-    for i in range(0 if first else 1, CHUNKS):
-        to = kept_ref if i == 0 else tile_ref.at[pl.ds((i - 1) * CHUNK, CHUNK)]
-        copies[i] = pltpu.make_async_copy(tiles_hbm.at[pl.ds(i * CHUNK, CHUNK)], to, sem.at[i])
+    for i in range(CHUNKS):
+        start, size = STARTS[i], STOPS[i] - STARTS[i]
+        if start < KEPT and not first:
+            continue
+        to, base = (kept_ref, 0) if start < KEPT else (tile_ref, KEPT)
+        copies[i] = pltpu.make_async_copy(
+            tiles_hbm.at[pl.ds(start, size)], to.at[pl.ds(start - base, size)], sem.at[i]
+        )
         copies[i].start()
 
     def arrive(i):
@@ -147,22 +164,20 @@
     def __getitem__(self, at):
         s = at[0] if isinstance(at, tuple) else at
         rest = at[1:] if isinstance(at, tuple) else ()
-        ref, base = (self.refs[0], 0) if s < CHUNK else (self.refs[1], CHUNK)
+        ref, base = (self.refs[0], 0) if s < KEPT else (self.refs[1], KEPT)
         return ref[(s - base, *rest)]
 
 
 def first_kernel(
-    count_hbm, column_hbm, place_ref, tiles_hbm, dual_hbm, primal_hbm,
-    owner_ref, image_out, own_ref, other_ref, kept_ref,
-    count_ref, column_ref, dual_ref, wide_ref, table_ref, tile_ref, sum_ref, image_ref,
+    raw_ref, tiles_hbm, dual_hbm, primal_hbm,
+    index_ref, image_out, own_ref, other_ref, kept_ref,
+    dual_ref, wide_ref, table_ref, tile_ref, sum_ref, image_ref,
     tile_sem, side_sem,
 ):
     sides = [
         pltpu.make_async_copy(src, dst, side_sem.at[i])
         for i, (src, dst) in enumerate(
             (
-                (count_hbm, count_ref),
-                (column_hbm, column_ref),
                 (dual_hbm, dual_ref),
                 (primal_hbm, table_ref),
             )
@@ -174,20 +189,15 @@
     tiles = Tiles(kept_ref, tile_ref)
     clear_blocks(sum_ref)
     clear_blocks(image_ref)
+    fill_index(raw_ref, index_ref)
+    column_ref, owner_ref, place_ref, _ = views(index_ref)
     for copy in sides:
         copy.wait()
-    find_owners(count_ref, owner_ref)
     wide_ref[pl.ds(0, BLOCKS), :] = dual_ref[...].astype(f32)
     wide_ref[pl.ds(BLOCKS, 8), :] = jnp.zeros((8, TR), f32)
 
-    def fill(i, carry):
-        table_ref[i] = round_bf16(table_ref[i])
-        return carry
-
-    lax.fori_loop(0, COL_BLOCKS, fill, 0, unroll=8)
-
     for i in range(CHUNKS):
-        row_chunk(i, arrive, column_ref, owner_ref, tiles, table_ref, image_ref)
+        row_chunk(i, arrive, column_ref, owner_ref, tiles, table_ref, image_ref, True)
         lefts = [wide_ref[pl.ds(owner_ref[s], 1), :] for s in chunk_of(i)]
         column_tiles(chunk_of(i), lefts, column_ref, tiles, sum_ref)
     image_out[...] = image_rows(image_ref)
@@ -241,11 +251,12 @@
 
 
 def middle_kernel(
-    column_ref, owner_ref, place_ref, tiles_hbm, kept_ref, own_in, other_in, bounds_ref, dual_in,
+    index_ref, tiles_hbm, kept_ref, own_in, other_in, bounds_ref, dual_in,
     before_ref, change_in, sigma_in,
     dual_ref, image_out, own_ref, other_ref,
     table_ref, tile_ref, sum_ref, image_ref, tile_sem,
 ):
+    column_ref, owner_ref, place_ref, target_ref = views(index_ref)
     core = place_ref[0]
     arrive = start_tiles(tiles_hbm, kept_ref, tile_ref, tile_sem, False)
     tiles = Tiles(kept_ref, tile_ref)
@@ -263,41 +274,42 @@
         return jnp.where(b < BLOCKS, row, 0.0)
 
     done = 0
-    for i in range(CHUNKS + 1):
-        ready = SLOTS if i == CHUNKS else max(i * CHUNK - 4, 0)
-        slots = range(done, ready)
+    for i in range(CHUNKS):
+        slots = range(done, max(STARTS[i] - 3, 0))
         lefts = [left(s) for s in slots]
-        if i < CHUNKS:
-            row_chunk(i, arrive, column_ref, owner_ref, tiles, table_ref, image_ref)
+        row_chunk(i, arrive, column_ref, owner_ref, tiles, table_ref, image_ref)
         column_tiles(slots, lefts, column_ref, tiles, sum_ref)
-        done = ready
+        done = slots.stop
+    slots = range(done, SLOTS)
+    lefts = [left(s) for s in slots]
     image = image_rows(image_ref)
     dual, scalars = dual_step(bounds_ref, dual_in, before_ref[...], image, change_in, sigma)
     image_out[...] = image
     dual_ref[...] = dual
+    column_tiles(slots, lefts, column_ref, tiles, sum_ref)
     put_sums(sum_ref, core, own_ref, other_ref, scalars)
 
 
 def last_kernel(
-    column_ref, owner_ref, place_ref, target_ref, tiles_hbm, kept_ref, own_in, other_in, bounds_ref,
+    index_ref, tiles_hbm, kept_ref, own_in, other_in, bounds_ref,
     dual_in, before_ref, change_in, sigma_in,
-    primal_ref, send_ref,
-    table_ref, tile_ref, image_ref, tile_sem,
+    primal_hbm, send_ref,
+    table_ref, tile_ref, image_ref, tile_sem, out_sem,
 ):
+    column_ref, owner_ref, place_ref, target_ref = views(index_ref)
     core = place_ref[0]
     arrive = start_tiles(tiles_hbm, kept_ref, tile_ref, tile_sem, False)
     tiles = Tiles(kept_ref, tile_ref)
     fill_table(own_in, other_in, core, table_ref)
     clear_blocks(image_ref)
 
-    def lay(i, carry):
-        for ref, side in ((own_in, core), (other_in, 1 - core)):
-            at = pl.multiple_of((side * CHIPS + i) * SHARE, SHARE)
-            primal_ref[pl.ds(at, SHARE), :] = ref[i]
-        return carry
-
-    lax.fori_loop(0, CHIPS, lay, 0, unroll=4)
-
+    half = CHIPS
+    outs = [
+        pltpu.make_async_copy(ref, primal_hbm.at[pl.ds(side * half, half)], out_sem.at[i])
+        for i, (ref, side) in enumerate(((own_in, core), (other_in, 1 - core)))
+    ]
+    for copy in outs:
+        copy.start()
     for i in range(CHUNKS):
         row_chunk(i, arrive, column_ref, owner_ref, tiles, table_ref, image_ref)
     dual, scalars = dual_step(
@@ -315,6 +327,8 @@
         send_ref[first + jnp.right_shift(to, 1), pl.ds(jnp.bitwise_and(to, 1), 1), :] = dual[
             b : b + 1, :
         ]
+    for copy in outs:
+        copy.wait()
 
 
 def next_weight(weight, scalars):
@@ -327,15 +341,17 @@
 
 def update_kernel(first, *refs):
     if first:
-        (arrived_ref, place_ref, primal_full, cost_full, upper_full,
+        (arrived_ref, index_ref, primal_full, cost_full, upper_full,
          primal_ref, send_ref, change_ref, weight_ref, sigma_ref, cost_ref, upper_ref) = refs
+        place_ref = views(index_ref)[2]
         at = pl.ds(pl.multiple_of(place_ref[1] * SHARE, SHARE), SHARE)
         primal, cost, upper = primal_full[at, :], cost_full[at, :], upper_full[at, :]
         cost_ref[...] = cost
         upper_ref[...] = upper
     else:
         (arrived_ref, primal_in, cost_in, upper_in, weight_in,
-         primal_ref, send_ref, change_ref, weight_ref, sigma_ref) = refs
+         send_ref, change_ref, weight_ref, sigma_ref, *primal_ref) = refs
+        primal_ref = primal_ref[0] if primal_ref else None
         primal, cost, upper = primal_in[...], cost_in[...], upper_in[...]
     rows = arrived_ref.shape[1]
 
@@ -351,7 +367,8 @@
         weight = next_weight(weight_in[...], jnp.broadcast_to(scalars, (8, 128)))
     tau = STEP / weight[0:1, :]
     new = jnp.clip(primal - tau * (cost - total[:SHARE, :]), 0.0, upper)
-    primal_ref[...] = new
+    if primal_ref is not None:
+        primal_ref[...] = new
     moved = new - primal
     change_ref[...] = jnp.full((8, 128), jnp.sum(moved * moved), f32)
     weight_ref[...] = weight
@@ -365,12 +382,13 @@
     lax.fori_loop(0, CHIPS, put, 0, unroll=8)
 
 
-def finish_kernel(place_ref, same_ref, cross_ref, weight_in, dual_ref, weight_ref):
+def finish_kernel(index_ref, same_ref, cross_ref, weight_in, dual_ref, weight_ref):
     def add(i, total):
         return total + (same_ref[i] + cross_ref[i])
 
     total = lax.fori_loop(0, CHIPS, add, jnp.zeros((8, 128), f32), unroll=8)
     total = jnp.broadcast_to(total[2:3, :], (8, 128))
+    place_ref = views(index_ref)[2]
     weight_ref[0] = next_weight(weight_in[...], total)[0, 0]
     core = place_ref[0]
     first = place_ref[2] * (BLOCKS // 2)
@@ -402,7 +420,7 @@
     )
 
 
-TILE = pltpu.VMEM((SLOTS - CHUNK, TR, CB), bf16)
+TILE = pltpu.VMEM((SLOTS - KEPT, TR, CB), bf16)
 TABLE = pltpu.VMEM((COL_BLOCKS, 8, 128), f32)
 IMAGE = pltpu.VMEM((BLOCKS + 1, 8, 128), f32)
 DMA = pltpu.SemaphoreType.DMA
@@ -412,18 +430,16 @@
     return call(
         first_kernel,
         "first_pass",
-        [ANY, ANY, SMEM, ANY, ANY, ANY],
+        [SMEM, ANY, ANY, ANY],
         (
-            sds((SLOTS,), jnp.int32),
+            sds((INDEX,), jnp.int32),
             sds((BLOCKS, TR)),
             sds((CHIPS, SHARE, 128)),
             sds((CHIPS, SHARE, 128)),
-            sds((CHUNK, TR, CB), bf16),
+            sds((KEPT, TR, CB), bf16),
         ),
         (SMEM, VMEM, VMEM, VMEM, VMEM),
         (
-            pltpu.SMEM((BLOCKS,), jnp.int32),
-            pltpu.SMEM((SLOTS,), jnp.int32),
             pltpu.VMEM((BLOCKS, TR), bf16),
             pltpu.VMEM((BLOCKS + 8, TR), f32),
             TABLE,
@@ -431,7 +447,7 @@
             TABLE,
             IMAGE,
             DMA((CHUNKS,)),
-            DMA((4,)),
+            DMA((2,)),
         ),
         limit=PASS_LIMIT,
     )(*args)
@@ -441,7 +457,7 @@
     return call(
         middle_kernel,
         "middle_pass",
-        [SMEM] * 3 + [ANY] + [VMEM] * 8,
+        [SMEM, ANY] + [VMEM] * 8,
         (sds((BLOCKS, TR)), sds((BLOCKS, TR))) + (sds((CHIPS, SHARE + 8, 128)),) * 2,
         (VMEM,) * 4,
         (TABLE, TILE, TABLE, IMAGE, DMA((CHUNKS,))),
@@ -453,10 +469,10 @@
     return call(
         last_kernel,
         "last_pass",
-        [SMEM] * 4 + [ANY] + [VMEM] * 8,
-        (sds((ROWS_P, 128)), sds((CHIPS, 8, 128))),
-        (VMEM,) * 2,
-        (TABLE, TILE, IMAGE, DMA((CHUNKS,))),
+        [SMEM, ANY] + [VMEM] * 8,
+        (sds((2 * CHIPS, SHARE, 128)), sds((CHIPS, 8, 128))),
+        (ANY, VMEM),
+        (TABLE, TILE, IMAGE, DMA((CHUNKS,)), DMA((2,))),
         limit=PASS_LIMIT,
     )(*args)
 
@@ -489,6 +505,7 @@
     place = jnp.stack(
         [core, core * CHIPS + lax.axis_index(CHIP), lax.axis_index("grp")]
     ).astype(jnp.int32)
+    raw = jnp.concatenate([block_counts, tile_column, destination, place])
     bounds = row_bounds.astype(f32).reshape(BLOCKS, TR)
     dual_bf = dual_start.reshape(BLOCKS, TR)
     dual = dual_bf.astype(f32)
@@ -496,8 +513,8 @@
     part = sds((SHARE, 128))
     tiny = sds((8, 128))
 
-    owners, before, own, other, kept = first_call(
-        block_counts, tile_column, place, matrix_tiles, dual_bf,
+    index, before, own, other, kept = first_call(
+        raw, matrix_tiles, dual_bf,
         primal_start.reshape(COL_BLOCKS, 8, 128),
     )
 
@@ -514,27 +531,28 @@
                 (VMEM,) * 7,
                 limit=4,
             )(
-                arrived, place, primal_start.reshape(wide), cost_vector.reshape(wide),
+                arrived, index, primal_start.reshape(wide), cost_vector.reshape(wide),
                 upper_bound.reshape(wide),
             )
         else:
-            primal, send, change, weight, sigma = call(
+            send, change, weight, sigma, *primal = call(
                 lambda *refs: update_kernel(False, *refs),
                 "update",
                 [VMEM] * 5,
-                (part, send_shape, tiny, tiny, tiny),
-                (VMEM,) * 5,
+                (send_shape, tiny, tiny, tiny) + (() if last else (part,)),
+                (VMEM,) * (4 if last else 5),
                 limit=4,
             )(arrived, primal, cost, upper, weight)
+            primal = None if last else primal[0]
         near, far = gathered(send)
         if last:
             break
         dual, before, own, other = middle_call(
-            tile_column, owners, place, matrix_tiles, kept, near, far, bounds, dual, before, change,
+            index, matrix_tiles, kept, near, far, bounds, dual, before, change,
             sigma,
         )
     primal_final, send = last_call(
-        tile_column, owners, place, destination, matrix_tiles, kept, near, far, bounds, dual, before, change,
+        index, matrix_tiles, kept, near, far, bounds, dual, before, change,
         sigma,
     )
     same, cross = gathered(send)
@@ -545,7 +563,7 @@
         (sds((BLOCKS, TR)), sds((1,))),
         (VMEM, SMEM),
         limit=4,
-    )(place, same, cross, weight)
+    )(index, same, cross, weight)
     return (primal_final.reshape(-1), dual_final.reshape(-1), weight)
 
 

time: 178 us -> 175 us (0.983)
  Pallas kernels: 40.3 us -> 38.1 us
    pallas_call x6, Pallas kernels: 37.9 us -> 35.7 us  [the longest x2 17.1 us: middle_call(): call(middle_kernel, 'middle_pass', [SMEM, ANY] + [VMEM] * 8, (sds((BLOCKS...]
where the time goes in v4:
time: 175 us
  blocking collectives  109 us (62%)
  Pallas kernels  38.1 us (22%)
  starting transfers between devices  13.4 us (8%)
  waiting for transfers between devices  10.4 us (6%)
  local copies, waits for them, and re-layouts  2.7 us (2%)
    all_to_all x4, blocking collectives, gathered(): own = lax.all_to_all(send, CHIP, 0, 0, tiled=True)  57.6 us
    all_to_all x3, blocking collectives, summed(): return lax.all_to_all(merged, CHIP, 0, 0, tiled=True)  51.7 us
    pallas_call x2, Pallas kernels, middle_call(): call(middle_kernel, 'middle_pass', [SMEM, ANY] + [VMEM] * 8, (sds((BLOCKS...  17.1 us
    ppermute x4, starting transfers between devices, gathered(): return (own, lax.ppermute(own, CORE, SWAP))  11 us
    pallas_call x1, Pallas kernels, first_call(): call(first_kernel, 'first_pass', [SMEM, ANY, ANY, ANY], (sds((INDEX,), jn...  9.94 us
    pallas_call x1, Pallas kernels, last_call(): call(last_kernel, 'last_pass', [SMEM, ANY] + [VMEM] * 8, (sds((2 * CHIPS,...  7.92 us
    ppermute x3, waiting for transfers between devices, summed(): crossed = lax.ppermute(other, CORE, SWAP)  5.36 us
    ppermute x4, waiting for transfers between devices, gathered(): return (own, lax.ppermute(own, CORE, SWAP))  5.01 us
  transfers between devices with their start and end apart: 7, of which 7 were waited for; matrix products, arithmetic and copies ran while one was open for 0% of the time, Pallas kernels for 0%

profile of v4, /device:TPU:1, one launch (start us, length us, event | category | flops | bytes accessed | tf_op | source)
XLA Modules:
  0.0 174.8 jit_solution(7387545836130716434)
XLA Ops:
  0.6 0.0 copy-start.4
  0.7 0.8 concatenate.3.raw_ref
  1.4 0.0 copy-start
  1.4 1.2 copy-done
  2.6 0.0 copy-start.3
  2.6 0.7 copy-done.3
  3.3 0.0 copy-start.1
  3.3 0.0 copy-start.2
  3.3 9.9 %first_pass.1 = (s32[256]{0:T(256)S(1)}, f32[32,128]{1,0:T(8,128)S(1)}, f32[64,16,128]{2,1,0:T(8,128)S(1)}, f32[64,16,128]{2,1,0:T(8,128)S(1)}, bf16[12,128,1024]{2,1,0:T(8,128)(2,1)S(1)}) custom-call(s32[147]{0:T(256)S(1)} %concatenate.3.raw_ref, bf16[80,128,1024]{2,1,0:T(8,128)(2,1)} %tiles_hbm.7, bf16[32,128]{1,0:T(8,128)(2,1)S(1)} %bitcast.18, ...), custom_call_target="tpu_custom_call" | custom-call | tf_op jit(solution)/shard_map/first_pass/pallas_call | solution.py:430
  13.3 1.5 collective-permute-start
  14.8 1.5 collective-permute-done.other_ref
  16.3 0.1 merge.3
  16.4 21.0 %all_to_all.35.refs_0_ = bf16[64,16,128]{2,1,0:T(8,128)(2,1)S(1)} all-to-all(bf16[64,16,128]{2,1,0:T(8,128)(2,1)S(1)} %merge.3), channel_id=1, replica_groups=mesh['grp'=4,'dev_0'=4,'dev_1'=4,'dev_2'=2] {'grp','dev_0','dev_1'}, dimensions={0} | all-to-all | bytes 524288 | tf_op jit(solution)/shard_map/all_to_all | solution.py:485
  37.3 0.0 copy-done.1
  37.3 0.0 copy-done.2
  37.3 0.8 update.3
  38.1 13.8 %all_to_all.36.own_in = bf16[64,16,128]{2,1,0:T(8,128)(2,1)S(1)} all-to-all(bf16[64,16,128]{2,1,0:T(8,128)(2,1)S(1)} %get-tuple-element.40), channel_id=1, replica_groups=mesh['grp'=4,'dev_0'=4,'dev_1'=4,'dev_2'=2] {'grp','dev_0','dev_1'}, dimensions={0} | all-to-all | bytes 524288 | tf_op jit(solution)/shard_map/all_to_all | solution.py:489
  51.9 3.1 %collective-permute-start.1 = (bf16[64,16,128]{2,1,0:T(8,128)(2,1)S(1)}, bf16[64,16,128]{2,1,0:T(8,128)(2,1)S(1)}, u32[]{:S(2)}, u32[]{:S(2)}) collective-permute-start(bf16[64,16,128]{2,1,0:T(8,128)(2,1)S(1)} %all_to_all.36.own_in), channel_id=1, source_target_pairs={{0,1},{1,0},{2,3},{3,2},{4,5},{5,4},{6,7},{7,6},{8,9},{9,8},{10,11... | collective-permute-start | bytes 786440 | tf_op jit(solution)/shard_map/ppermute | solution.py:490
  55.0 0.0 copy-done.4
  55.0 1.2 collective-permute-done.1.other_in
  56.2 8.5 %middle_pass.2 = (f32[32,128]{1,0:T(8,128)S(1)}, f32[32,128]{1,0:T(8,128)S(1)}, f32[64,24,128]{2,1,0:T(8,128)S(1)}, f32[64,24,128]{2,1,0:T(8,128)S(1)}) custom-call(s32[256]{0:T(256)S(1)} %get-tuple-element.36.refs_1_.index_ref, bf16[80,128,1024]{2,1,0:T(8,128)(2,1)} %tiles_hbm.7, bf16[12,128,1024]{2,1,0:T(8,128)(2,1)S(1)} %get-tuple-element.37.kept_ref, ...), custom_call_target="tpu_custom_call" | custom-call | tf_op jit(solution)/shard_map/middle_pass/pallas_call | solution.py:457
  64.7 0.5 collective-permute-start.2
  65.2 1.9 %collective-permute-done.2.other_ref = f32[64,24,128]{2,1,0:T(8,128)S(1)} collective-permute-done((f32[64,24,128]{2,1,0:T(8,128)S(1)}, f32[64,24,128]{2,1,0:T(8,128)S(1)}, u32[]{:S(2)}, u32[]{:S(2)}) %collective-permute-start.2) | collective-permute-done | bytes 786464 | tf_op jit(solution)/shard_map/ppermute | solution.py:481
  67.1 0.1 merge.4
  67.2 15.4 %all_to_all.37.refs_0_ = bf16[64,24,128]{2,1,0:T(8,128)(2,1)S(1)} all-to-all(bf16[64,24,128]{2,1,0:T(8,128)(2,1)S(1)} %merge.4), channel_id=1, replica_groups=mesh['grp'=4,'dev_0'=4,'dev_1'=4,'dev_2'=2] {'grp','dev_0','dev_1'}, dimensions={0} | all-to-all | bytes 786432 | tf_op jit(solution)/shard_map/all_to_all | solution.py:485
  82.6 0.4 update.4
  83.0 14.0 %all_to_all.38.own_in = bf16[64,16,128]{2,1,0:T(8,128)(2,1)S(1)} all-to-all(bf16[64,16,128]{2,1,0:T(8,128)(2,1)S(1)} %get-tuple-element.50), channel_id=1, replica_groups=mesh['grp'=4,'dev_0'=4,'dev_1'=4,'dev_2'=2] {'grp','dev_0','dev_1'}, dimensions={0} | all-to-all | bytes 524288 | tf_op jit(solution)/shard_map/all_to_all | solution.py:489
  96.9 3.2 %collective-permute-start.3 = (bf16[64,16,128]{2,1,0:T(8,128)(2,1)S(1)}, bf16[64,16,128]{2,1,0:T(8,128)(2,1)S(1)}, u32[]{:S(2)}, u32[]{:S(2)}) collective-permute-start(bf16[64,16,128]{2,1,0:T(8,128)(2,1)S(1)} %all_to_all.38.own_in), channel_id=1, source_target_pairs={{0,1},{1,0},{2,3},{3,2},{4,5},{5,4},{6,7},{7,6},{8,9},{9,8},{10,11... | collective-permute-start | bytes 786440 | tf_op jit(solution)/shard_map/ppermute | solution.py:490
  100.1 1.2 collective-permute-done.3.other_in
  101.3 8.5 %middle_pass.3 = (f32[32,128]{1,0:T(8,128)S(1)}, f32[32,128]{1,0:T(8,128)S(1)}, f32[64,24,128]{2,1,0:T(8,128)S(1)}, f32[64,24,128]{2,1,0:T(8,128)S(1)}) custom-call(s32[256]{0:T(256)S(1)} %get-tuple-element.36.refs_1_.index_ref, bf16[80,128,1024]{2,1,0:T(8,128)(2,1)} %tiles_hbm.7, bf16[12,128,1024]{2,1,0:T(8,128)(2,1)S(1)} %get-tuple-element.37.kept_ref, ...), custom_call_target="tpu_custom_call" | custom-call | tf_op jit(solution)/shard_map/middle_pass/pallas_call | solution.py:457
  109.8 0.5 collective-permute-start.4
  110.3 1.9 %collective-permute-done.4.other_ref = f32[64,24,128]{2,1,0:T(8,128)S(1)} collective-permute-done((f32[64,24,128]{2,1,0:T(8,128)S(1)}, f32[64,24,128]{2,1,0:T(8,128)S(1)}, u32[]{:S(2)}, u32[]{:S(2)}) %collective-permute-start.4) | collective-permute-done | bytes 786464 | tf_op jit(solution)/shard_map/ppermute | solution.py:481
  112.2 0.1 merge.5
  112.3 15.4 %all_to_all.39.refs_0_ = bf16[64,24,128]{2,1,0:T(8,128)(2,1)S(1)} all-to-all(bf16[64,24,128]{2,1,0:T(8,128)(2,1)S(1)} %merge.5), channel_id=1, replica_groups=mesh['grp'=4,'dev_0'=4,'dev_1'=4,'dev_2'=2] {'grp','dev_0','dev_1'}, dimensions={0} | all-to-all | bytes 786432 | tf_op jit(solution)/shard_map/all_to_all | solution.py:485
  127.7 0.4 update.5
  128.0 15.6 %all_to_all.40.own_in = f32[64,16,128]{2,1,0:T(8,128)S(1)} all-to-all(f32[64,16,128]{2,1,0:T(8,128)S(1)} %get-tuple-element.59), channel_id=1, replica_groups=mesh['grp'=4,'dev_0'=4,'dev_1'=4,'dev_2'=2] {'grp','dev_0','dev_1'}, dimensions={0} | all-to-all | bytes 1048576 | tf_op jit(solution)/shard_map/all_to_all | solution.py:489
  143.6 3.2 %collective-permute-start.5 = (f32[64,16,128]{2,1,0:T(8,128)S(1)}, f32[64,16,128]{2,1,0:T(8,128)S(1)}, u32[]{:S(2)}, u32[]{:S(2)}) collective-permute-start(f32[64,16,128]{2,1,0:T(8,128)S(1)} %all_to_all.40.own_in), channel_id=1, source_target_pairs={{0,1},{1,0},{2,3},{3,2},{4,5},{5,4},{6,7},{7,6},{8,9},{9,8},{10,11... | collective-permute-start | bytes 1572872 | tf_op jit(solution)/shard_map/ppermute | solution.py:490
  146.8 1.5 collective-permute-done.5.other_in
  148.4 7.9 %last_pass.1 = (f32[128,16,128]{2,1,0:T(8,128)}, f32[64,8,128]{2,1,0:T(8,128)S(1)}) custom-call(s32[256]{0:T(256)S(1)} %get-tuple-element.36.refs_1_.index_ref, bf16[80,128,1024]{2,1,0:T(8,128)(2,1)} %tiles_hbm.7, bf16[12,128,1024]{2,1,0:T(8,128)(2,1)S(1)} %get-tuple-element.37.kept_ref, f32[64,16,128]{2,1,0:T(8,128)S(1)} %all_to_all.40.own_in, ...), custom_call_target="tpu_custom_call" | custom-call | tf_op jit(solution)/shard_map/last_pass/pallas_call | solution.py:469
  156.3 14.3 %all_to_all.41.same_ref = f32[64,8,128]{2,1,0:T(8,128)S(1)} all-to-all(f32[64,8,128]{2,1,0:T(8,128)S(1)} %get-tuple-element.65), channel_id=1, replica_groups=mesh['grp'=4,'dev_0'=4,'dev_1'=4,'dev_2'=2] {'grp','dev_0','dev_1'}, dimensions={0} | all-to-all | bytes 524288 | tf_op jit(solution)/shard_map/all_to_all | solution.py:489
  170.5 1.6 collective-permute-start.6
  172.1 1.2 collective-permute-done.6.cross_ref
  173.3 1.3 finish.1
  (2 shorter events, 0.0 us)
Async XLA Ops:
  0.6 54.4 %copy-start.4 = (bf16[4096]{0:T(1024)(128)(2,1)S(1)}, bf16[4096]{0:T(1024)(128)(2,1)}, u32[]{:S(2)}) copy-start(bf16[4096]{0:T(1024)(128)(2,1)} %param.13) | copy-start | bytes 24580
  1.4 1.2 copy-start
  2.6 0.7 copy-start.3
  3.3 34.0 %copy-start.1 = (f32[262144]{0:T(1024)S(1)}, f32[262144]{0:T(1024)}, u32[]{:S(2)}) copy-start(f32[262144]{0:T(1024)} %param.16) | copy-start | bytes 3145732
  3.3 34.0 %copy-start.2 = (f32[262144]{0:T(1024)S(1)}, f32[262144]{0:T(1024)}, u32[]{:S(2)}) copy-start(f32[262144]{0:T(1024)} %param.17) | copy-start | bytes 3145732
  13.3 3.0 %collective-permute-start = (f32[64,16,128]{2,1,0:T(8,128)S(1)}, f32[64,16,128]{2,1,0:T(8,128)S(1)}, u32[]{:S(2)}, u32[]{:S(2)}) collective-permute-start(f32[64,16,128]{2,1,0:T(8,128)S(1)} %get-tuple-element.39), channel_id=1, source_target_pairs={{0,1},{1,0},{2,3},{3,2},{4,5},{5,4},{6,7},{7,6},{8,9},{9,8},{10,11... | collective-permute-start | bytes 1572872 | tf_op jit(solution)/shard_map/ppermute | solution.py:481
  51.9 4.2 %collective-permute-start.1 = (bf16[64,16,128]{2,1,0:T(8,128)(2,1)S(1)}, bf16[64,16,128]{2,1,0:T(8,128)(2,1)S(1)}, u32[]{:S(2)}, u32[]{:S(2)}) collective-permute-start(bf16[64,16,128]{2,1,0:T(8,128)(2,1)S(1)} %all_to_all.36.own_in), channel_id=1, source_target_pairs={{0,1},{1,0},{2,3},{3,2},{4,5},{5,4},{6,7},{7,6},{8,9},{9,8},{10,11... | collective-permute-start | bytes 786440 | tf_op jit(solution)/shard_map/ppermute | solution.py:490
  64.7 2.4 %collective-permute-start.2 = (f32[64,24,128]{2,1,0:T(8,128)S(1)}, f32[64,24,128]{2,1,0:T(8,128)S(1)}, u32[]{:S(2)}, u32[]{:S(2)}) collective-permute-start(f32[64,24,128]{2,1,0:T(8,128)S(1)} %get-tuple-element.45), channel_id=1, source_target_pairs={{0,1},{1,0},{2,3},{3,2},{4,5},{5,4},{6,7},{7,6},{8,9},{9,8},{10,11... | collective-permute-start | bytes 2359304 | tf_op jit(solution)/shard_map/ppermute | solution.py:481
  96.9 4.3 %collective-permute-start.3 = (bf16[64,16,128]{2,1,0:T(8,128)(2,1)S(1)}, bf16[64,16,128]{2,1,0:T(8,128)(2,1)S(1)}, u32[]{:S(2)}, u32[]{:S(2)}) collective-permute-start(bf16[64,16,128]{2,1,0:T(8,128)(2,1)S(1)} %all_to_all.38.own_in), channel_id=1, source_target_pairs={{0,1},{1,0},{2,3},{3,2},{4,5},{5,4},{6,7},{7,6},{8,9},{9,8},{10,11... | collective-permute-start | bytes 786440 | tf_op jit(solution)/shard_map/ppermute | solution.py:490
  109.8 2.4 %collective-permute-start.4 = (f32[64,24,128]{2,1,0:T(8,128)S(1)}, f32[64,24,128]{2,1,0:T(8,128)S(1)}, u32[]{:S(2)}, u32[]{:S(2)}) collective-permute-start(f32[64,24,128]{2,1,0:T(8,128)S(1)} %get-tuple-element.56), channel_id=1, source_target_pairs={{0,1},{1,0},{2,3},{3,2},{4,5},{5,4},{6,7},{7,6},{8,9},{9,8},{10,11... | collective-permute-start | bytes 2359304 | tf_op jit(solution)/shard_map/ppermute | solution.py:481
  143.6 4.7 %collective-permute-start.5 = (f32[64,16,128]{2,1,0:T(8,128)S(1)}, f32[64,16,128]{2,1,0:T(8,128)S(1)}, u32[]{:S(2)}, u32[]{:S(2)}) collective-permute-start(f32[64,16,128]{2,1,0:T(8,128)S(1)} %all_to_all.40.own_in), channel_id=1, source_target_pairs={{0,1},{1,0},{2,3},{3,2},{4,5},{5,4},{6,7},{7,6},{8,9},{9,8},{10,11... | collective-permute-start | bytes 1572872 | tf_op jit(solution)/shard_map/ppermute | solution.py:490
  170.5 2.8 %collective-permute-start.6 = (f32[64,8,128]{2,1,0:T(8,128)S(1)}, f32[64,8,128]{2,1,0:T(8,128)S(1)}, u32[]{:S(2)}, u32[]{:S(2)}) collective-permute-start(f32[64,8,128]{2,1,0:T(8,128)S(1)} %all_to_all.41.same_ref), channel_id=1, source_target_pairs={{0,1},{1,0},{2,3},{3,2},{4,5},{5,4},{6,7},{7,6},{8,9},{9,8},{10,11... | collective-permute-start | bytes 786440 | tf_op jit(solution)/shard_map/ppermute | solution.py:490

commit v5 on v4

--- a/solution.py
+++ b/solution.py
@@ -127,11 +127,13 @@
             at = side * (COL_BLOCKS // 2) + 2 * i
             ref[i, pl.ds(0, 8), :] = sum_ref[at]
             ref[i, pl.ds(8, 8), :] = sum_ref[at + 1]
-            if scalars is not None:
-                ref[i, pl.ds(SHARE, 8), :] = scalars
         return carry
 
     lax.fori_loop(0, CHIPS, put, 0, unroll=4)
+    if scalars is not None:
+        for ref in (own_ref, other_ref):
+            ref[CHIPS, pl.ds(0, 8), :] = scalars
+            ref[CHIPS, pl.ds(8, 8), :] = scalars
 
 
 def chunk_of(i):
@@ -205,9 +207,9 @@
 
 
 def merge_kernel(own_ref, other_ref, out_ref):
-    rows = own_ref.shape[1]
+    rows = out_ref.shape[1]
     if rows > SHARE:
-        rest = own_ref[0, pl.ds(SHARE, 8), :] + other_ref[0, pl.ds(SHARE, 8), :]
+        rest = own_ref[CHIPS, pl.ds(0, 8), :] + other_ref[CHIPS, pl.ds(0, 8), :]
         sub = lax.broadcasted_iota(jnp.int32, (8, 128), 0)
         parts = jnp.zeros((8, 128), f32)
         for p in range(3):
@@ -458,7 +460,7 @@
         middle_kernel,
         "middle_pass",
         [SMEM, ANY] + [VMEM] * 8,
-        (sds((BLOCKS, TR)), sds((BLOCKS, TR))) + (sds((CHIPS, SHARE + 8, 128)),) * 2,
+        (sds((BLOCKS, TR)), sds((BLOCKS, TR))) + (sds((CHIPS + 1, SHARE, 128)),) * 2,
         (VMEM,) * 4,
         (TABLE, TILE, TABLE, IMAGE, DMA((CHUNKS,))),
         limit=PASS_LIMIT,
@@ -479,9 +481,10 @@
 
 def summed(own, other):
     crossed = lax.ppermute(other, CORE, SWAP)
-    merged = call(merge_kernel, "merge", [VMEM] * 2, sds(own.shape, bf16), VMEM, limit=4)(
-        own, crossed
-    )
+    rows = SHARE if own.shape[0] == CHIPS else SHARE + 8
+    merged = call(
+        merge_kernel, "merge", [VMEM] * 2, sds((CHIPS, rows, 128), bf16), VMEM, limit=4
+    )(own, crossed)
     return lax.all_to_all(merged, CHIP, 0, 0, tiled=True)
 
 

time: 175 us -> 175 us (level)
  no operation moved by 1% of the time
where the time goes in v5:
time: 175 us; the launch traced here: 174 us
  blocking collectives  109 us (62%)
  Pallas kernels  38.1 us (22%)
  starting transfers between devices  13.3 us (8%)
  waiting for transfers between devices  9.72 us (6%)
  local copies, waits for them, and re-layouts  2.7 us (2%)
    all_to_all x4, blocking collectives, gathered(): own = lax.all_to_all(send, CHIP, 0, 0, tiled=True)  57.6 us
    all_to_all x3, blocking collectives, summed(): return lax.all_to_all(merged, CHIP, 0, 0, tiled=True)  51.7 us
    pallas_call x2, Pallas kernels, middle_call(): call(middle_kernel, 'middle_pass', [SMEM, ANY] + [VMEM] * 8, (sds((BLOCKS...  17.1 us
    ppermute x4, starting transfers between devices, gathered(): return (own, lax.ppermute(own, CORE, SWAP))  11 us
    pallas_call x1, Pallas kernels, first_call(): call(first_kernel, 'first_pass', [SMEM, ANY, ANY, ANY], (sds((INDEX,), jn...  9.94 us
    pallas_call x1, Pallas kernels, last_call(): call(last_kernel, 'last_pass', [SMEM, ANY] + [VMEM] * 8, (sds((2 * CHIPS,...  7.92 us
    ppermute x4, waiting for transfers between devices, gathered(): return (own, lax.ppermute(own, CORE, SWAP))  5.01 us
    ppermute x3, waiting for transfers between devices, summed(): crossed = lax.ppermute(other, CORE, SWAP)  4.71 us
  transfers between devices with their start and end apart: 7, of which 7 were waited for; matrix products, arithmetic and copies ran while one was open for 0% of the time, Pallas kernels for 0%

profile of v5, /device:TPU:1, one launch (start us, length us, event | category | flops | bytes accessed | tf_op | source)
XLA Modules:
  0.0 174.1 jit_solution(4677496380609104403)
XLA Ops:
  0.6 0.0 copy-start.4
  0.7 0.8 concatenate.3.raw_ref
  1.4 0.0 copy-start
  1.4 1.2 copy-done
  2.6 0.0 copy-start.3
  2.6 0.7 copy-done.3
  3.3 0.0 copy-start.1
  3.3 0.0 copy-start.2
  3.3 9.9 %first_pass.1 = (s32[256]{0:T(256)S(1)}, f32[32,128]{1,0:T(8,128)S(1)}, f32[64,16,128]{2,1,0:T(8,128)S(1)}, f32[64,16,128]{2,1,0:T(8,128)S(1)}, bf16[12,128,1024]{2,1,0:T(8,128)(2,1)S(1)}) custom-call(s32[147]{0:T(256)S(1)} %concatenate.3.raw_ref, bf16[80,128,1024]{2,1,0:T(8,128)(2,1)} %tiles_hbm.7, bf16[32,128]{1,0:T(8,128)(2,1)S(1)} %bitcast.18, ...), custom_call_target="tpu_custom_call" | custom-call | tf_op jit(solution)/shard_map/first_pass/pallas_call | solution.py:432
  13.3 1.5 collective-permute-start
  14.8 1.5 collective-permute-done.other_ref
  16.3 0.1 merge.3
  16.4 21.0 %all_to_all.35.refs_0_ = bf16[64,16,128]{2,1,0:T(8,128)(2,1)S(1)} all-to-all(bf16[64,16,128]{2,1,0:T(8,128)(2,1)S(1)} %merge.3), channel_id=1, replica_groups=mesh['grp'=4,'dev_0'=4,'dev_1'=4,'dev_2'=2] {'grp','dev_0','dev_1'}, dimensions={0} | all-to-all | bytes 524288 | tf_op jit(solution)/shard_map/all_to_all | solution.py:488
  37.3 0.0 copy-done.1
  37.3 0.0 copy-done.2
  37.3 0.8 update.3
  38.1 13.8 %all_to_all.36.own_in = bf16[64,16,128]{2,1,0:T(8,128)(2,1)S(1)} all-to-all(bf16[64,16,128]{2,1,0:T(8,128)(2,1)S(1)} %get-tuple-element.40), channel_id=1, replica_groups=mesh['grp'=4,'dev_0'=4,'dev_1'=4,'dev_2'=2] {'grp','dev_0','dev_1'}, dimensions={0} | all-to-all | bytes 524288 | tf_op jit(solution)/shard_map/all_to_all | solution.py:492
  51.9 3.1 %collective-permute-start.1 = (bf16[64,16,128]{2,1,0:T(8,128)(2,1)S(1)}, bf16[64,16,128]{2,1,0:T(8,128)(2,1)S(1)}, u32[]{:S(2)}, u32[]{:S(2)}) collective-permute-start(bf16[64,16,128]{2,1,0:T(8,128)(2,1)S(1)} %all_to_all.36.own_in), channel_id=1, source_target_pairs={{0,1},{1,0},{2,3},{3,2},{4,5},{5,4},{6,7},{7,6},{8,9},{9,8},{10,11... | collective-permute-start | bytes 786440 | tf_op jit(solution)/shard_map/ppermute | solution.py:493
  55.0 0.0 copy-done.4
  55.0 1.2 collective-permute-done.1.other_in
  56.2 8.5 %middle_pass.2 = (f32[32,128]{1,0:T(8,128)S(1)}, f32[32,128]{1,0:T(8,128)S(1)}, f32[65,16,128]{2,1,0:T(8,128)S(1)}, f32[65,16,128]{2,1,0:T(8,128)S(1)}) custom-call(s32[256]{0:T(256)S(1)} %get-tuple-element.36.refs_1_.index_ref, bf16[80,128,1024]{2,1,0:T(8,128)(2,1)} %tiles_hbm.7, bf16[12,128,1024]{2,1,0:T(8,128)(2,1)S(1)} %get-tuple-element.37.kept_ref, ...), custom_call_target="tpu_custom_call" | custom-call | tf_op jit(solution)/shard_map/middle_pass/pallas_call | solution.py:459
  64.7 0.4 collective-permute-start.2
  65.1 1.6 collective-permute-done.2.other_ref
  66.7 0.1 merge.4
  66.9 15.4 %all_to_all.37.refs_0_ = bf16[64,24,128]{2,1,0:T(8,128)(2,1)S(1)} all-to-all(bf16[64,24,128]{2,1,0:T(8,128)(2,1)S(1)} %merge.4), channel_id=1, replica_groups=mesh['grp'=4,'dev_0'=4,'dev_1'=4,'dev_2'=2] {'grp','dev_0','dev_1'}, dimensions={0} | all-to-all | bytes 786432 | tf_op jit(solution)/shard_map/all_to_all | solution.py:488
  82.2 0.4 update.4
  82.6 14.0 %all_to_all.38.own_in = bf16[64,16,128]{2,1,0:T(8,128)(2,1)S(1)} all-to-all(bf16[64,16,128]{2,1,0:T(8,128)(2,1)S(1)} %get-tuple-element.50), channel_id=1, replica_groups=mesh['grp'=4,'dev_0'=4,'dev_1'=4,'dev_2'=2] {'grp','dev_0','dev_1'}, dimensions={0} | all-to-all | bytes 524288 | tf_op jit(solution)/shard_map/all_to_all | solution.py:492
  96.6 3.1 %collective-permute-start.3 = (bf16[64,16,128]{2,1,0:T(8,128)(2,1)S(1)}, bf16[64,16,128]{2,1,0:T(8,128)(2,1)S(1)}, u32[]{:S(2)}, u32[]{:S(2)}) collective-permute-start(bf16[64,16,128]{2,1,0:T(8,128)(2,1)S(1)} %all_to_all.38.own_in), channel_id=1, source_target_pairs={{0,1},{1,0},{2,3},{3,2},{4,5},{5,4},{6,7},{7,6},{8,9},{9,8},{10,11... | collective-permute-start | bytes 786440 | tf_op jit(solution)/shard_map/ppermute | solution.py:493
  99.8 1.2 collective-permute-done.3.other_in
  100.9 8.5 %middle_pass.3 = (f32[32,128]{1,0:T(8,128)S(1)}, f32[32,128]{1,0:T(8,128)S(1)}, f32[65,16,128]{2,1,0:T(8,128)S(1)}, f32[65,16,128]{2,1,0:T(8,128)S(1)}) custom-call(s32[256]{0:T(256)S(1)} %get-tuple-element.36.refs_1_.index_ref, bf16[80,128,1024]{2,1,0:T(8,128)(2,1)} %tiles_hbm.7, bf16[12,128,1024]{2,1,0:T(8,128)(2,1)S(1)} %get-tuple-element.37.kept_ref, ...), custom_call_target="tpu_custom_call" | custom-call | tf_op jit(solution)/shard_map/middle_pass/pallas_call | solution.py:459
  109.5 0.4 collective-permute-start.4
  109.9 1.6 collective-permute-done.4.other_ref
  111.5 0.1 merge.5
  111.6 15.4 %all_to_all.39.refs_0_ = bf16[64,24,128]{2,1,0:T(8,128)(2,1)S(1)} all-to-all(bf16[64,24,128]{2,1,0:T(8,128)(2,1)S(1)} %merge.5), channel_id=1, replica_groups=mesh['grp'=4,'dev_0'=4,'dev_1'=4,'dev_2'=2] {'grp','dev_0','dev_1'}, dimensions={0} | all-to-all | bytes 786432 | tf_op jit(solution)/shard_map/all_to_all | solution.py:488
  127.0 0.4 update.5
  127.4 15.6 %all_to_all.40.own_in = f32[64,16,128]{2,1,0:T(8,128)S(1)} all-to-all(f32[64,16,128]{2,1,0:T(8,128)S(1)} %get-tuple-element.59), channel_id=1, replica_groups=mesh['grp'=4,'dev_0'=4,'dev_1'=4,'dev_2'=2] {'grp','dev_0','dev_1'}, dimensions={0} | all-to-all | bytes 1048576 | tf_op jit(solution)/shard_map/all_to_all | solution.py:492
  142.9 3.2 %collective-permute-start.5 = (f32[64,16,128]{2,1,0:T(8,128)S(1)}, f32[64,16,128]{2,1,0:T(8,128)S(1)}, u32[]{:S(2)}, u32[]{:S(2)}) collective-permute-start(f32[64,16,128]{2,1,0:T(8,128)S(1)} %all_to_all.40.own_in), channel_id=1, source_target_pairs={{0,1},{1,0},{2,3},{3,2},{4,5},{5,4},{6,7},{7,6},{8,9},{9,8},{10,11... | collective-permute-start | bytes 1572872 | tf_op jit(solution)/shard_map/ppermute | solution.py:493
  146.1 1.5 collective-permute-done.5.other_in
  147.7 7.9 %last_pass.1 = (f32[128,16,128]{2,1,0:T(8,128)}, f32[64,8,128]{2,1,0:T(8,128)S(1)}) custom-call(s32[256]{0:T(256)S(1)} %get-tuple-element.36.refs_1_.index_ref, bf16[80,128,1024]{2,1,0:T(8,128)(2,1)} %tiles_hbm.7, bf16[12,128,1024]{2,1,0:T(8,128)(2,1)S(1)} %get-tuple-element.37.kept_ref, f32[64,16,128]{2,1,0:T(8,128)S(1)} %all_to_all.40.own_in, ...), custom_call_target="tpu_custom_call" | custom-call | tf_op jit(solution)/shard_map/last_pass/pallas_call | solution.py:471
  155.6 14.2 %all_to_all.41.same_ref = f32[64,8,128]{2,1,0:T(8,128)S(1)} all-to-all(f32[64,8,128]{2,1,0:T(8,128)S(1)} %get-tuple-element.65), channel_id=1, replica_groups=mesh['grp'=4,'dev_0'=4,'dev_1'=4,'dev_2'=2] {'grp','dev_0','dev_1'}, dimensions={0} | all-to-all | bytes 524288 | tf_op jit(solution)/shard_map/all_to_all | solution.py:492
  169.8 1.6 collective-permute-start.6
  171.4 1.2 collective-permute-done.6.cross_ref
  172.6 1.3 finish.1
  (2 shorter events, 0.0 us)
Async XLA Ops:
  0.6 54.4 %copy-start.4 = (bf16[4096]{0:T(1024)(128)(2,1)S(1)}, bf16[4096]{0:T(1024)(128)(2,1)}, u32[]{:S(2)}) copy-start(bf16[4096]{0:T(1024)(128)(2,1)} %param.13) | copy-start | bytes 24580
  1.4 1.2 copy-start
  2.6 0.7 copy-start.3
  3.3 34.0 %copy-start.1 = (f32[262144]{0:T(1024)S(1)}, f32[262144]{0:T(1024)}, u32[]{:S(2)}) copy-start(f32[262144]{0:T(1024)} %param.16) | copy-start | bytes 3145732
  3.3 34.0 %copy-start.2 = (f32[262144]{0:T(1024)S(1)}, f32[262144]{0:T(1024)}, u32[]{:S(2)}) copy-start(f32[262144]{0:T(1024)} %param.17) | copy-start | bytes 3145732
  13.3 3.0 %collective-permute-start = (f32[64,16,128]{2,1,0:T(8,128)S(1)}, f32[64,16,128]{2,1,0:T(8,128)S(1)}, u32[]{:S(2)}, u32[]{:S(2)}) collective-permute-start(f32[64,16,128]{2,1,0:T(8,128)S(1)} %get-tuple-element.39), channel_id=1, source_target_pairs={{0,1},{1,0},{2,3},{3,2},{4,5},{5,4},{6,7},{7,6},{8,9},{9,8},{10,11... | collective-permute-start | bytes 1572872 | tf_op jit(solution)/shard_map/ppermute | solution.py:483
  51.9 4.2 %collective-permute-start.1 = (bf16[64,16,128]{2,1,0:T(8,128)(2,1)S(1)}, bf16[64,16,128]{2,1,0:T(8,128)(2,1)S(1)}, u32[]{:S(2)}, u32[]{:S(2)}) collective-permute-start(bf16[64,16,128]{2,1,0:T(8,128)(2,1)S(1)} %all_to_all.36.own_in), channel_id=1, source_target_pairs={{0,1},{1,0},{2,3},{3,2},{4,5},{5,4},{6,7},{7,6},{8,9},{9,8},{10,11... | collective-permute-start | bytes 786440 | tf_op jit(solution)/shard_map/ppermute | solution.py:493
  64.7 2.0 %collective-permute-start.2 = (f32[65,16,128]{2,1,0:T(8,128)S(1)}, f32[65,16,128]{2,1,0:T(8,128)S(1)}, u32[]{:S(2)}, u32[]{:S(2)}) collective-permute-start(f32[65,16,128]{2,1,0:T(8,128)S(1)} %get-tuple-element.45), channel_id=1, source_target_pairs={{0,1},{1,0},{2,3},{3,2},{4,5},{5,4},{6,7},{7,6},{8,9},{9,8},{10,11... | collective-permute-start | bytes 1597448 | tf_op jit(solution)/shard_map/ppermute | solution.py:483
  96.6 4.3 %collective-permute-start.3 = (bf16[64,16,128]{2,1,0:T(8,128)(2,1)S(1)}, bf16[64,16,128]{2,1,0:T(8,128)(2,1)S(1)}, u32[]{:S(2)}, u32[]{:S(2)}) collective-permute-start(bf16[64,16,128]{2,1,0:T(8,128)(2,1)S(1)} %all_to_all.38.own_in), channel_id=1, source_target_pairs={{0,1},{1,0},{2,3},{3,2},{4,5},{5,4},{6,7},{7,6},{8,9},{9,8},{10,11... | collective-permute-start | bytes 786440 | tf_op jit(solution)/shard_map/ppermute | solution.py:493
  109.5 2.0 %collective-permute-start.4 = (f32[65,16,128]{2,1,0:T(8,128)S(1)}, f32[65,16,128]{2,1,0:T(8,128)S(1)}, u32[]{:S(2)}, u32[]{:S(2)}) collective-permute-start(f32[65,16,128]{2,1,0:T(8,128)S(1)} %get-tuple-element.56), channel_id=1, source_target_pairs={{0,1},{1,0},{2,3},{3,2},{4,5},{5,4},{6,7},{7,6},{8,9},{9,8},{10,11... | collective-permute-start | bytes 1597448 | tf_op jit(solution)/shard_map/ppermute | solution.py:483
  142.9 4.7 %collective-permute-start.5 = (f32[64,16,128]{2,1,0:T(8,128)S(1)}, f32[64,16,128]{2,1,0:T(8,128)S(1)}, u32[]{:S(2)}, u32[]{:S(2)}) collective-permute-start(f32[64,16,128]{2,1,0:T(8,128)S(1)} %all_to_all.40.own_in), channel_id=1, source_target_pairs={{0,1},{1,0},{2,3},{3,2},{4,5},{5,4},{6,7},{7,6},{8,9},{9,8},{10,11... | collective-permute-start | bytes 1572872 | tf_op jit(solution)/shard_map/ppermute | solution.py:493
  169.8 2.8 %collective-permute-start.6 = (f32[64,8,128]{2,1,0:T(8,128)S(1)}, f32[64,8,128]{2,1,0:T(8,128)S(1)}, u32[]{:S(2)}, u32[]{:S(2)}) collective-permute-start(f32[64,8,128]{2,1,0:T(8,128)S(1)} %all_to_all.41.same_ref), channel_id=1, source_target_pairs={{0,1},{1,0},{2,3},{3,2},{4,5},{5,4},{6,7},{7,6},{8,9},{9,8},{10,11... | collective-permute-start | bytes 786440 | tf_op jit(solution)/shard_map/ppermute | solution.py:493
